TPU v7x, 32 devices: a whole 2x2x4 slice. The times are simulated.
32 devices in a mesh: gx: 2 (over core), gy: 4 (over y, x), ma: 4 (over z).
Axes of the slice: x: 2, y: 2, z: 4, core: 2. Of those that a mesh axis runs over, the one named last changes fastest.
Arguments:
- object_field: float32 [2, 256, 1024], P(None, 'gx', 'gy'), may hold values from -5 to 5
- probe_modes: float32 [8, 2, 256, 256], P('ma'), may hold values from -1.5 to 1.5
- measured: float32 [2, 4, 2, 256, 256], P('gx', 'gy'), may hold values from 0.1 to 4
- positions: int32 [2, 4, 2, 2], P('gx', 'gy'), may hold values from 0 to 255, as said below
- slot_counts: int32 [2, 4], P('gx', 'gy'), may hold values from 1 to 2, as said below
Outputs:
- updated_object: float32 [2, 256, 1024], P(None, 'gx', 'gy')
Inputs may be any that keep to these rules, and one draw needn't show every extreme that they name: positions[a, b, s] holds a row 0 to 127 and a column 0 to 255 of tile (a, b); slots s >= slot_counts[a, b] are unused. `slot_counts`: some tile uses all 2 slots.
All inputs are finite; a program needn't handle non-finite values.
Results may differ from a plain program's by a relative error of at most 0.0023.
Values sent between devices are 32-bit elements; how exact they have to be, the bound alone decides.
No kernel may reach another device: no remote copies, remote signals or barrier semaphores. Data moves between devices by JAX's collectives and lax.ppermute only.
A program may use at most 64 MiB of HBM per device.

v0:
```python
import math

import jax
import jax.numpy as jnp
from jax import lax
from jax.sharding import PartitionSpec as P

OUTER = 2


DAMPING = 1.0


def padded_2(block, sides, width):
    for axis, dim in sides:
        count = lax.axis_size(axis)
        forward = [(i, i + 1) for i in range(count - 1)]
        backward = [(target, source) for source, target in forward]
        low = lax.ppermute(
            lax.slice_in_dim(block, block.shape[dim] - width, None, axis=dim), axis, forward
        )
        high = lax.ppermute(lax.slice_in_dim(block, 0, width, axis=dim), axis, backward)
        block = jnp.concatenate([low, block, high], axis=dim)
    return block


def dft_tables(patch_width):
    ladder = jnp.arange(patch_width, dtype=jnp.int32)
    phases = ladder[:, None] * ladder[None, :] % patch_width
    angles = phases.astype(jnp.float32) * (2.0 * math.pi / patch_width)
    factor = 1.0 / math.sqrt(patch_width)
    real_part = jnp.cos(angles) * factor
    imag_part = -jnp.sin(angles) * factor
    table_one = jnp.concatenate(
        [jnp.concatenate([real_part, -imag_part], 1), jnp.concatenate([imag_part, real_part], 1)], 0
    ).astype(jnp.bfloat16)
    table_two = jnp.concatenate(
        [jnp.concatenate([real_part, imag_part], 1), jnp.concatenate([-imag_part, real_part], 1)], 0
    ).astype(jnp.bfloat16)
    return (table_one, table_two)


def forward_transform(wavefield, tables):
    patch_width = wavefield.shape[-1]
    halfway = jnp.einsum(
        "pqci,bcik->bpqk",
        tables[0].reshape(2, patch_width, 2, patch_width),
        wavefield,
        preferred_element_type=jnp.float32,
    ).astype(jnp.bfloat16)
    return jnp.einsum(
        "bcik,ckl->bil",
        halfway,
        tables[1].reshape(2, patch_width, 2 * patch_width),
        preferred_element_type=jnp.float32,
    )


def adjoint_transform(weighted, tables):
    patch_width = weighted.shape[1]
    halfway = jnp.einsum(
        "bik,kl->bil", weighted, tables[0], preferred_element_type=jnp.float32
    ).astype(jnp.bfloat16)
    return jnp.einsum(
        "pqci,bicl->bpql",
        tables[1].reshape(2, patch_width, 2, patch_width),
        halfway.reshape(halfway.shape[0], patch_width, 2, patch_width),
        preferred_element_type=jnp.float32,
    )


def exit_waves(probe_modes, windows):
    probe_real = probe_modes[None, :, 0]
    probe_imag = probe_modes[None, :, 1]
    window_real = windows[:, None, 0]
    window_imag = windows[:, None, 1]
    real_part = probe_real * window_real - probe_imag * window_imag
    imag_part = probe_real * window_imag + probe_imag * window_real
    wavefield = jnp.stack([real_part, imag_part], 2).astype(jnp.bfloat16)
    return wavefield.reshape(-1, 2, probe_modes.shape[-1], probe_modes.shape[-1])


def intensity_part(spectra, mode_count):
    patch_width = spectra.shape[1]
    grouped = spectra.reshape(-1, mode_count, patch_width, 2 * patch_width)
    squared = grouped * grouped
    return jnp.sum(squared[..., :patch_width] + squared[..., patch_width:], axis=1)


def change_part(spectra, moved_spectra, mode_count):
    patch_width = spectra.shape[1]
    grouped = spectra.reshape(-1, mode_count, patch_width, 2 * patch_width)
    shifted = moved_spectra.reshape(-1, mode_count, patch_width, 2 * patch_width)
    product = grouped * shifted
    return 2.0 * jnp.sum(product[..., :patch_width] + product[..., patch_width:], axis=1)


def mode_images(weights, spectra, probe_modes, tables):
    mode_count = probe_modes.shape[0]
    patch_width = probe_modes.shape[-1]
    doubled = jnp.concatenate([weights, weights], -1)
    grouped = spectra.reshape(-1, mode_count, patch_width, 2 * patch_width)
    weighted = (2.0 * grouped * doubled[:, None]).astype(jnp.bfloat16)
    returned = adjoint_transform(weighted.reshape(-1, patch_width, 2 * patch_width), tables)
    returned = returned.reshape(-1, mode_count, 2, patch_width, patch_width)
    probe_real = probe_modes[None, :, 0]
    probe_imag = probe_modes[None, :, 1]
    real_part = jnp.sum(probe_real * returned[:, :, 0] + probe_imag * returned[:, :, 1], axis=1)
    imag_part = jnp.sum(probe_real * returned[:, :, 1] - probe_imag * returned[:, :, 0], axis=1)
    return jnp.stack([real_part, imag_part], 1)


def fold_edges(widened, axis_dim, length, rim_width):
    middle = lax.slice_in_dim(widened, 2 * rim_width, 2 * rim_width + length, axis=axis_dim)
    low_rim = lax.slice_in_dim(widened, 0, rim_width, axis=axis_dim)
    high_rim = lax.slice_in_dim(
        widened, length + 3 * rim_width, length + 4 * rim_width, axis=axis_dim
    )
    low_pads = [(0, 0), (0, 0), (0, 0)]
    high_pads = [(0, 0), (0, 0), (0, 0)]
    low_pads[axis_dim] = (0, length - rim_width)
    high_pads[axis_dim] = (length - rim_width, 0)
    return middle + jnp.pad(low_rim, low_pads) + jnp.pad(high_rim, high_pads)


def shards(object_field, probe_modes, measured, positions, slot_counts):
    patch_width = probe_modes.shape[-1]
    mode_count = probe_modes.shape[0]
    rim_width = patch_width // 2
    tile_rows = object_field.shape[1]
    tile_cols = object_field.shape[2]
    slot_count = measured.shape[2]
    share_rows = tile_rows // lax.axis_size("ma")
    tables = dft_tables(patch_width)
    targets = measured[0, 0]
    centres = positions[0, 0]
    live_mask = (jnp.arange(slot_count, dtype=jnp.int32) < slot_counts[0, 0]).astype(jnp.float32)[
        :, None, None
    ]
    anchor = jnp.zeros((), jnp.int32)

    def spectra_of(current):
        padded = padded_2(current, (("gx", 1), ("gy", 2)), rim_width)
        windows = jnp.stack(
            [
                lax.dynamic_slice(
                    padded,
                    (anchor, centres[slot_index, 0], centres[slot_index, 1]),
                    (2, patch_width, patch_width),
                )
                for slot_index in range(slot_count)
            ],
            0,
        )
        return forward_transform(exit_waves(probe_modes, windows), tables)

    def mode_total(partial_value):
        return lax.psum(partial_value, "ma")

    def combine(folded):
        summed = lax.psum(folded, "ma")
        return summed

    def project(weights, spectra):
        pieces = mode_images(weights, spectra, probe_modes, tables)
        extended = jnp.zeros((2, tile_rows + patch_width, tile_cols + patch_width), jnp.float32)
        for slot_index in range(slot_count):
            corner = (anchor, centres[slot_index, 0], centres[slot_index, 1])
            extended = lax.dynamic_update_slice(
                extended,
                lax.dynamic_slice(extended, corner, (2, patch_width, patch_width))
                + pieces[slot_index],
                corner,
            )
        widened = padded_2(extended, (("gx", 1), ("gy", 2)), rim_width)
        folded = fold_edges(fold_edges(widened, 1, tile_rows, rim_width), 2, tile_cols, rim_width)
        result = combine(folded)
        return result

    def local_sum(first_vec, second_vec):
        first_vec = lax.dynamic_slice_in_dim(
            first_vec, lax.axis_index("ma") * share_rows, share_rows, 1
        )
        second_vec = lax.dynamic_slice_in_dim(
            second_vec, lax.axis_index("ma") * share_rows, share_rows, 1
        )
        return jnp.sum(first_vec * second_vec)

    current = object_field
    for outer_step in range(OUTER):
        spectra = spectra_of(current)
        misfit = live_mask * (mode_total(intensity_part(spectra, mode_count)) - targets)
        gradient = project(misfit, spectra)
        residual = -gradient
        direction = residual
        norm_now = lax.psum(local_sum(residual, residual), ("gx", "gy", "ma"))
        moved_spectra = spectra_of(direction)
        change = live_mask * mode_total(change_part(spectra, moved_spectra, mode_count))
        applied = project(change, spectra) + DAMPING * direction
        step_size = norm_now / lax.psum(local_sum(direction, applied), ("gx", "gy", "ma"))
        update = step_size * direction
        residual = residual - step_size * applied
        current = current + update
    return current


def solution(mesh):
    return jax.shard_map(
        shards,
        mesh=mesh,
        in_specs=(
            P(None, "gx", "gy"),
            P("ma", None, None, None),
            P("gx", "gy", None, None, None),
            P("gx", "gy", None, None),
            P("gx", "gy"),
        ),
        out_specs=P(None, "gx", "gy"),
        check_vma=False,
    )
```

profile of v0, /device:TPU:0, one launch (start us, length us, event | category | flops | bytes accessed | tf_op | source)
XLA Modules:
  0.0 797.5 jit_solution(15070351154825093424)
XLA Ops:
  6.5 2.5 collective-permute-start
  13.7 4.2 collective-permute-start.2
  31.0 6.3 collective-permute-done.3
  45.2 36.3 %all-reduce.15.cloned.1.call-done = f32[2,256,256]{2,1,0:T(8,128)} async-done(((f32[2,256,256]{2,1,0:T(8,128)}), f32[2,256,256]{2,1,0:T(8,128)}) %all-reduce.15.cloned.1.call-update) | async-done | bytes 524304 | tf_op jit(solution)/shard_map/psum | solution.py:158
  89.3 7.4 dynamic_update_slice.24
  98.8 7.1 dynamic_update_slice.25
  106.0 2.3 collective-permute-start.4
  109.7 2.3 collective-permute-done.5
  115.5 12.9 %collective-permute-done.6 = f32[2,640,128]{1,2,0:T(8,128)S(1)} collective-permute-done((f32[2,640,128]{1,2,0:T(8,128)S(1)}, f32[2,640,128]{1,2,0:T(8,128)S(1)}, u32[]{:S(2)}, u32[]{:S(2)}) %collective-permute-start.6) | collective-permute-done | bytes 655392 | tf_op jit(solution)/shard_map/ppermute | solution.py:19
  128.4 18.5 %collective-permute-done.7 = f32[2,640,128]{1,2,0:T(8,128)S(1)} collective-permute-done((f32[2,640,128]{1,2,0:T(8,128)S(1)}, f32[2,640,128]{1,2,0:T(8,128)S(1)}, u32[]{:S(2)}, u32[]{:S(2)}) %collective-permute-start.7) | collective-permute-done | bytes 655392 | tf_op jit(solution)/shard_map/ppermute | solution.py:22
  148.5 33.7 %all-reduce.17.cloned.1.call-done = f32[2,128,256]{1,2,0:T(8,128)} async-done(((f32[2,128,256]{1,2,0:T(8,128)}), f32[2,128,256]{1,2,0:T(8,128)}) %all-reduce.17.cloned.1.call-update) | async-done | bytes 262160 | tf_op jit(solution)/shard_map/psum | solution.py:161
  185.8 2.1 collective-permute-done.9
  188.0 3.4 collective-permute-start.10
  192.9 7.2 collective-permute-done.10
  200.0 10.3 %collective-permute-done.11 = f32[2,384,128]{1,2,0:T(8,128)S(1)} collective-permute-done((f32[2,384,128]{1,2,0:T(8,128)S(1)}, f32[2,384,128]{1,2,0:T(8,128)S(1)}, u32[]{:S(2)}, u32[]{:S(2)}) %collective-permute-start.11) | collective-permute-done | bytes 393248 | tf_op jit(solution)/shard_map/ppermute | solution.py:22
  218.2 37.7 %all-reduce.19.cloned.1.call-done = f32[2,256,256]{2,1,0:T(8,128)} async-done(((f32[2,256,256]{2,1,0:T(8,128)}), f32[2,256,256]{2,1,0:T(8,128)}) %all-reduce.19.cloned.1.call-update) | async-done | bytes 524304 | tf_op jit(solution)/shard_map/psum | solution.py:158
  263.6 7.5 dynamic_update_slice.26
  273.1 7.1 dynamic_update_slice.27
  280.3 2.3 collective-permute-start.12
  284.1 2.3 collective-permute-done.13
  289.8 12.9 %collective-permute-done.14 = f32[2,640,128]{1,2,0:T(8,128)S(1)} collective-permute-done((f32[2,640,128]{1,2,0:T(8,128)S(1)}, f32[2,640,128]{1,2,0:T(8,128)S(1)}, u32[]{:S(2)}, u32[]{:S(2)}) %collective-permute-start.14) | collective-permute-done | bytes 655392 | tf_op jit(solution)/shard_map/ppermute | solution.py:19
  302.8 18.5 %collective-permute-done.15 = f32[2,640,128]{1,2,0:T(8,128)S(1)} collective-permute-done((f32[2,640,128]{1,2,0:T(8,128)S(1)}, f32[2,640,128]{1,2,0:T(8,128)S(1)}, u32[]{:S(2)}, u32[]{:S(2)}) %collective-permute-start.15) | collective-permute-done | bytes 655392 | tf_op jit(solution)/shard_map/ppermute | solution.py:22
  322.4 33.6 %all-reduce.21.cloned.1.call-done = f32[2,128,256]{1,2,0:T(8,128)} async-done(((f32[2,128,256]{1,2,0:T(8,128)}), f32[2,128,256]{1,2,0:T(8,128)}) %all-reduce.21.cloned.1.call-update) | async-done | bytes 262160 | tf_op jit(solution)/shard_map/psum | solution.py:161
  357.8 40.4 %all-reduce.5 = (f32[]{:T(128)}, f32[]{:T(128)}) all-reduce(f32[]{:T(128)} %get-tuple-element.16, f32[]{:T(128)} %get-tuple-element.15), channel_id=1, replica_groups=mesh['gx'=2,'gy'=4,'ma'=4] {'gx','gy','ma'}, use_global_device_ids=true, to_apply=%region_6.7 | all-reduce | flops 2 | bytes 16 | tf_op jit(solution)/shard_map/psum | solution.py:196
  402.2 2.1 collective-permute-done.17
  404.4 4.2 collective-permute-start.18
  409.9 7.3 collective-permute-done.18
  417.3 10.6 %collective-permute-done.19 = f32[2,384,128]{1,2,0:T(8,128)S(1)} collective-permute-done((f32[2,384,128]{1,2,0:T(8,128)S(1)}, f32[2,384,128]{1,2,0:T(8,128)S(1)}, u32[]{:S(2)}, u32[]{:S(2)}) %collective-permute-start.19) | collective-permute-done | bytes 393248 | tf_op jit(solution)/shard_map/ppermute | solution.py:22
  435.3 36.4 %all-reduce.23.cloned.1.call-done = f32[2,256,256]{2,1,0:T(8,128)} async-done(((f32[2,256,256]{2,1,0:T(8,128)}), f32[2,256,256]{2,1,0:T(8,128)}) %all-reduce.23.cloned.1.call-update) | async-done | bytes 524304 | tf_op jit(solution)/shard_map/psum | solution.py:158
  479.6 7.4 dynamic_update_slice.28
  489.0 7.1 dynamic_update_slice.29
  496.2 2.3 collective-permute-start.20
  499.9 2.3 collective-permute-done.21
  505.7 12.9 %collective-permute-done.22 = f32[2,640,128]{1,2,0:T(8,128)S(1)} collective-permute-done((f32[2,640,128]{1,2,0:T(8,128)S(1)}, f32[2,640,128]{1,2,0:T(8,128)S(1)}, u32[]{:S(2)}, u32[]{:S(2)}) %collective-permute-start.22) | collective-permute-done | bytes 655392 | tf_op jit(solution)/shard_map/ppermute | solution.py:19
  518.6 18.5 %collective-permute-done.23 = f32[2,640,128]{1,2,0:T(8,128)S(1)} collective-permute-done((f32[2,640,128]{1,2,0:T(8,128)S(1)}, f32[2,640,128]{1,2,0:T(8,128)S(1)}, u32[]{:S(2)}, u32[]{:S(2)}) %collective-permute-start.23) | collective-permute-done | bytes 655392 | tf_op jit(solution)/shard_map/ppermute | solution.py:22
  538.1 33.7 %all-reduce.25.cloned.1.call-done = f32[2,128,256]{1,2,0:T(8,128)} async-done(((f32[2,128,256]{1,2,0:T(8,128)}), f32[2,128,256]{1,2,0:T(8,128)}) %all-reduce.25.cloned.1.call-update) | async-done | bytes 262160 | tf_op jit(solution)/shard_map/psum | solution.py:161
  577.7 3.4 collective-permute-start.26
  582.4 7.3 collective-permute-done.26
  589.7 10.3 %collective-permute-done.27 = f32[2,384,128]{1,2,0:T(8,128)S(1)} collective-permute-done((f32[2,384,128]{1,2,0:T(8,128)S(1)}, f32[2,384,128]{1,2,0:T(8,128)S(1)}, u32[]{:S(2)}, u32[]{:S(2)}) %collective-permute-start.27) | collective-permute-done | bytes 393248 | tf_op jit(solution)/shard_map/ppermute | solution.py:22
  607.8 37.7 %all-reduce.27.cloned.1.call-done = f32[2,256,256]{2,1,0:T(8,128)} async-done(((f32[2,256,256]{2,1,0:T(8,128)}), f32[2,256,256]{2,1,0:T(8,128)}) %all-reduce.27.cloned.1.call-update) | async-done | bytes 524304 | tf_op jit(solution)/shard_map/psum | solution.py:158
  653.1 7.7 dynamic_update_slice.30
  661.9 7.3 dynamic_update_slice.31
  669.3 2.9 collective-permute-start.28
  673.7 2.3 collective-permute-done.29
  678.8 13.1 %collective-permute-done.30 = f32[2,640,128]{1,2,0:T(8,128)S(1)} collective-permute-done((f32[2,640,128]{1,2,0:T(8,128)S(1)}, f32[2,640,128]{1,2,0:T(8,128)S(1)}, u32[]{:S(2)}, u32[]{:S(2)}) %collective-permute-start.30) | collective-permute-done | bytes 655392 | tf_op jit(solution)/shard_map/ppermute | solution.py:19
  691.9 19.1 %collective-permute-done.31 = f32[2,640,128]{1,2,0:T(8,128)S(1)} collective-permute-done((f32[2,640,128]{1,2,0:T(8,128)S(1)}, f32[2,640,128]{1,2,0:T(8,128)S(1)}, u32[]{:S(2)}, u32[]{:S(2)}) %collective-permute-start.31) | collective-permute-done | bytes 655392 | tf_op jit(solution)/shard_map/ppermute | solution.py:22
  712.1 33.7 %all-reduce.29.cloned.1.call-done = f32[2,128,256]{1,2,0:T(8,128)} async-done(((f32[2,128,256]{1,2,0:T(8,128)}), f32[2,128,256]{1,2,0:T(8,128)}) %all-reduce.29.cloned.1.call-update) | async-done | bytes 262160 | tf_op jit(solution)/shard_map/psum | solution.py:161
  747.6 40.4 %all-reduce.4 = (f32[]{:T(128)}, f32[]{:T(128)}) all-reduce(f32[]{:T(128)} %get-tuple-element.14, f32[]{:T(128)} %get-tuple-element.13), channel_id=1, replica_groups=mesh['gx'=2,'gy'=4,'ma'=4] {'gx','gy','ma'}, use_global_device_ids=true, to_apply=%region_20.21 | all-reduce | flops 2 | bytes 16 | tf_op jit(solution)/shard_map/psum | solution.py:196
  (248 shorter events, 122.4 us)
Async XLA Ops:
  6.5 74.9 %all-reduce.15.cloned.1.call-start = ((), (), s32[]{:S(2)}) async-start(), calls=%async_computation | async-start | bytes 1048576 | tf_op jit(solution)/shard_map/psum | solution.py:158
  6.5 5.2 collective-permute-start
  9.1 3.6 collective-permute-start.1
  13.7 17.3 %collective-permute-start.2 = (f32[2,384,128]{2,1,0:T(8,128)}, f32[2,384,128]{2,1,0:T(8,128)S(1)}, u32[]{:S(2)}, u32[]{:S(2)}) collective-permute-start(f32[2,384,128]{2,1,0:T(8,128)} %get-tuple-element.69), channel_id=1, source_target_pairs={{0,4},{4,8},{8,12},{1,5},{5,9},{9,13},{2,6},{6,10},{10,14},{3,7},{... | collective-permute-start | bytes 1179656 | tf_op jit(solution)/shard_map/ppermute | solution.py:19
  17.9 19.4 %collective-permute-start.3 = (f32[2,384,128]{2,1,0:T(8,128)}, f32[2,384,128]{2,1,0:T(8,128)}, u32[]{:S(2)}, u32[]{:S(2)}) collective-permute-start(f32[2,384,128]{2,1,0:T(8,128)} %get-tuple-element.70), channel_id=1, source_target_pairs={{4,0},{8,4},{12,8},{5,1},{9,5},{13,9},{6,2},{10,6},{14,10},{7,3},{... | collective-permute-start | bytes 1179656 | tf_op jit(solution)/shard_map/ppermute | solution.py:22
  28.3 10.1 %copy-start.18 = (bf16[512,512]{1,0:T(8,128)(2,1)}, bf16[512,512]{1,0:T(8,128)(2,1)S(1)}, u32[]{:S(2)}) copy-start(bf16[512,512]{1,0:T(8,128)(2,1)S(1)} %get-tuple-element.72) | copy-start | bytes 1572868
  28.4 11.2 %copy-start.27 = (bf16[2,256,2,256]{3,2,1,0:T(2,128)(2,1)}, bf16[2,256,2,256]{3,2,1,0:T(2,128)(2,1)S(1)}, u32[]{:S(2)}) copy-start(bf16[2,256,2,256]{3,2,1,0:T(2,128)(2,1)S(1)} %convert_element_type.132) | copy-start | bytes 1572868
  41.4 41.4 %copy-start = (f32[2,2,256,512,1]{3,2,4,1,0:T(8,128)}, f32[2,2,256,512,1]{3,2,4,1,0:T(8,128)S(1)}, u32[]{:S(2)}) copy-start(f32[2,2,256,512,1]{3,2,4,1,0:T(8,128)S(1)} %get-tuple-element.78) | copy-start | bytes 6291460
  42.5 139.7 %all-reduce.17.cloned.1.call-start = ((), (), s32[]{:S(2)}) async-start(), calls=%async_computation.1 | async-start | bytes 524288 | tf_op jit(solution)/shard_map/psum | solution.py:161
  106.0 3.8 collective-permute-start.4
  108.2 3.8 collective-permute-start.5
  112.1 16.3 %collective-permute-start.6 = (f32[2,640,128]{1,2,0:T(8,128)S(1)}, f32[2,640,128]{1,2,0:T(8,128)S(1)}, u32[]{:S(2)}, u32[]{:S(2)}) collective-permute-start(f32[2,640,128]{1,2,0:T(8,128)S(1)} %get-tuple-element.27), channel_id=1, source_target_pairs={{0,4},{4,8},{8,12},{1,5},{5,9},{9,13},{2,6},{6,10},{10,14},{3,7},{... | collective-permute-start | bytes 1966088 | tf_op jit(solution)/shard_map/ppermute | solution.py:19
  114.2 32.7 %collective-permute-start.7 = (f32[2,640,128]{1,2,0:T(8,128)S(1)}, f32[2,640,128]{1,2,0:T(8,128)S(1)}, u32[]{:S(2)}, u32[]{:S(2)}) collective-permute-start(f32[2,640,128]{1,2,0:T(8,128)S(1)} %get-tuple-element.28), channel_id=1, source_target_pairs={{4,0},{8,4},{12,8},{5,1},{9,5},{13,9},{6,2},{10,6},{14,10},{7,3},{... | collective-permute-start | bytes 1966088 | tf_op jit(solution)/shard_map/ppermute | solution.py:22
  148.4 107.5 %all-reduce.19.cloned.1.call-start = ((), (), s32[]{:S(2)}) async-start(), calls=%async_computation.2 | async-start | bytes 1048576 | tf_op jit(solution)/shard_map/psum | solution.py:158
  183.1 2.6 collective-permute-start.8
  184.5 3.4 collective-permute-start.9
  188.0 12.0 %collective-permute-start.10 = (f32[2,384,128]{1,2,0:T(8,128)S(1)}, f32[2,384,128]{1,2,0:T(8,128)S(1)}, u32[]{:S(2)}, u32[]{:S(2)}) collective-permute-start(f32[2,384,128]{1,2,0:T(8,128)S(1)} %get-tuple-element.67), channel_id=1, source_target_pairs={{0,4},{4,8},{8,12},{1,5},{5,9},{9,13},{2,6},{6,10},{10,14},{3,7},{... | collective-permute-start | bytes 1179656 | tf_op jit(solution)/shard_map/ppermute | solution.py:19
  191.4 19.0 %collective-permute-start.11 = (f32[2,384,128]{1,2,0:T(8,128)S(1)}, f32[2,384,128]{1,2,0:T(8,128)S(1)}, u32[]{:S(2)}, u32[]{:S(2)}) collective-permute-start(f32[2,384,128]{1,2,0:T(8,128)S(1)} %get-tuple-element.68), channel_id=1, source_target_pairs={{4,0},{8,4},{12,8},{5,1},{9,5},{13,9},{6,2},{10,6},{14,10},{7,3},{... | collective-permute-start | bytes 1179656 | tf_op jit(solution)/shard_map/ppermute | solution.py:22
  218.1 137.9 %all-reduce.21.cloned.1.call-start = ((), (), s32[]{:S(2)}) async-start(), calls=%async_computation.3 | async-start | bytes 524288 | tf_op jit(solution)/shard_map/psum | solution.py:161
  280.3 3.8 collective-permute-start.12
  282.6 3.8 collective-permute-start.13
  286.5 16.3 %collective-permute-start.14 = (f32[2,640,128]{1,2,0:T(8,128)S(1)}, f32[2,640,128]{1,2,0:T(8,128)S(1)}, u32[]{:S(2)}, u32[]{:S(2)}) collective-permute-start(f32[2,640,128]{1,2,0:T(8,128)S(1)} %get-tuple-element.25), channel_id=1, source_target_pairs={{0,4},{4,8},{8,12},{1,5},{5,9},{9,13},{2,6},{6,10},{10,14},{3,7},{... | collective-permute-start | bytes 1966088 | tf_op jit(solution)/shard_map/ppermute | solution.py:19
  288.5 32.7 %collective-permute-start.15 = (f32[2,640,128]{1,2,0:T(8,128)S(1)}, f32[2,640,128]{1,2,0:T(8,128)S(1)}, u32[]{:S(2)}, u32[]{:S(2)}) collective-permute-start(f32[2,640,128]{1,2,0:T(8,128)S(1)} %get-tuple-element.26), channel_id=1, source_target_pairs={{4,0},{8,4},{12,8},{5,1},{9,5},{13,9},{6,2},{10,6},{14,10},{7,3},{... | collective-permute-start | bytes 1966088 | tf_op jit(solution)/shard_map/ppermute | solution.py:22
  321.4 78.1 %copy-start.25 = (f32[2,128,256]{1,2,0:T(8,128)S(1)}, f32[2,128,256]{1,2,0:T(8,128)}, u32[]{:S(2)}) copy-start(f32[2,128,256]{1,2,0:T(8,128)} %all-reduce.17.cloned.1.call-done) | copy-start | bytes 786436
  322.2 149.4 %all-reduce.23.cloned.1.call-start = ((), (), s32[]{:S(2)}) async-start(), calls=%async_computation.4 | async-start | bytes 1048576 | tf_op jit(solution)/shard_map/psum | solution.py:158
  399.6 28.3 %copy-start.16 = (f32[2,128,256]{1,2,0:T(8,128)}, f32[2,128,256]{1,2,0:T(8,128)S(1)}, u32[]{:S(2)}) copy-start(f32[2,128,256]{1,2,0:T(8,128)S(1)} %multiply_add_fusion.1) | copy-start | bytes 786436
  399.6 2.6 collective-permute-start.16
  400.9 3.4 collective-permute-start.17
  404.4 12.8 %collective-permute-start.18 = (f32[2,384,128]{1,2,0:T(8,128)S(1)}, f32[2,384,128]{1,2,0:T(8,128)S(1)}, u32[]{:S(2)}, u32[]{:S(2)}) collective-permute-start(f32[2,384,128]{1,2,0:T(8,128)S(1)} %get-tuple-element.65), channel_id=1, source_target_pairs={{0,4},{4,8},{8,12},{1,5},{5,9},{9,13},{2,6},{6,10},{10,14},{3,7},{... | collective-permute-start | bytes 1179656 | tf_op jit(solution)/shard_map/ppermute | solution.py:19
  408.6 19.2 %collective-permute-start.19 = (f32[2,384,128]{1,2,0:T(8,128)S(1)}, f32[2,384,128]{1,2,0:T(8,128)S(1)}, u32[]{:S(2)}, u32[]{:S(2)}) collective-permute-start(f32[2,384,128]{1,2,0:T(8,128)S(1)} %get-tuple-element.66), channel_id=1, source_target_pairs={{4,0},{8,4},{12,8},{5,1},{9,5},{13,9},{6,2},{10,6},{14,10},{7,3},{... | collective-permute-start | bytes 1179656 | tf_op jit(solution)/shard_map/ppermute | solution.py:22
  433.9 39.2 %copy-start.2 = (f32[2,2,256,512,1]{3,2,4,1,0:T(8,128)}, f32[2,2,256,512,1]{3,2,4,1,0:T(8,128)S(1)}, u32[]{:S(2)}) copy-start(f32[2,2,256,512,1]{3,2,4,1,0:T(8,128)S(1)} %get-tuple-element.80) | copy-start | bytes 6291460
  435.0 136.8 %all-reduce.25.cloned.1.call-start = ((), (), s32[]{:S(2)}) async-start(), calls=%async_computation.5 | async-start | bytes 524288 | tf_op jit(solution)/shard_map/psum | solution.py:161
  496.2 3.8 collective-permute-start.20
  498.4 3.8 collective-permute-start.21
  502.3 16.3 %collective-permute-start.22 = (f32[2,640,128]{1,2,0:T(8,128)S(1)}, f32[2,640,128]{1,2,0:T(8,128)S(1)}, u32[]{:S(2)}, u32[]{:S(2)}) collective-permute-start(f32[2,640,128]{1,2,0:T(8,128)S(1)} %get-tuple-element.23), channel_id=1, source_target_pairs={{0,4},{4,8},{8,12},{1,5},{5,9},{9,13},{2,6},{6,10},{10,14},{3,7},{... | collective-permute-start | bytes 1966088 | tf_op jit(solution)/shard_map/ppermute | solution.py:19
  504.4 32.7 %collective-permute-start.23 = (f32[2,640,128]{1,2,0:T(8,128)S(1)}, f32[2,640,128]{1,2,0:T(8,128)S(1)}, u32[]{:S(2)}, u32[]{:S(2)}) collective-permute-start(f32[2,640,128]{1,2,0:T(8,128)S(1)} %get-tuple-element.24), channel_id=1, source_target_pairs={{4,0},{8,4},{12,8},{5,1},{9,5},{13,9},{6,2},{10,6},{14,10},{7,3},{... | collective-permute-start | bytes 1966088 | tf_op jit(solution)/shard_map/ppermute | solution.py:22
  538.1 107.4 %all-reduce.27.cloned.1.call-start = ((), (), s32[]{:S(2)}) async-start(), calls=%async_computation.6 | async-start | bytes 1048576 | tf_op jit(solution)/shard_map/psum | solution.py:158
  572.8 2.6 collective-permute-start.24
  574.1 3.4 collective-permute-start.25
  577.7 12.0 %collective-permute-start.26 = (f32[2,384,128]{1,2,0:T(8,128)S(1)}, f32[2,384,128]{1,2,0:T(8,128)S(1)}, u32[]{:S(2)}, u32[]{:S(2)}) collective-permute-start(f32[2,384,128]{1,2,0:T(8,128)S(1)} %get-tuple-element.63), channel_id=1, source_target_pairs={{0,4},{4,8},{8,12},{1,5},{5,9},{9,13},{2,6},{6,10},{10,14},{3,7},{... | collective-permute-start | bytes 1179656 | tf_op jit(solution)/shard_map/ppermute | solution.py:19
  581.1 19.0 %collective-permute-start.27 = (f32[2,384,128]{1,2,0:T(8,128)S(1)}, f32[2,384,128]{1,2,0:T(8,128)S(1)}, u32[]{:S(2)}, u32[]{:S(2)}) collective-permute-start(f32[2,384,128]{1,2,0:T(8,128)S(1)} %get-tuple-element.64), channel_id=1, source_target_pairs={{4,0},{8,4},{12,8},{5,1},{9,5},{13,9},{6,2},{10,6},{14,10},{7,3},{... | collective-permute-start | bytes 1179656 | tf_op jit(solution)/shard_map/ppermute | solution.py:22
  607.8 138.1 %all-reduce.29.cloned.1.call-start = ((), (), s32[]{:S(2)}) async-start(), calls=%async_computation.7 | async-start | bytes 524288 | tf_op jit(solution)/shard_map/psum | solution.py:161
  669.3 4.4 collective-permute-start.28
  672.2 3.8 collective-permute-start.29
  676.1 15.9 %collective-permute-start.30 = (f32[2,640,128]{1,2,0:T(8,128)S(1)}, f32[2,640,128]{1,2,0:T(8,128)S(1)}, u32[]{:S(2)}, u32[]{:S(2)}) collective-permute-start(f32[2,640,128]{1,2,0:T(8,128)S(1)} %get-tuple-element.21), channel_id=1, source_target_pairs={{0,4},{4,8},{8,12},{1,5},{5,9},{9,13},{2,6},{6,10},{10,14},{3,7},{... | collective-permute-start | bytes 1966088 | tf_op jit(solution)/shard_map/ppermute | solution.py:19
  677.5 33.5 %collective-permute-start.31 = (f32[2,640,128]{1,2,0:T(8,128)S(1)}, f32[2,640,128]{1,2,0:T(8,128)S(1)}, u32[]{:S(2)}, u32[]{:S(2)}) collective-permute-start(f32[2,640,128]{1,2,0:T(8,128)S(1)} %get-tuple-element.22), channel_id=1, source_target_pairs={{4,0},{8,4},{12,8},{5,1},{9,5},{13,9},{6,2},{10,6},{14,10},{7,3},{... | collective-permute-start | bytes 1966088 | tf_op jit(solution)/shard_map/ppermute | solution.py:22
  711.2 78.2 %copy-start.17 = (f32[2,128,256]{1,2,0:T(8,128)S(1)}, f32[2,128,256]{1,2,0:T(8,128)}, u32[]{:S(2)}) copy-start(f32[2,128,256]{1,2,0:T(8,128)} %copy-done.16) | copy-start | bytes 786436
  711.2 78.2 %copy-start.26 = (f32[2,128,256]{1,2,0:T(8,128)S(1)}, f32[2,128,256]{1,2,0:T(8,128)}, u32[]{:S(2)}) copy-start(f32[2,128,256]{1,2,0:T(8,128)} %all-reduce.25.cloned.1.call-done) | copy-start | bytes 786436
  (25 other events, 40.2 us)
Sparse Core Ops, SparseCore 0:
  42.6 38.7 all-reduce.14
  148.5 33.5 all-reduce.16
  218.2 37.6 all-reduce.18
  322.4 33.5 all-reduce.20
  435.1 36.4 all-reduce.22
  538.2 33.5 all-reduce.24
  607.9 37.5 all-reduce.26
  712.2 33.5 all-reduce.28
where the time goes:
time: 809 us; the launch traced here: 797 us
  waiting for transfers between devices  486 us (60%)
  local copies, waits for them, and re-layouts  87.9 us (11%)
  blocking collectives  80.8 us (10%)
  starting transfers between devices  60.3 us (7%)
  other arithmetic  40.6 us (5%)
  between operations  26.1 us (3%)
  matrix products  15.7 us (2%)
    psum x4, waiting for transfers between devices, mode_total(): return lax.psum(partial_value, 'ma')  148 us
    psum x4, waiting for transfers between devices, combine(): summed = lax.psum(folded, 'ma')  135 us
    ppermute x16, waiting for transfers between devices, padded_2(): lax.ppermute(lax.slice_in_dim(block, 0, width, axis=dim), axis, backward)  129 us
    psum x2, blocking collectives, shards(): norm_now = lax.psum(local_sum(residual, residual), ('gx', 'gy', 'ma'))  80.8 us
    ppermute x16, waiting for transfers between devices, padded_2(): lax.ppermute(lax.slice_in_dim(block, block.shape[dim] - width, None, axis...  74.5 us
    dynamic_update_slice x8, local copies, waits for them, and re-layouts, project(): lax.dynamic_update_slice(extended, lax.dynamic_slice(extended, corner, (2...  58.6 us
    ppermute x16, starting transfers between devices, padded_2(): lax.ppermute(lax.slice_in_dim(block, block.shape[dim] - width, None, axis...  39 us
    ppermute x16, starting transfers between devices, padded_2(): lax.ppermute(lax.slice_in_dim(block, 0, width, axis=dim), axis, backward)  20.8 us
  transfers between devices with their start and end apart: 40, of which 35 were waited for; matrix products, arithmetic and copies ran while one was open for 1% of the time, Pallas kernels for 0%

commit v1 on v0

v1 whole, which is shorter than its diff:
```python
import functools
import math

import jax
import jax.numpy as jnp
import ml_dtypes
import numpy as np
from jax import lax
from jax.experimental import pallas as pl
from jax.experimental.pallas import tpu as pltpu
from jax.sharding import PartitionSpec as P

DAMPING = 1.0
UNROLL = 2


def dft_tables(width):
    ladder = np.arange(width, dtype=np.int64)
    angles = (ladder[:, None] * ladder[None, :] % width) * (2.0 * math.pi / width)
    real_part = np.cos(angles) / math.sqrt(width)
    imag_part = -np.sin(angles) / math.sqrt(width)
    table_one = np.block([[real_part, -imag_part], [imag_part, real_part]])
    table_two = np.block([[real_part, imag_part], [-imag_part, real_part]])
    return table_one.astype(ml_dtypes.bfloat16), table_two.astype(ml_dtypes.bfloat16)


def pair_swaps(count):
    even = [(i, i ^ 1) for i in range(count) if (i ^ 1) < count]
    if count < 3:
        return [even]
    odd = [(i, i + 1) for i in range(1, count - 1, 2)]
    if count % 2 == 0:
        odd = odd + [(count - 1, 0)]
    return [even, odd + [(target, source) for source, target in odd]]


def side_weights(axis):
    count = lax.axis_size(axis)
    place = lax.axis_index(axis)
    even = place % 2 == 0
    has_low = place > 0
    has_high = place + 1 < count
    flags = [even & has_high, ~even & has_low]
    if count > 2:
        flags = [~even & has_low, even & has_low, even & has_high, ~even & has_high]
    else:
        flags = [~even & has_low, even & has_high]
    return jnp.stack(flags).astype(jnp.float32)


def swap(axis, blocks):
    return [
        lax.ppermute(block, axis, pairs)
        for block, pairs in zip(blocks, pair_swaps(lax.axis_size(axis)))
    ]


def dot(left, right):
    return jnp.dot(left, right, preferred_element_type=jnp.float32)


def call(body, name, out_shapes, in_spaces, operands, out_spaces=None, scratch=()):
    specs = [pl.BlockSpec(memory_space=space) for space in in_spaces]
    out_spaces = out_spaces or [pltpu.VMEM] * len(out_shapes)
    return pl.pallas_call(
        body,
        name=name,
        out_shape=[jax.ShapeDtypeStruct(shape, jnp.float32) for shape in out_shapes],
        in_specs=specs,
        out_specs=[pl.BlockSpec(memory_space=space) for space in out_spaces],
        scratch_shapes=list(scratch),
        compiler_params=pltpu.CompilerParams(vmem_limit_bytes=60 * 2**20),
    )(*operands)


class Plan:
    def __init__(self, tile_rows, tile_cols, patch, modes, slots):
        self.tile_rows, self.tile_cols = tile_rows, tile_cols
        self.patch, self.modes, self.slots = patch, modes, slots
        self.rim = patch // 2
        self.rows = tile_rows + patch
        self.cols = tile_cols + patch

    def scratch(self):
        wide = self.patch
        return [
            pltpu.VMEM((2, self.rows, self.cols), jnp.float32),
            pltpu.VMEM((self.slots, 2, wide, wide), jnp.float32),
            pltpu.VMEM((UNROLL, 2 * wide, wide), jnp.bfloat16),
            pltpu.VMEM((UNROLL, 2 * wide, wide), jnp.bfloat16),
        ]

    def fill_region(self, region, middle, received, weights):
        rim, rows = self.rim, self.tile_rows
        count = len(received)
        low = sum(received[k][...] * weights[k] for k in range(count))
        high = sum(received[k][...] * weights[count + k] for k in range(count))
        region[:, :rim] = low
        region[:, rim : rim + rows] = middle[...]
        region[:, rim + rows :] = high

    def row_split(self, row):
        shift = lax.rem(row, 8)
        return pl.multiple_of(row - shift, 8), shift

    def take_windows(self, windows, region, centres):
        wide = self.patch
        for slot in range(self.slots):
            for part in range(2):
                base, shift = self.row_split(centres[slot, 0])
                strip = region[part, pl.ds(base, wide + 8), :]
                strip = pltpu.roll(strip, wide + 8 - shift, 0)[:wide]
                turned = pltpu.roll(strip, self.cols - centres[slot, 1], 1)
                windows[slot, part] = turned[:, :wide]

    def place(self, canvas, slot, part, piece, centres):
        strip = jnp.concatenate([piece, jnp.zeros((self.patch, self.cols - self.patch), jnp.float32)], 1)
        strip = jnp.concatenate([strip, jnp.zeros((8, self.cols), jnp.float32)], 0)
        base, shift = self.row_split(centres[slot, 0])
        turned = pltpu.roll(pltpu.roll(strip, centres[slot, 1], 1), shift, 0)
        canvas[part, pl.ds(base, self.patch + 8), :] += turned

    def each_modes(self, slot, body):
        def step(index, carry):
            body([index * UNROLL + j for j in range(UNROLL)])
            return carry

        lax.fori_loop(0, self.modes // UNROLL, step, 0)

    def spectra(self, slot, modes, probes, windows, wave, half, tables):
        wide = self.patch
        x_real, x_imag = windows[slot, 0], windows[slot, 1]
        for j, mode in enumerate(modes):
            p_real, p_imag = probes[mode, 0], probes[mode, 1]
            wave[j, :wide] = (p_real * x_real - p_imag * x_imag).astype(jnp.bfloat16)
            wave[j, wide:] = (p_real * x_imag + p_imag * x_real).astype(jnp.bfloat16)
        for j in range(len(modes)):
            half[j] = dot(tables[0][...], wave[j]).astype(jnp.bfloat16)
        return [
            dot(half[j, :wide], tables[1][:wide]) + dot(half[j, wide:], tables[1][wide:])
            for j in range(len(modes))
        ]

    def images(self, fields, weight, modes, probes, wave, half, tables):
        wide = self.patch
        for j, field in enumerate(fields):
            half[j, :wide] = (2.0 * field[:, :wide] * weight).astype(jnp.bfloat16)
            half[j, wide:] = (2.0 * field[:, wide:] * weight).astype(jnp.bfloat16)
        for j in range(len(modes)):
            turned = dot(half[j, :wide], tables[0][:wide]) + dot(half[j, wide:], tables[0][wide:])
            turned = turned.astype(jnp.bfloat16)
            wave[j, :wide] = turned[:, :wide]
            wave[j, wide:] = turned[:, wide:]
        real_sum = imag_sum = 0.0
        for j, mode in enumerate(modes):
            back = dot(tables[1][...], wave[j])
            p_real, p_imag = probes[mode, 0], probes[mode, 1]
            real_sum = real_sum + (p_real * back[:wide] + p_imag * back[wide:])
            imag_sum = imag_sum + (p_real * back[wide:] - p_imag * back[:wide])
        return real_sum, imag_sum

    def send(self, canvas, parity, middle_out, sends):
        rim, rows = self.rim, self.tile_rows
        middle_out[...] = canvas[:, rim : rim + rows]
        for k, out in enumerate(sends):
            upper = parity[0] if k == 0 else 1 - parity[0]
            start = pl.multiple_of((1 - upper) * (rim + rows), 8)
            out[...] = canvas[:, pl.ds(start, rim), :]


def start_body(plan, swaps, shards, *refs):
    refs = list(refs)
    info, centres, weights, middle = refs[:4]
    received = refs[4 : 4 + swaps]
    shard, *rest = refs[4 + swaps : 4 + swaps + 2 * shards - 1]
    direct, crossed = rest[: shards - 1], rest[shards - 1 :]
    targets, one, two = refs[3 + swaps + 2 * shards : 6 + swaps + 2 * shards]
    spectra, intensity, probes, middle_out, *tail = refs[6 + swaps + 2 * shards :]
    sends = tail[:swaps]
    region, windows, wave, half, image = tail[swaps:]
    wide, lead = plan.patch, plan.modes // shards
    tables = (one, two)
    place, side = info[2], info[3]
    span = wide // 2

    probes[pl.ds(place * lead, lead)] = shard[...]
    for k in range(1, shards):
        home = lax.rem(place - k + shards, shards) * lead
        near = pl.multiple_of(side * span, 8)
        far = pl.multiple_of((1 - side) * span, 8)
        probes[pl.ds(home, lead), :, pl.ds(near, span), :] = direct[k - 1][...]
        probes[pl.ds(home, lead), :, pl.ds(far, span), :] = crossed[k - 1][...]

    plan.fill_region(region, middle, received, weights)
    plan.take_windows(windows, region, centres)
    region[...] = jnp.zeros_like(region)
    for slot in range(plan.slots):
        intensity[slot] = jnp.zeros((wide, wide), jnp.float32)

        def forward(modes):
            fields = plan.spectra(slot, modes, probes, windows, wave, half, tables)
            power = 0.0
            for mode, field in zip(modes, fields):
                spectra[slot * plan.modes + mode] = field
                power = power + (field[:, :wide] * field[:, :wide] + field[:, wide:] * field[:, wide:])
            intensity[slot] += power

        plan.each_modes(slot, forward)
        live = jnp.where(slot < info[0], 1.0, 0.0)
        windows[slot, 0] = live * (intensity[slot] - targets[slot])
        image[...] = jnp.zeros_like(image)

        def backward(modes):
            fields = [spectra[slot * plan.modes + mode] for mode in modes]
            real_sum, imag_sum = plan.images(fields, windows[slot, 0], modes, probes, wave, half, tables)
            image[0] += real_sum
            image[1] += imag_sum

        plan.each_modes(slot, backward)
        for part in range(2):
            plan.place(region, slot, part, image[part], centres)
    plan.send(region, [info[1]], middle_out, sends)


def change_body(plan, swaps, last, *refs):
    refs = list(refs)
    info, centres, weights, middle = refs[:4]
    received = refs[4 : 4 + swaps]
    spectra, probes, one, two = refs[4 + swaps : 8 + swaps]
    outs = refs[8 + swaps :]
    if last:
        sums, region, windows, wave, half, change, power = outs
    else:
        sums, moved, change, power, region, windows, wave, half = outs
    wide, rim = plan.patch, plan.rim
    tables = (one, two)
    plan.fill_region(region, middle, received, weights)
    plan.take_windows(windows, region, centres)
    own = middle[:, :, rim : rim + plan.tile_cols]
    sums[0] = jnp.sum(own * own)
    bend = 0.0
    for slot in range(plan.slots):
        change[slot] = jnp.zeros((wide, wide), jnp.float32)
        if not last:
            power[slot] = jnp.zeros((wide, wide), jnp.float32)

        def forward(modes):
            fields = plan.spectra(slot, modes, probes, windows, wave, half, tables)
            cross = square = 0.0
            for mode, field in zip(modes, fields):
                base = spectra[slot * plan.modes + mode]
                cross = cross + (base[:, :wide] * field[:, :wide] + base[:, wide:] * field[:, wide:])
                if not last:
                    moved[slot * plan.modes + mode] = field
                    square = square + (
                        field[:, :wide] * field[:, :wide] + field[:, wide:] * field[:, wide:]
                    )
            change[slot] += 2.0 * cross
            if not last:
                power[slot] += square

        plan.each_modes(slot, forward)
        live = jnp.where(slot < info[0], 1.0, 0.0)
        bend = bend + live * jnp.sum(change[slot] * change[slot])
    sums[1] = bend


def image_body(plan, swaps, parts, *refs):
    refs = list(refs)
    info, centres = refs[:2]
    totals = refs[2 : 2 + parts]
    spectra, moved, intensity, change, power, probes, targets, one, two = refs[2 + parts : 11 + parts]
    fresh, step_out, middle_out, *tail = refs[11 + parts :]
    sends = tail[:swaps]
    region, windows, wave, half, image = tail[swaps:]
    tables = (one, two)
    step = step_of(totals)
    step_out[0] = step
    region[...] = jnp.zeros_like(region)
    for slot in range(plan.slots):
        live = jnp.where(slot < info[0], 1.0, 0.0)
        bright = intensity[slot] + step * (change[slot] + step * power[slot])
        windows[slot, 0] = live * (bright - targets[slot])
        image[...] = jnp.zeros_like(image)

        def backward(modes):
            fields = []
            for mode in modes:
                field = spectra[slot * plan.modes + mode] + step * moved[slot * plan.modes + mode]
                fresh[slot * plan.modes + mode] = field
                fields.append(field)
            real_sum, imag_sum = plan.images(fields, windows[slot, 0], modes, probes, wave, half, tables)
            image[0] += real_sum
            image[1] += imag_sum

        plan.each_modes(slot, backward)
        for part in range(2):
            plan.place(region, slot, part, image[part], centres)
    plan.send(region, [info[1]], middle_out, sends)


def step_of(totals):
    values = [[part[k] for part in totals] for k in range(2)]
    while len(values[0]) > 1:
        values = [[v[i] + v[i + 1] for i in range(0, len(v), 2)] for v in values]
    norm, bend = values[0][0], values[1][0]
    top = jnp.full((8, 128), norm, jnp.float32)
    return jnp.max(top / (bend + DAMPING * norm))


def totals_of(sums):
    if lax.axis_size("gx") == 2:
        sums = sums + swap("gx", [sums])[0]
    else:
        sums = lax.psum(sums, "gx")
    count = lax.axis_size("gy")
    if count & (count - 1):
        return [lax.psum(sums, "gy")]
    return [sums] + [
        lax.ppermute(sums, "gy", [(i, i ^ step) for i in range(count)]) for step in range(1, count)
    ]


def shards(object_field, probe_shard, measured, positions, slot_counts):
    patch = probe_shard.shape[-1]
    tile_rows, tile_cols = object_field.shape[1:]
    groups = lax.axis_size("ma")
    modes = probe_shard.shape[0] * groups
    slots = measured.shape[2]
    plan = Plan(tile_rows, tile_cols, patch, modes, slots)
    rim, units = plan.rim, slots * modes
    one, two = (jnp.asarray(table) for table in dft_tables(patch))
    targets = measured[0, 0]
    centres = positions[0, 0]
    gx, gy, ma = (lax.axis_index(axis) for axis in ("gx", "gy", "ma"))
    even_x, even_y = gx % 2 == 0, gy % 2 == 0
    info = jnp.stack([slot_counts[0, 0], even_x.astype(jnp.int32) * 0 + gx % 2, ma, gx % 2])
    swaps_x, swaps_y = (len(pair_swaps(lax.axis_size(axis))) for axis in ("gx", "gy"))
    weights_x = side_weights("gx")
    smem, vmem = pltpu.SMEM, pltpu.VMEM
    tall = (2, tile_rows, plan.cols)
    fold = (2, rim, plan.cols)
    image_scratch = pltpu.VMEM((2, patch, patch), jnp.float32)

    def halves(block, dim, low_start, high_start, width, is_even, swaps):
        def piece(start):
            return lax.dynamic_slice_in_dim(block, start, width, dim)

        first = piece(jnp.where(is_even, high_start, low_start))
        return [first] + [piece(jnp.where(is_even, low_start, high_start))] * (swaps - 1)

    def rows_around(middle):
        if rim == tile_rows:
            return swap("gx", [middle] * swaps_x)
        return swap("gx", halves(middle, 1, 0, tile_rows - rim, rim, even_x, swaps_x))

    def sides(axis, received):
        weights = side_weights(axis)
        count = len(received)
        low = sum(received[k] * weights[k] for k in range(count))
        high = sum(received[k] * weights[count + k] for k in range(count))
        return low, high

    def descent(middle, sends):
        low, high = sides("gx", swap("gx", sends))
        gap = tile_rows - rim
        middle = middle + jnp.pad(low, ((0, 0), (0, gap), (0, 0)))
        middle = middle + jnp.pad(high, ((0, 0), (gap, 0), (0, 0)))
        blocks = halves(middle, 2, 0, tile_cols, patch, even_y, swaps_y)
        low, high = sides("gy", swap("gy", blocks))
        column = jnp.arange(plan.cols)
        first = jnp.where(gy == 0, rim, 0)
        final = jnp.where(gy == lax.axis_size("gy") - 1, rim + tile_cols, plan.cols)
        middle = middle + jnp.pad(low, ((0, 0), (0, 0), (0, tile_cols)))
        middle = middle + jnp.pad(high, ((0, 0), (0, 0), (tile_cols, 0)))
        return jnp.where((column >= first) & (column < final), -middle, 0.0)

    def own(middle):
        return middle[:, :, rim : rim + tile_cols]

    span = patch // 2
    mine = lax.dynamic_slice_in_dim(probe_shard, (gx % 2) * span, span, 2)
    direct = [
        lax.ppermute(mine, "ma", [(i, (i + k) % groups) for i in range(groups)])
        for k in range(1, groups)
    ]
    crossed = [swap("gx", [block])[0] for block in direct]

    blocks = halves(object_field, 2, 0, tile_cols - rim, rim, even_y, swaps_y)
    low, high = sides("gy", swap("gy", blocks))
    middle = jnp.concatenate([low, object_field, high], 2)

    spectra, intensity, probes, middle, *sends = call(
        functools.partial(start_body, plan, swaps_x, groups),
        "start",
        [(units, patch, 2 * patch), (slots, patch, patch), (modes, 2, patch, patch), tall]
        + [fold] * swaps_x,
        [smem] * 3 + [vmem] * (1 + swaps_x + 2 * groups - 1 + 3),
        [info, centres, weights_x, middle, *rows_around(middle), probe_shard]
        + direct
        + crossed
        + [targets, one, two],
        scratch=plan.scratch() + [image_scratch],
    )
    middle = descent(middle, sends)
    sums, moved, change, power = call(
        functools.partial(change_body, plan, swaps_x, False),
        "change",
        [(2,), (units, patch, 2 * patch), (slots, patch, patch), (slots, patch, patch)],
        [smem] * 3 + [vmem] * (5 + swaps_x),
        [info, centres, weights_x, middle, *rows_around(middle), spectra, probes, one, two],
        [smem] + [vmem] * 3,
        scratch=plan.scratch(),
    )
    first_way = own(middle)
    totals = totals_of(sums)
    spectra, first_step, middle, *sends = call(
        functools.partial(image_body, plan, swaps_x, len(totals)),
        "image",
        [(units, patch, 2 * patch), (1,), tall] + [fold] * swaps_x,
        [smem] * (2 + len(totals)) + [vmem] * 9,
        [info, centres, *totals, spectra, moved, intensity, change, power, probes, targets, one, two],
        [vmem, smem] + [vmem] * (1 + swaps_x),
        scratch=plan.scratch() + [image_scratch],
    )
    middle = descent(middle, sends)
    (sums,) = call(
        functools.partial(change_body, plan, swaps_x, True),
        "last_change",
        [(2,)],
        [smem] * 3 + [vmem] * (5 + swaps_x),
        [info, centres, weights_x, middle, *rows_around(middle), spectra, probes, one, two],
        [smem],
        scratch=plan.scratch()
        + [pltpu.VMEM((slots, patch, patch), jnp.float32), pltpu.VMEM((1, 8, 128), jnp.float32)],
    )
    totals = sum(totals_of(sums))
    last_step = totals[0] / (totals[1] + DAMPING * totals[0])
    return object_field + first_step[0] * first_way + last_step * own(middle)


def solution(mesh):
    return jax.shard_map(
        shards,
        mesh=mesh,
        in_specs=(
            P(None, "gx", "gy"),
            P("ma", None, None, None),
            P("gx", "gy", None, None, None),
            P("gx", "gy", None, None),
            P("gx", "gy"),
        ),
        out_specs=P(None, "gx", "gy"),
        check_vma=False,
    )
```

time: 809 us -> 202 us (0.25); the launches traced: 797 us -> 202 us
  waiting for transfers between devices: 486 us -> 73.2 us
  blocking collectives: 80.8 us -> 0 us
  local copies, waits for them, and re-layouts: 87.9 us -> 8.44 us
  Pallas kernels: 0 us -> 75.4 us
  starting transfers between devices: 60.3 us -> 23 us
  between operations: 26.1 us -> 2.86 us
  other arithmetic: 40.6 us -> 18.9 us
  matrix products: 15.7 us -> 0 us
    psum x8 -> x0, waiting for transfers between devices: 283 us -> none  [the longest x4 148 us: mode_total(): return lax.psum(partial_value, 'ma')]
    ppermute x32 -> x25, waiting for transfers between devices: 203 us -> 73.2 us  [the longest x16 37.5 us: swap(): lax.ppermute(block, axis, pairs)]
    psum x2 -> x0, blocking collectives: 80.8 us -> none  [shards(): norm_now = lax.psum(local_sum(residual, residual), ('gx', 'gy', 'ma'))]
    pallas_call x0 -> x4, Pallas kernels: none -> 75.4 us  [call(): pl.pallas_call(body, name=name, out_shape=[jax.ShapeDtypeStruct(shape, jn...]
    dynamic_update_slice x8 -> x0, local copies, waits for them, and re-layouts: 58.6 us -> none  [project(): lax.dynamic_update_slice(extended, lax.dynamic_slice(extended, corner, (2...]
    ppermute x32 -> x25, starting transfers between devices: 59.8 us -> 23 us  [the longest x16 9.95 us: swap(): lax.ppermute(block, axis, pairs)]
    dot_general x16 -> x0, matrix products: 15.7 us -> none  [the longest x4 6.75 us: adjoint_transform(): jnp.einsum('bik,kl->bil', weighted, tables[0], preferred_element_type=jnp...]
    mul x15 -> x0, other arithmetic: 10.7 us -> none  [the longest x4 2.71 us: exit_waves(): real_part = probe_real * window_real - probe_imag * window_imag]
  transfers between devices with their start and end apart: 40 -> 25, of which waited for: 35 -> 20; matrix products, arithmetic and copies ran while one was open for 1% -> 4% of each run, Pallas kernels for 0% -> 0%
where the time goes in v1:
time: 202 us
  Pallas kernels  75.4 us (37%)
  waiting for transfers between devices  73.2 us (36%)
  starting transfers between devices  23 us (11%)
  other arithmetic  18.9 us (9%)
  local copies, waits for them, and re-layouts  8.44 us (4%)
  between operations  2.86 us (1%)
    pallas_call x4, Pallas kernels, call(): pl.pallas_call(body, name=name, out_shape=[jax.ShapeDtypeStruct(shape, jn...  75.4 us
    ppermute x16, waiting for transfers between devices, swap(): lax.ppermute(block, axis, pairs)  37.5 us
    ppermute x3, waiting for transfers between devices, shards(): lax.ppermute(mine, 'ma', [(i, (i + k) % groups) for i in range(groups)])  30.6 us
    ppermute x16, starting transfers between devices, swap(): lax.ppermute(block, axis, pairs)  9.95 us
    add x3, other arithmetic, sides(): low = sum((received[k] * weights[k] for k in range(count)))  7.77 us
    ppermute x6, starting transfers between devices, totals_of(): lax.ppermute(sums, 'gy', [(i, i ^ step) for i in range(count)])  6.98 us
    ppermute x3, starting transfers between devices, shards(): lax.ppermute(mine, 'ma', [(i, (i + k) % groups) for i in range(groups)])  6.09 us
    ppermute x6, waiting for transfers between devices, totals_of(): lax.ppermute(sums, 'gy', [(i, i ^ step) for i in range(count)])  5.11 us
  transfers between devices with their start and end apart: 25, of which 20 were waited for; matrix products, arithmetic and copies ran while one was open for 4% of the time, Pallas kernels for 0%

profile of v1, /device:TPU:0, one launch (start us, length us, event | category | flops | bytes accessed | tf_op | source)
XLA Modules:
  0.0 201.9 jit_solution(17859711343999338261)
XLA Ops:
  0.0 1.9 constant_dynamic-slice_fusion.4
  1.9 5.1 %collective-permute-start.5 = (f32[2,2,128,256]{3,2,1,0:T(8,128)}, f32[2,2,128,256]{3,2,1,0:T(8,128)S(1)}, u32[]{:S(2)}, u32[]{:S(2)}) collective-permute-start(f32[2,2,128,256]{3,2,1,0:T(8,128)} %constant_dynamic-slice_fusion.4), channel_id=1, source_target_pairs={{0,3},{1,0},{2,1},{3,2},{4,7},{5,4},{6,5},{7,6},{8,11},{9,8},{10,9... | collective-permute-start | bytes 1572872 | tf_op jit(solution)/shard_map/ppermute | solution.py:384
  7.0 1.0 collective-permute-start.3
  8.0 1.0 constant_dynamic-slice_fusion.6
  9.0 1.6 collective-permute-start
  10.5 1.5 collective-permute-start.1
  12.1 0.7 fusion.5
  12.7 2.5 %collective-permute-done = f32[2,128,128]{2,1,0:T(8,128)S(1)} collective-permute-done((f32[2,128,128]{2,1,0:T(8,128)S(1)}, f32[2,128,128]{2,1,0:T(8,128)S(1)}, u32[]{:S(2)}, u32[]{:S(2)}) %collective-permute-start) | collective-permute-done | bytes 131104 | tf_op jit(solution)/shard_map/ppermute | solution.py:53
  15.2 2.0 collective-permute-done.1
  17.2 2.6 %multiply_add_fusion.7 = (f32[2,128,128]{2,1,0:T(8,128)S(1)}, f32[2,128,128]{2,1,0:T(8,128)S(1)}) fusion(f32[2,128,128]{2,1,0:T(8,128)S(1)} %collective-permute-done.1, f32[2,128,128]{2,1,0:T(8,128)S(1)} %collective-permute-done, f32[]{:T(128)} %bitcast.11, f32[]{:T(128)} %bitcast.10, f32[]{:T(128)} %bitcast.13, f32[]{:T(128)} %bitcast.12), kind=kLoop, calls=%fused_computation.14 | loop fusion | flops 196608 | bytes 524304 | tf_op jit(solution)/shard_map/add | solution.py:360
  19.8 1.0 pad_maximum_fusion.refs_3_
  21.4 30.6 %collective-permute-done.4.refs_7_ = f32[2,2,128,256]{3,2,1,0:T(8,128)S(1)} collective-permute-done((f32[2,2,128,256]{3,2,1,0:T(8,128)}, f32[2,2,128,256]{3,2,1,0:T(8,128)S(1)}, u32[]{:S(2)}, u32[]{:S(2)}) %collective-permute-start.4) | collective-permute-done | bytes 524320 | tf_op jit(solution)/shard_map/ppermute | solution.py:384
  53.1 0.7 add_convert_fusion.refs_2_
  53.8 0.6 pad_add_fusion.refs_0_
  55.4 24.4 %start.1 = (f32[16,256,512]{2,1,0:T(8,128)}, f32[2,256,256]{2,1,0:T(8,128)}, f32[8,2,256,256]{3,2,1,0:T(8,128)}, f32[2,128,512]{2,1,0:T(8,128)}, f32[2,128,512]{2,1,0:T(8,128)}) custom-call(s32[4]{0:T(128)} %pad_add_fusion.refs_0_, s32[2,2]{1,0:T(2,128)} %bitcast.23, f32[2]{0:T(128)} %add_convert_fusion.refs_2_, f32[2,128,512]{2,1,0:T(8,128)} %copy-done.4, ...), custom_call_target="tpu_custom_call" | custom-call | tf_op jit(solution)/shard_map/start/pallas_call | solution.py:65
  80.0 1.4 fusion.4
  82.0 2.5 %multiply_add_fusion.1 = f32[2,128,512]{2,1,0:T(8,128)S(1)} fusion(f32[2,128,512]{2,1,0:T(8,128)S(1)} %collective-permute-done.9, f32[2,128,512]{2,1,0:T(8,128)} %get-tuple-element.18, f32[]{:T(128)} %bitcast.16, f32[]{:T(128)} %bitcast.15), kind=kLoop, calls=%fused_computation.4 | loop fusion | flops 524288 | bytes 1572872 | tf_op jit(solution)/shard_map/add | solution.py:368
  84.5 1.6 collective-permute-start.10
  86.1 1.5 collective-permute-start.11
  87.6 6.2 %collective-permute-done.10 = f32[2,128,256]{2,1,0:T(8,128)S(1)} collective-permute-done((f32[2,128,256]{2,1,0:T(8,128)S(1)}, f32[2,128,256]{2,1,0:T(8,128)S(1)}, u32[]{:S(2)}, u32[]{:S(2)}) %collective-permute-start.10) | collective-permute-done | bytes 262176 | tf_op jit(solution)/shard_map/ppermute | solution.py:53
  93.8 5.8 %collective-permute-done.11 = f32[2,128,256]{2,1,0:T(8,128)S(1)} collective-permute-done((f32[2,128,256]{2,1,0:T(8,128)S(1)}, f32[2,128,256]{2,1,0:T(8,128)S(1)}, u32[]{:S(2)}, u32[]{:S(2)}) %collective-permute-start.11) | collective-permute-done | bytes 262176 | tf_op jit(solution)/shard_map/ppermute | solution.py:53
  99.5 2.6 %multiply_add_fusion.5 = (f32[2,128,256]{2,1,0:T(8,128)S(1)}, f32[2,128,256]{2,1,0:T(8,128)S(1)}) fusion(f32[2,128,256]{2,1,0:T(8,128)S(1)} %collective-permute-done.11, f32[2,128,256]{2,1,0:T(8,128)S(1)} %collective-permute-done.10, f32[]{:T(128)} %bitcast.11, f32[]{:T(128)} %bitcast.10, f32[]{:T(128)} %bitcast.13, f32[]{:T(128)} %bitcast.12), kind=kLoop, calls=%fused_computation.12 | loop fusion | flops 393216 | bytes 1048592 | tf_op jit(solution)/shard_map/add | solution.py:360
  102.3 1.9 collective-permute-done.12.refs_4_
  104.2 0.8 copy-done.11
  105.0 17.1 %change.1 = (f32[2]{0:T(128)}, f32[16,256,512]{2,1,0:T(8,128)}, f32[2,256,256]{2,1,0:T(8,128)}, f32[2,256,256]{2,1,0:T(8,128)}) custom-call(s32[4]{0:T(128)} %pad_add_fusion.refs_0_, s32[2,2]{1,0:T(2,128)} %bitcast.24, f32[2]{0:T(128)} %add_convert_fusion.refs_2_, f32[2,128,512]{2,1,0:T(8,128)} %copy-done, f32[2,128,512]{2,1,0:T(8,128)} %copy-done.11, ...), custom_call_target="tpu_custom_call" | custom-call | tf_op jit(solution)/shard_map/change/pallas_call | solution.py:65
  122.3 1.2 collective-permute-done.13
  123.6 0.6 add.121.refs_2_
  124.2 1.4 collective-permute-start.16
  125.6 1.5 collective-permute-start.15
  127.7 1.0 collective-permute-done.16.refs_5_
  129.2 1.5 collective-permute-done.14.refs_3_
  131.2 19.8 %image.1 = (f32[16,256,512]{2,1,0:T(8,128)}, f32[1]{0:T(128)}, f32[2,128,512]{2,1,0:T(8,128)}, f32[2,128,512]{2,1,0:T(8,128)}) custom-call(s32[4]{0:T(128)} %pad_add_fusion.refs_0_, s32[2,2]{1,0:T(2,128)} %bitcast.25, f32[2]{0:T(128)} %copy-done.12, f32[2]{0:T(128)} %copy-done.15, f32[2]{0:T(128)} %copy-done.14, f32[2]{0:T(128)} %copy-done.13, ...), custom_call_target="tpu_custom_call" | custom-call | tf_op jit(solution)/shard_map/image/pallas_call | solution.py:65
  151.1 2.1 %collective-permute-done.17 = f32[2,128,512]{2,1,0:T(8,128)S(1)} collective-permute-done((f32[2,128,512]{2,1,0:T(8,128)}, f32[2,128,512]{2,1,0:T(8,128)S(1)}, u32[]{:S(2)}, u32[]{:S(2)}) %collective-permute-start.17) | collective-permute-done | bytes 524320 | tf_op jit(solution)/shard_map/ppermute | solution.py:53
  153.2 2.5 %multiply_add_fusion = f32[2,128,512]{2,1,0:T(8,128)S(1)} fusion(f32[2,128,512]{2,1,0:T(8,128)S(1)} %collective-permute-done.17, f32[2,128,512]{2,1,0:T(8,128)} %get-tuple-element.28, f32[]{:T(128)} %bitcast.16, f32[]{:T(128)} %bitcast.15), kind=kLoop, calls=%fused_computation.2 | loop fusion | flops 524288 | bytes 1572872 | tf_op jit(solution)/shard_map/add | solution.py:368
  155.8 0.6 collective-permute-start.18
  156.4 1.4 collective-permute-start.19
  157.8 7.2 %collective-permute-done.18 = f32[2,128,256]{2,1,0:T(8,128)S(1)} collective-permute-done((f32[2,128,256]{2,1,0:T(8,128)S(1)}, f32[2,128,256]{2,1,0:T(8,128)S(1)}, u32[]{:S(2)}, u32[]{:S(2)}) %collective-permute-start.18) | collective-permute-done | bytes 262176 | tf_op jit(solution)/shard_map/ppermute | solution.py:53
  165.0 4.7 %collective-permute-done.19 = f32[2,128,256]{2,1,0:T(8,128)S(1)} collective-permute-done((f32[2,128,256]{2,1,0:T(8,128)S(1)}, f32[2,128,256]{2,1,0:T(8,128)S(1)}, u32[]{:S(2)}, u32[]{:S(2)}) %collective-permute-start.19) | collective-permute-done | bytes 262176 | tf_op jit(solution)/shard_map/ppermute | solution.py:53
  169.8 2.6 %multiply_add_fusion.3 = (f32[2,128,256]{2,1,0:T(8,128)S(1)}, f32[2,128,256]{2,1,0:T(8,128)S(1)}) fusion(f32[2,128,256]{2,1,0:T(8,128)S(1)} %collective-permute-done.19, f32[2,128,256]{2,1,0:T(8,128)S(1)} %collective-permute-done.18, f32[]{:T(128)} %bitcast.11, f32[]{:T(128)} %bitcast.10, f32[]{:T(128)} %bitcast.13, f32[]{:T(128)} %bitcast.12), kind=kLoop, calls=%fused_computation.10 | loop fusion | flops 393216 | bytes 1048592 | tf_op jit(solution)/shard_map/add | solution.py:360
  172.6 1.9 collective-permute-done.20.refs_4_
  174.5 0.8 copy-done.10
  175.3 14.1 %last_change.1 = f32[2]{0:T(128)} custom-call(s32[4]{0:T(128)} %pad_add_fusion.refs_0_, s32[2,2]{1,0:T(2,128)} %bitcast.26, f32[2]{0:T(128)} %add_convert_fusion.refs_2_, f32[2,128,512]{2,1,0:T(8,128)} %copy-done.2, f32[2,128,512]{2,1,0:T(8,128)} %copy-done.10, f32[16,256,512]{2,1,0:T(8,128)} %get-tuple-element.30.refs_5_, ...), custom_call_target="tpu_custom_call" | custom-call | tf_op jit(solution)/shard_map/last_change/pallas_call | solution.py:65
  189.6 1.1 collective-permute-done.21
  190.7 0.7 add.129
  191.4 1.5 collective-permute-start.24
  193.4 1.5 collective-permute-start.22
  194.9 1.0 collective-permute-done.24
  199.5 2.4 %fusion = f32[2,128,256]{2,1,0:T(8,128)} fusion(f32[2,128,512]{2,1,0:T(8,128)} %copy-done.2, f32[2,128,256]{2,1,0:T(8,128)S(1)} %copy-done.3, f32[2,128,512]{2,1,0:T(8,128)S(1)} %copy-done.1, f32[]{:T(128)S(6)} %div.3, f32[]{:T(128)} %bitcast.17), kind=kLoop, calls=%fused_computation.6 | loop fusion | flops 262144 | bytes 1048584 | tf_op jit(solution)/shard_map/add | solution.py:439
  (61 shorter events, 7.6 us)
Async XLA Ops:
  1.9 19.0 %collective-permute-start.5 = (f32[2,2,128,256]{3,2,1,0:T(8,128)}, f32[2,2,128,256]{3,2,1,0:T(8,128)S(1)}, u32[]{:S(2)}, u32[]{:S(2)}) collective-permute-start(f32[2,2,128,256]{3,2,1,0:T(8,128)} %constant_dynamic-slice_fusion.4), channel_id=1, source_target_pairs={{0,3},{1,0},{2,1},{3,2},{4,7},{5,4},{6,5},{7,6},{8,11},{9,8},{10,9... | collective-permute-start | bytes 1572872 | tf_op jit(solution)/shard_map/ppermute | solution.py:384
  6.9 45.0 %collective-permute-start.4 = (f32[2,2,128,256]{3,2,1,0:T(8,128)}, f32[2,2,128,256]{3,2,1,0:T(8,128)S(1)}, u32[]{:S(2)}, u32[]{:S(2)}) collective-permute-start(f32[2,2,128,256]{3,2,1,0:T(8,128)} %constant_dynamic-slice_fusion.4), channel_id=1, source_target_pairs={{0,2},{1,3},{2,0},{3,1},{4,6},{5,7},{6,4},{7,5},{8,10},{9,11},{10,... | collective-permute-start | bytes 1572872 | tf_op jit(solution)/shard_map/ppermute | solution.py:384
  7.0 45.0 %collective-permute-start.3 = (f32[2,2,128,256]{3,2,1,0:T(8,128)}, f32[2,2,128,256]{3,2,1,0:T(8,128)S(1)}, u32[]{:S(2)}, u32[]{:S(2)}) collective-permute-start(f32[2,2,128,256]{3,2,1,0:T(8,128)} %constant_dynamic-slice_fusion.4), channel_id=1, source_target_pairs={{0,1},{1,2},{2,3},{3,0},{4,5},{5,6},{6,7},{7,4},{8,9},{9,10},{10,1... | collective-permute-start | bytes 1572872 | tf_op jit(solution)/shard_map/ppermute | solution.py:384
  9.0 6.2 %collective-permute-start = (f32[2,128,128]{2,1,0:T(8,128)S(1)}, f32[2,128,128]{2,1,0:T(8,128)S(1)}, u32[]{:S(2)}, u32[]{:S(2)}) collective-permute-start(f32[2,128,128]{2,1,0:T(8,128)S(1)} %get-tuple-element.41), channel_id=1, source_target_pairs={{0,4},{4,0},{8,12},{12,8},{1,5},{5,1},{9,13},{13,9},{2,6},{6,2},{1... | collective-permute-start | bytes 393224 | tf_op jit(solution)/shard_map/ppermute | solution.py:53
  10.5 6.7 %collective-permute-start.1 = (f32[2,128,128]{2,1,0:T(8,128)S(1)}, f32[2,128,128]{2,1,0:T(8,128)S(1)}, u32[]{:S(2)}, u32[]{:S(2)}) collective-permute-start(f32[2,128,128]{2,1,0:T(8,128)S(1)} %get-tuple-element.42), channel_id=1, source_target_pairs={{4,8},{12,0},{8,4},{0,12},{5,9},{13,1},{9,5},{1,13},{6,10},{14,2},... | collective-permute-start | bytes 393224 | tf_op jit(solution)/shard_map/ppermute | solution.py:53
  20.8 34.0 %copy-start.4 = (f32[2,128,512]{2,1,0:T(8,128)}, f32[2,128,512]{2,1,0:T(8,128)S(1)}, u32[]{:S(2)}) copy-start(f32[2,128,512]{2,1,0:T(8,128)S(1)} %pad_maximum_fusion.refs_3_) | copy-start | bytes 1572868
  20.8 33.7 %collective-permute-start.2 = (f32[2,128,512]{2,1,0:T(8,128)S(1)}, f32[2,128,512]{2,1,0:T(8,128)S(1)}, u32[]{:S(2)}, u32[]{:S(2)}) collective-permute-start(f32[2,128,512]{2,1,0:T(8,128)S(1)} %pad_maximum_fusion.refs_3_), channel_id=1, source_target_pairs={{0,16},{16,0},{1,17},{17,1},{2,18},{18,2},{3,19},{19,3},{4,20},{20... | collective-permute-start | bytes 1572872 | tf_op jit(solution)/shard_map/ppermute | solution.py:53
  20.9 33.9 %copy-start.5 = (f32[2,2,128,256]{3,2,1,0:T(8,128)}, f32[2,2,128,256]{3,2,1,0:T(8,128)S(1)}, u32[]{:S(2)}) copy-start(f32[2,2,128,256]{3,2,1,0:T(8,128)S(1)} %collective-permute-done.5.refs_8_) | copy-start | bytes 1572868
  20.9 33.6 %collective-permute-start.8 = (f32[2,2,128,256]{3,2,1,0:T(8,128)S(1)}, f32[2,2,128,256]{3,2,1,0:T(8,128)S(1)}, u32[]{:S(2)}, u32[]{:S(2)}) collective-permute-start(f32[2,2,128,256]{3,2,1,0:T(8,128)S(1)} %collective-permute-done.5.refs_8_), channel_id=1, source_target_pairs={{0,16},{16,0},{1,17},{17,1},{2,18},{18,2},{3,19},{19,3},{4,20},{20... | collective-permute-start | bytes 1572872 | tf_op jit(solution)/shard_map/ppermute | solution.py:53
  51.9 2.8 %copy-start.6 = (f32[2,2,128,256]{3,2,1,0:T(8,128)}, f32[2,2,128,256]{3,2,1,0:T(8,128)S(1)}, u32[]{:S(2)}) copy-start(f32[2,2,128,256]{3,2,1,0:T(8,128)S(1)} %collective-permute-done.4.refs_7_) | copy-start | bytes 1572868
  51.9 2.5 %collective-permute-start.7 = (f32[2,2,128,256]{3,2,1,0:T(8,128)S(1)}, f32[2,2,128,256]{3,2,1,0:T(8,128)}, u32[]{:S(2)}, u32[]{:S(2)}) collective-permute-start(f32[2,2,128,256]{3,2,1,0:T(8,128)S(1)} %collective-permute-done.4.refs_7_), channel_id=1, source_target_pairs={{0,16},{16,0},{1,17},{17,1},{2,18},{18,2},{3,19},{19,3},{4,20},{20... | collective-permute-start | bytes 1572872 | tf_op jit(solution)/shard_map/ppermute | solution.py:53
  52.0 2.8 %copy-start.7 = (f32[2,2,128,256]{3,2,1,0:T(8,128)}, f32[2,2,128,256]{3,2,1,0:T(8,128)S(1)}, u32[]{:S(2)}) copy-start(f32[2,2,128,256]{3,2,1,0:T(8,128)S(1)} %collective-permute-done.3.refs_6_) | copy-start | bytes 1572868
  52.0 2.8 %collective-permute-start.6 = (f32[2,2,128,256]{3,2,1,0:T(8,128)S(1)}, f32[2,2,128,256]{3,2,1,0:T(8,128)}, u32[]{:S(2)}, u32[]{:S(2)}) collective-permute-start(f32[2,2,128,256]{3,2,1,0:T(8,128)S(1)} %collective-permute-done.3.refs_6_), channel_id=1, source_target_pairs={{0,16},{16,0},{1,17},{17,1},{2,18},{18,2},{3,19},{19,3},{4,20},{20... | collective-permute-start | bytes 1572872 | tf_op jit(solution)/shard_map/ppermute | solution.py:53
  54.4 0.8 copy-start.8
  54.4 1.0 copy-start.9
  79.9 2.1 %collective-permute-start.9 = (f32[2,128,512]{2,1,0:T(8,128)}, f32[2,128,512]{2,1,0:T(8,128)S(1)}, u32[]{:S(2)}, u32[]{:S(2)}) collective-permute-start(f32[2,128,512]{2,1,0:T(8,128)} %get-tuple-element.19), channel_id=1, source_target_pairs={{0,16},{16,0},{1,17},{17,1},{2,18},{18,2},{3,19},{19,3},{4,20},{20... | collective-permute-start | bytes 1572872 | tf_op jit(solution)/shard_map/ppermute | solution.py:53
  84.5 9.2 %collective-permute-start.10 = (f32[2,128,256]{2,1,0:T(8,128)S(1)}, f32[2,128,256]{2,1,0:T(8,128)S(1)}, u32[]{:S(2)}, u32[]{:S(2)}) collective-permute-start(f32[2,128,256]{2,1,0:T(8,128)S(1)} %get-tuple-element.37), channel_id=1, source_target_pairs={{0,4},{4,0},{8,12},{12,8},{1,5},{5,1},{9,13},{13,9},{2,6},{6,2},{1... | collective-permute-start | bytes 786440 | tf_op jit(solution)/shard_map/ppermute | solution.py:53
  86.1 13.4 %collective-permute-start.11 = (f32[2,128,256]{2,1,0:T(8,128)S(1)}, f32[2,128,256]{2,1,0:T(8,128)S(1)}, u32[]{:S(2)}, u32[]{:S(2)}) collective-permute-start(f32[2,128,256]{2,1,0:T(8,128)S(1)} %get-tuple-element.38), channel_id=1, source_target_pairs={{4,8},{12,0},{8,4},{0,12},{5,9},{13,1},{9,5},{1,13},{6,10},{14,2},... | collective-permute-start | bytes 786440 | tf_op jit(solution)/shard_map/ppermute | solution.py:53
  102.2 2.0 copy-start
  102.2 2.0 collective-permute-start.12
  104.2 0.8 copy-start.11
  122.1 1.4 collective-permute-start.13
  124.2 6.5 %copy-start.12 = (f32[2]{0:T(128)}, f32[2]{0:T(128)S(1)}, u32[]{:S(2)}) copy-start(f32[2]{0:T(128)S(1)} %add.121.refs_2_) | copy-start | bytes 28
  124.2 4.5 %collective-permute-start.16 = (f32[2]{0:T(128)S(1)}, f32[2]{0:T(128)S(1)}, u32[]{:S(2)}, u32[]{:S(2)}) collective-permute-start(f32[2]{0:T(128)S(1)} %add.121.refs_2_), channel_id=1, source_target_pairs={{0,12},{4,8},{8,4},{12,0},{1,13},{5,9},{9,5},{13,1},{2,14},{6,10},... | collective-permute-start | bytes 32 | tf_op jit(solution)/shard_map/ppermute | solution.py:320
  125.6 3.6 %collective-permute-start.15 = (f32[2]{0:T(128)S(1)}, f32[2]{0:T(128)S(1)}, u32[]{:S(2)}, u32[]{:S(2)}) collective-permute-start(f32[2]{0:T(128)S(1)} %add.121.refs_2_), channel_id=1, source_target_pairs={{0,8},{4,12},{8,0},{12,4},{1,9},{5,13},{9,1},{13,5},{2,10},{6,14},... | collective-permute-start | bytes 32 | tf_op jit(solution)/shard_map/ppermute | solution.py:320
  127.1 3.6 %collective-permute-start.14 = (f32[2]{0:T(128)S(1)}, f32[2]{0:T(128)S(1)}, u32[]{:S(2)}, u32[]{:S(2)}) collective-permute-start(f32[2]{0:T(128)S(1)} %add.121.refs_2_), channel_id=1, source_target_pairs={{0,4},{4,0},{8,12},{12,8},{1,5},{5,1},{9,13},{13,9},{2,6},{6,2},{1... | collective-permute-start | bytes 32 | tf_op jit(solution)/shard_map/ppermute | solution.py:320
  128.7 2.0 %copy-start.13 = (f32[2]{0:T(128)}, f32[2]{0:T(128)S(1)}, u32[]{:S(2)}) copy-start(f32[2]{0:T(128)S(1)} %collective-permute-done.16.refs_5_) | copy-start | bytes 28
  129.2 1.5 copy-start.14
  130.7 0.5 copy-start.15
  151.1 2.2 %collective-permute-start.17 = (f32[2,128,512]{2,1,0:T(8,128)}, f32[2,128,512]{2,1,0:T(8,128)S(1)}, u32[]{:S(2)}, u32[]{:S(2)}) collective-permute-start(f32[2,128,512]{2,1,0:T(8,128)} %get-tuple-element.29), channel_id=1, source_target_pairs={{0,16},{16,0},{1,17},{17,1},{2,18},{18,2},{3,19},{19,3},{4,20},{20... | collective-permute-start | bytes 1572872 | tf_op jit(solution)/shard_map/ppermute | solution.py:53
  155.8 9.2 %collective-permute-start.18 = (f32[2,128,256]{2,1,0:T(8,128)S(1)}, f32[2,128,256]{2,1,0:T(8,128)S(1)}, u32[]{:S(2)}, u32[]{:S(2)}) collective-permute-start(f32[2,128,256]{2,1,0:T(8,128)S(1)} %get-tuple-element.33), channel_id=1, source_target_pairs={{0,4},{4,0},{8,12},{12,8},{1,5},{5,1},{9,13},{13,9},{2,6},{6,2},{1... | collective-permute-start | bytes 786440 | tf_op jit(solution)/shard_map/ppermute | solution.py:53
  156.4 13.4 %collective-permute-start.19 = (f32[2,128,256]{2,1,0:T(8,128)S(1)}, f32[2,128,256]{2,1,0:T(8,128)S(1)}, u32[]{:S(2)}, u32[]{:S(2)}) collective-permute-start(f32[2,128,256]{2,1,0:T(8,128)S(1)} %get-tuple-element.34), channel_id=1, source_target_pairs={{4,8},{12,0},{8,4},{0,12},{5,9},{13,1},{9,5},{1,13},{6,10},{14,2},... | collective-permute-start | bytes 786440 | tf_op jit(solution)/shard_map/ppermute | solution.py:53
  172.4 27.1 %copy-start.1 = (f32[2,128,512]{2,1,0:T(8,128)S(1)}, f32[2,128,512]{2,1,0:T(8,128)}, u32[]{:S(2)}) copy-start(f32[2,128,512]{2,1,0:T(8,128)} %copy-done) | copy-start | bytes 1572868
  172.4 27.1 %copy-start.3 = (f32[2,128,256]{2,1,0:T(8,128)S(1)}, f32[2,128,256]{2,1,0:T(8,128)}, u32[]{:S(2)}) copy-start(f32[2,128,256]{2,1,0:T(8,128)} %param.7) | copy-start | bytes 786436
  172.5 2.0 copy-start.2
  172.5 2.0 collective-permute-start.20
  174.5 0.8 copy-start.10
  189.3 1.4 collective-permute-start.21
  191.4 4.5 %collective-permute-start.24 = (f32[2]{0:T(128)S(1)}, f32[2]{0:T(128)S(1)}, u32[]{:S(2)}, u32[]{:S(2)}) collective-permute-start(f32[2]{0:T(128)S(1)} %add.129), channel_id=1, source_target_pairs={{0,12},{4,8},{8,4},{12,0},{1,13},{5,9},{9,5},{13,1},{2,14},{6,10},... | collective-permute-start | bytes 32 | tf_op jit(solution)/shard_map/ppermute | solution.py:320
  192.9 3.6 %collective-permute-start.23 = (f32[2]{0:T(128)S(1)}, f32[2]{0:T(128)S(1)}, u32[]{:S(2)}, u32[]{:S(2)}) collective-permute-start(f32[2]{0:T(128)S(1)} %add.129), channel_id=1, source_target_pairs={{0,8},{4,12},{8,0},{12,4},{1,9},{5,13},{9,1},{13,5},{2,10},{6,14},... | collective-permute-start | bytes 32 | tf_op jit(solution)/shard_map/ppermute | solution.py:320
  193.4 3.6 %collective-permute-start.22 = (f32[2]{0:T(128)S(1)}, f32[2]{0:T(128)S(1)}, u32[]{:S(2)}, u32[]{:S(2)}) collective-permute-start(f32[2]{0:T(128)S(1)} %add.129), channel_id=1, source_target_pairs={{0,4},{4,0},{8,12},{12,8},{1,5},{5,1},{9,13},{13,9},{2,6},{6,2},{1... | collective-permute-start | bytes 32 | tf_op jit(solution)/shard_map/ppermute | solution.py:320

commit v2 on v1

--- a/solution.py
+++ b/solution.py
@@ -12,6 +12,7 @@
 
 DAMPING = 1.0
 UNROLL = 2
+USED, PLACE_MA, SIDE, PLACE_Y, SIDE_Y = range(5)
 
 
 def dft_tables(width):
@@ -55,6 +56,18 @@
     ]
 
 
+def exchanges(count):
+    if count & (count - 1):
+        return [[(i, (i + k) % count) for i in range(count)] for k in range(1, count)]
+    return [[(i, i ^ k) for i in range(count)] for k in range(1, count)]
+
+
+def source_of(place, k, count):
+    if count & (count - 1):
+        return lax.rem(place - k + count, count)
+    return place ^ k
+
+
 def dot(left, right):
     return jnp.dot(left, right, preferred_element_type=jnp.float32)
 
@@ -62,14 +75,23 @@
 def call(body, name, out_shapes, in_spaces, operands, out_spaces=None, scratch=()):
     specs = [pl.BlockSpec(memory_space=space) for space in in_spaces]
     out_spaces = out_spaces or [pltpu.VMEM] * len(out_shapes)
+    operands = [
+        pltpu.with_memory_space_constraint(operand, pltpu.VMEM) if space == pltpu.VMEM else operand
+        for operand, space in zip(operands, in_spaces)
+    ]
     return pl.pallas_call(
         body,
         name=name,
-        out_shape=[jax.ShapeDtypeStruct(shape, jnp.float32) for shape in out_shapes],
+        out_shape=[
+            pltpu.VMEM(shape, jnp.float32)
+            if space == pltpu.VMEM
+            else jax.ShapeDtypeStruct(shape, jnp.float32)
+            for shape, space in zip(out_shapes, out_spaces)
+        ],
         in_specs=specs,
         out_specs=[pl.BlockSpec(memory_space=space) for space in out_spaces],
         scratch_shapes=list(scratch),
-        compiler_params=pltpu.CompilerParams(vmem_limit_bytes=60 * 2**20),
+        compiler_params=pltpu.CompilerParams(vmem_limit_bytes=16 * 2**20),
     )(*operands)
 
 
@@ -163,33 +185,34 @@
         rim, rows = self.rim, self.tile_rows
         middle_out[...] = canvas[:, rim : rim + rows]
         for k, out in enumerate(sends):
-            upper = parity[0] if k == 0 else 1 - parity[0]
+            upper = parity if k == 0 else 1 - parity
             start = pl.multiple_of((1 - upper) * (rim + rows), 8)
             out[...] = canvas[:, pl.ds(start, rim), :]
 
 
-def start_body(plan, swaps, shards, *refs):
+def start_body(plan, swaps, grid, *refs):
     refs = list(refs)
     info, centres, weights, middle = refs[:4]
     received = refs[4 : 4 + swaps]
-    shard, *rest = refs[4 + swaps : 4 + swaps + 2 * shards - 1]
-    direct, crossed = rest[: shards - 1], rest[shards - 1 :]
-    targets, one, two = refs[3 + swaps + 2 * shards : 6 + swaps + 2 * shards]
-    spectra, intensity, probes, middle_out, *tail = refs[6 + swaps + 2 * shards :]
+    shard, packed, crossed, targets, one, two = refs[4 + swaps : 10 + swaps]
+    spectra, intensity, probes, middle_out, *tail = refs[10 + swaps :]
     sends = tail[:swaps]
     region, windows, wave, half, image = tail[swaps:]
-    wide, lead = plan.patch, plan.modes // shards
+    wide = plan.patch
+    columns, shards = grid
+    lead = plan.modes // shards
     tables = (one, two)
-    place, side = info[2], info[3]
-    span = wide // 2
-
-    probes[pl.ds(place * lead, lead)] = shard[...]
+    span = wide // (2 * columns)
+
+    probes[pl.ds(info[PLACE_MA] * lead, lead)] = shard[...]
     for k in range(1, shards):
-        home = lax.rem(place - k + shards, shards) * lead
-        near = pl.multiple_of(side * span, 8)
-        far = pl.multiple_of((1 - side) * span, 8)
-        probes[pl.ds(home, lead), :, pl.ds(near, span), :] = direct[k - 1][...]
-        probes[pl.ds(home, lead), :, pl.ds(far, span), :] = crossed[k - 1][...]
+        home = source_of(info[PLACE_MA], k, shards) * lead
+        for c in range(columns):
+            column = source_of(info[PLACE_Y], c, columns) * span
+            near = pl.multiple_of(info[SIDE] * (wide // 2) + column, 8)
+            far = pl.multiple_of((1 - info[SIDE]) * (wide // 2) + column, 8)
+            probes[pl.ds(home, lead), :, pl.ds(near, span), :] = packed[k - 1, c]
+            probes[pl.ds(home, lead), :, pl.ds(far, span), :] = crossed[k - 1, c]
 
     plan.fill_region(region, middle, received, weights)
     plan.take_windows(windows, region, centres)
@@ -206,7 +229,7 @@
             intensity[slot] += power
 
         plan.each_modes(slot, forward)
-        live = jnp.where(slot < info[0], 1.0, 0.0)
+        live = jnp.where(slot < info[USED], 1.0, 0.0)
         windows[slot, 0] = live * (intensity[slot] - targets[slot])
         image[...] = jnp.zeros_like(image)
 
@@ -219,7 +242,7 @@
         plan.each_modes(slot, backward)
         for part in range(2):
             plan.place(region, slot, part, image[part], centres)
-    plan.send(region, [info[1]], middle_out, sends)
+    plan.send(region, info[SIDE], middle_out, sends)
 
 
 def change_body(plan, swaps, last, *refs):
@@ -260,7 +283,7 @@
                 power[slot] += square
 
         plan.each_modes(slot, forward)
-        live = jnp.where(slot < info[0], 1.0, 0.0)
+        live = jnp.where(slot < info[USED], 1.0, 0.0)
         bend = bend + live * jnp.sum(change[slot] * change[slot])
     sums[1] = bend
 
@@ -278,7 +301,7 @@
     step_out[0] = step
     region[...] = jnp.zeros_like(region)
     for slot in range(plan.slots):
-        live = jnp.where(slot < info[0], 1.0, 0.0)
+        live = jnp.where(slot < info[USED], 1.0, 0.0)
         bright = intensity[slot] + step * (change[slot] + step * power[slot])
         windows[slot, 0] = live * (bright - targets[slot])
         image[...] = jnp.zeros_like(image)
@@ -296,7 +319,7 @@
         plan.each_modes(slot, backward)
         for part in range(2):
             plan.place(region, slot, part, image[part], centres)
-    plan.send(region, [info[1]], middle_out, sends)
+    plan.send(region, info[SIDE], middle_out, sends)
 
 
 def step_of(totals):
@@ -306,6 +329,69 @@
     norm, bend = values[0][0], values[1][0]
     top = jnp.full((8, 128), norm, jnp.float32)
     return jnp.max(top / (bend + DAMPING * norm))
+
+
+def pack_body(plan, swaps, columns, *refs):
+    info, shard, tile, mine, *rims = refs
+    span = plan.patch // (2 * columns)
+    start = pl.multiple_of(info[SIDE] * (plan.patch // 2) + info[PLACE_Y] * span, 8)
+    mine[...] = shard[:, :, pl.ds(start, span), :]
+    low, high = tile[:, :, : plan.rim], tile[:, :, plan.tile_cols - plan.rim :]
+    for k, rim in enumerate(rims):
+        rim[...] = jnp.where((info[SIDE_Y] == 0) == (k == 0), high, low)
+
+
+def join_body(plan, swaps, columns, shards, *refs):
+    weights, tile = refs[:2]
+    received = refs[2 : 2 + swaps]
+    parts = refs[2 + swaps : -2]
+    middle, packed = refs[-2:]
+    low, high = sides_of(received, weights)
+    middle[:, :, : plan.rim] = low
+    middle[:, :, plan.rim : plan.rim + plan.tile_cols] = tile[...]
+    middle[:, :, plan.rim + plan.tile_cols :] = high
+    for k in range(shards - 1):
+        for c in range(columns):
+            packed[k, c] = parts[k * columns + c][...]
+
+
+def sides_of(received, weights):
+    count = len(received)
+    low = sum(received[k][...] * weights[k] for k in range(count))
+    high = sum(received[k][...] * weights[count + k] for k in range(count))
+    return low, high
+
+
+def fold_body(plan, swaps, *refs):
+    info, weights, middle = refs[:3]
+    received = refs[3 : 3 + swaps]
+    merged, *sends = refs[3 + swaps :]
+    low, high = sides_of(received, weights)
+    merged[...] = middle[...]
+    merged[:, : plan.rim] += low
+    merged[:, plan.tile_rows - plan.rim :] += high
+    for k, out in enumerate(sends):
+        left, right = merged[:, :, : plan.patch], merged[:, :, plan.tile_cols :]
+        out[...] = jnp.where((info[SIDE_Y] == 0) == (k == 0), right, left)
+
+
+def halo_body(plan, swaps, *refs):
+    weights, inside, merged = refs[:3]
+    received = refs[3 : 3 + swaps]
+    (middle,) = refs[3 + swaps :]
+    low, high = sides_of(received, weights)
+    middle[...] = -merged[...]
+    middle[:, :, : plan.patch] -= low
+    middle[:, :, plan.tile_cols :] -= high
+    middle[:, :, : plan.rim] *= inside[0]
+    middle[:, :, plan.rim + plan.tile_cols :] *= inside[1]
+
+
+def finish_body(plan, parts, *refs):
+    totals = refs[:parts]
+    first_step, tile, first, last, out = refs[parts:]
+    span = pl.ds(plan.rim, plan.tile_cols)
+    out[...] = tile[...] + first_step[0] * first[:, :, span] + step_of(totals) * last[:, :, span]
 
 
 def totals_of(sums):
@@ -316,16 +402,15 @@
     count = lax.axis_size("gy")
     if count & (count - 1):
         return [lax.psum(sums, "gy")]
-    return [sums] + [
-        lax.ppermute(sums, "gy", [(i, i ^ step) for i in range(count)]) for step in range(1, count)
-    ]
+    return [sums] + [lax.ppermute(sums, "gy", pairs) for pairs in exchanges(count)]
 
 
 def shards(object_field, probe_shard, measured, positions, slot_counts):
     patch = probe_shard.shape[-1]
     tile_rows, tile_cols = object_field.shape[1:]
-    groups = lax.axis_size("ma")
-    modes = probe_shard.shape[0] * groups
+    columns, groups = lax.axis_size("gy"), lax.axis_size("ma")
+    lead = probe_shard.shape[0]
+    modes = lead * groups
     slots = measured.shape[2]
     plan = Plan(tile_rows, tile_cols, patch, modes, slots)
     rim, units = plan.rim, slots * modes
@@ -333,86 +418,84 @@
     targets = measured[0, 0]
     centres = positions[0, 0]
     gx, gy, ma = (lax.axis_index(axis) for axis in ("gx", "gy", "ma"))
-    even_x, even_y = gx % 2 == 0, gy % 2 == 0
-    info = jnp.stack([slot_counts[0, 0], even_x.astype(jnp.int32) * 0 + gx % 2, ma, gx % 2])
+    info = jnp.stack([slot_counts[0, 0], ma, gx % 2, gy, gy % 2])
+    weights_x, weights_y = side_weights("gx"), side_weights("gy")
+    inside = jnp.stack([gy > 0, gy + 1 < columns]).astype(jnp.float32)
+    info, centres, weights_x, weights_y, inside = lax.optimization_barrier(
+        (info, centres, weights_x, weights_y, inside)
+    )
     swaps_x, swaps_y = (len(pair_swaps(lax.axis_size(axis))) for axis in ("gx", "gy"))
-    weights_x = side_weights("gx")
     smem, vmem = pltpu.SMEM, pltpu.VMEM
     tall = (2, tile_rows, plan.cols)
     fold = (2, rim, plan.cols)
     image_scratch = pltpu.VMEM((2, patch, patch), jnp.float32)
-
-    def halves(block, dim, low_start, high_start, width, is_even, swaps):
-        def piece(start):
-            return lax.dynamic_slice_in_dim(block, start, width, dim)
-
-        first = piece(jnp.where(is_even, high_start, low_start))
-        return [first] + [piece(jnp.where(is_even, low_start, high_start))] * (swaps - 1)
+    span = patch // (2 * columns)
 
     def rows_around(middle):
         if rim == tile_rows:
             return swap("gx", [middle] * swaps_x)
-        return swap("gx", halves(middle, 1, 0, tile_rows - rim, rim, even_x, swaps_x))
-
-    def sides(axis, received):
-        weights = side_weights(axis)
-        count = len(received)
-        low = sum(received[k] * weights[k] for k in range(count))
-        high = sum(received[k] * weights[count + k] for k in range(count))
-        return low, high
+        even = gx % 2 == 0
+        ends = [middle[:, :rim], middle[:, tile_rows - rim :]]
+        blocks = [jnp.where(even, ends[1], ends[0]), jnp.where(even, ends[0], ends[1])]
+        return swap("gx", blocks[:swaps_x])
 
     def descent(middle, sends):
-        low, high = sides("gx", swap("gx", sends))
-        gap = tile_rows - rim
-        middle = middle + jnp.pad(low, ((0, 0), (0, gap), (0, 0)))
-        middle = middle + jnp.pad(high, ((0, 0), (gap, 0), (0, 0)))
-        blocks = halves(middle, 2, 0, tile_cols, patch, even_y, swaps_y)
-        low, high = sides("gy", swap("gy", blocks))
-        column = jnp.arange(plan.cols)
-        first = jnp.where(gy == 0, rim, 0)
-        final = jnp.where(gy == lax.axis_size("gy") - 1, rim + tile_cols, plan.cols)
-        middle = middle + jnp.pad(low, ((0, 0), (0, 0), (0, tile_cols)))
-        middle = middle + jnp.pad(high, ((0, 0), (0, 0), (tile_cols, 0)))
-        return jnp.where((column >= first) & (column < final), -middle, 0.0)
-
-    def own(middle):
-        return middle[:, :, rim : rim + tile_cols]
-
-    span = patch // 2
-    mine = lax.dynamic_slice_in_dim(probe_shard, (gx % 2) * span, span, 2)
-    direct = [
-        lax.ppermute(mine, "ma", [(i, (i + k) % groups) for i in range(groups)])
-        for k in range(1, groups)
-    ]
-    crossed = [swap("gx", [block])[0] for block in direct]
-
-    blocks = halves(object_field, 2, 0, tile_cols - rim, rim, even_y, swaps_y)
-    low, high = sides("gy", swap("gy", blocks))
-    middle = jnp.concatenate([low, object_field, high], 2)
+        merged, *blocks = call(
+            functools.partial(fold_body, plan, swaps_x),
+            "fold",
+            [tall] + [(2, tile_rows, patch)] * swaps_y,
+            [smem] * 2 + [vmem] * (1 + swaps_x),
+            [info, weights_x, middle, *swap("gx", sends)],
+        )
+        (middle,) = call(
+            functools.partial(halo_body, plan, swaps_y),
+            "halo",
+            [tall],
+            [smem] * 2 + [vmem] * (1 + swaps_y),
+            [weights_y, inside, merged, *swap("gy", blocks)],
+        )
+        return middle
+
+    mine, *rims = call(
+        functools.partial(pack_body, plan, swaps_y, columns),
+        "pack",
+        [(lead, 2, span, patch)] + [(2, tile_rows, rim)] * swaps_y,
+        [smem] + [vmem] * 2,
+        [info, probe_shard, object_field],
+    )
+    parts = []
+    for pairs in exchanges(groups):
+        block = lax.ppermute(mine, "ma", pairs)
+        parts += [block] + [lax.ppermute(block, "gy", others) for others in exchanges(columns)]
+    middle, packed = call(
+        functools.partial(join_body, plan, swaps_y, columns, groups),
+        "join",
+        [tall, (groups - 1, columns, lead, 2, span, patch)],
+        [smem] + [vmem] * (1 + swaps_y + len(parts)),
+        [weights_y, object_field, *swap("gy", rims), *parts],
+    )
+    (crossed,) = swap("gx", [packed])[:1]
 
     spectra, intensity, probes, middle, *sends = call(
-        functools.partial(start_body, plan, swaps_x, groups),
+        functools.partial(start_body, plan, swaps_x, (columns, groups)),
         "start",
         [(units, patch, 2 * patch), (slots, patch, patch), (modes, 2, patch, patch), tall]
         + [fold] * swaps_x,
-        [smem] * 3 + [vmem] * (1 + swaps_x + 2 * groups - 1 + 3),
-        [info, centres, weights_x, middle, *rows_around(middle), probe_shard]
-        + direct
-        + crossed
+        [smem] * 3 + [vmem] * (7 + swaps_x),
+        [info, centres, weights_x, middle, *rows_around(middle), probe_shard, packed, crossed]
         + [targets, one, two],
         scratch=plan.scratch() + [image_scratch],
     )
-    middle = descent(middle, sends)
+    first_way = descent(middle, sends)
     sums, moved, change, power = call(
         functools.partial(change_body, plan, swaps_x, False),
         "change",
         [(2,), (units, patch, 2 * patch), (slots, patch, patch), (slots, patch, patch)],
         [smem] * 3 + [vmem] * (5 + swaps_x),
-        [info, centres, weights_x, middle, *rows_around(middle), spectra, probes, one, two],
+        [info, centres, weights_x, first_way, *rows_around(first_way), spectra, probes, one, two],
         [smem] + [vmem] * 3,
         scratch=plan.scratch(),
     )
-    first_way = own(middle)
     totals = totals_of(sums)
     spectra, first_step, middle, *sends = call(
         functools.partial(image_body, plan, swaps_x, len(totals)),
@@ -423,20 +506,26 @@
         [vmem, smem] + [vmem] * (1 + swaps_x),
         scratch=plan.scratch() + [image_scratch],
     )
-    middle = descent(middle, sends)
+    last_way = descent(middle, sends)
     (sums,) = call(
         functools.partial(change_body, plan, swaps_x, True),
         "last_change",
         [(2,)],
         [smem] * 3 + [vmem] * (5 + swaps_x),
-        [info, centres, weights_x, middle, *rows_around(middle), spectra, probes, one, two],
+        [info, centres, weights_x, last_way, *rows_around(last_way), spectra, probes, one, two],
         [smem],
         scratch=plan.scratch()
         + [pltpu.VMEM((slots, patch, patch), jnp.float32), pltpu.VMEM((1, 8, 128), jnp.float32)],
     )
-    totals = sum(totals_of(sums))
-    last_step = totals[0] / (totals[1] + DAMPING * totals[0])
-    return object_field + first_step[0] * first_way + last_step * own(middle)
+    totals = totals_of(sums)
+    (current,) = call(
+        functools.partial(finish_body, plan, len(totals)),
+        "finish",
+        [(2, tile_rows, tile_cols)],
+        [smem] * (len(totals) + 1) + [vmem] * 3,
+        [*totals, first_step, object_field, first_way, last_way],
+    )
+    return current
 
 
 def solution(mesh):

time: 202 us -> 152 us (0.75)
  waiting for transfers between devices: 73.2 us -> 51.9 us
  Pallas kernels: 75.4 us -> 54.2 us
  other arithmetic: 18.9 us -> 0.16 us
  starting transfers between devices: 23 us -> 35.3 us
    ppermute x9 -> x18, waiting for transfers between devices: 35.7 us -> 12.5 us  [the longest x9 7.09 us: shards(): lax.ppermute(block, 'gy', others)]
    pallas_call x4 -> x11, Pallas kernels: 75.4 us -> 54.2 us  [call(): pl.pallas_call(body, name=name, out_shape=[pltpu.VMEM(shape, jnp.float32)...]
    add x7 -> x0, other arithmetic: 15.1 us -> none  [the longest x3 7.77 us: sides(): low = sum((received[k] * weights[k] for k in range(count)))]
    ppermute x9 -> x18, starting transfers between devices: 13.1 us -> 26.1 us  [the longest x9 13.2 us: shards(): lax.ppermute(block, 'gy', others)]
    unnamed x32 -> x23, local copies, waits for them, and re-layouts: 2.86 us -> 8.87 us
    dynamic_slice x4 -> x0, local copies, waits for them, and re-layouts: 2.94 us -> none  [the longest x1 1.87 us: shards(): mine = lax.dynamic_slice_in_dim(probe_shard, gx % 2 * span, span, 2)]
    slice x3 -> x0, local copies, waits for them, and re-layouts: 2.64 us -> none  [the longest x2 2.06 us: sides(): low = sum((received[k] * weights[k] for k in range(count)))]
    ppermute x16 -> x14, waiting for transfers between devices: 37.5 us -> 39.4 us  [swap(): lax.ppermute(block, axis, pairs)]
  transfers between devices with their start and end apart: 25 -> 32, of which waited for: 20 -> 22; matrix products, arithmetic and copies ran while one was open for 4% -> 0% of each run, Pallas kernels for 0% -> 0%
where the time goes in v2:
time: 152 us; the launch traced here: 151 us
  Pallas kernels  54.2 us (36%)
  waiting for transfers between devices  51.9 us (34%)
  starting transfers between devices  35.3 us (23%)
  local copies, waits for them, and re-layouts  8.96 us (6%)
    pallas_call x11, Pallas kernels, call(): pl.pallas_call(body, name=name, out_shape=[pltpu.VMEM(shape, jnp.float32)...  54.2 us
    ppermute x14, waiting for transfers between devices, swap(): lax.ppermute(block, axis, pairs)  39.4 us
    ppermute x9, starting transfers between devices, shards(): lax.ppermute(block, 'gy', others)  13.2 us
    ppermute x14, starting transfers between devices, swap(): lax.ppermute(block, axis, pairs)  9.17 us
    unnamed x23, local copies, waits for them, and re-layouts  8.87 us
    ppermute x9, waiting for transfers between devices, shards(): lax.ppermute(block, 'gy', others)  7.09 us
    ppermute x6, starting transfers between devices, totals_of(): lax.ppermute(sums, 'gy', pairs)  6.98 us
    ppermute x3, starting transfers between devices, shards(): block = lax.ppermute(mine, 'ma', pairs)  5.93 us
  transfers between devices with their start and end apart: 32, of which 22 were waited for; matrix products, arithmetic and copies ran while one was open for 0% of the time, Pallas kernels for 0%

profile of v2, /device:TPU:0, one launch (start us, length us, event | category | flops | bytes accessed | tf_op | source)
XLA Modules:
  0.0 151.4 jit_solution(761990143859483307)
XLA Ops:
  1.0 1.2 copy-done.3
  2.2 0.9 copy-done.5
  3.7 5.1 %collective-permute-start.10 = (f32[2,2,32,256]{3,2,1,0:T(8,128)S(1)}, f32[2,2,32,256]{3,2,1,0:T(8,128)S(1)}, u32[]{:S(2)}, u32[]{:S(2)}) collective-permute-start(f32[2,2,32,256]{3,2,1,0:T(8,128)S(1)} %get-tuple-element.41), channel_id=1, source_target_pairs={{0,3},{1,2},{2,1},{3,0},{4,7},{5,6},{6,5},{7,4},{8,11},{9,10},{10,... | collective-permute-start | bytes 393224 | tf_op jit(solution)/shard_map/ppermute | solution.py:468
  8.9 1.5 collective-permute-start
  10.4 1.5 collective-permute-start.1
  12.6 2.6 %collective-permute-start.13 = (f32[2,2,32,256]{3,2,1,0:T(8,128)S(1)}, f32[2,2,32,256]{3,2,1,0:T(8,128)S(1)}, u32[]{:S(2)}, u32[]{:S(2)}) collective-permute-start(f32[2,2,32,256]{3,2,1,0:T(8,128)S(1)} %collective-permute-done.10.refs_12_), channel_id=1, source_target_pairs={{0,12},{4,8},{8,4},{12,0},{1,13},{5,9},{9,5},{13,1},{2,14},{6,10},... | collective-permute-start | bytes 393224 | tf_op jit(solution)/shard_map/ppermute | solution.py:469
  15.2 1.5 %collective-permute-start.12 = (f32[2,2,32,256]{3,2,1,0:T(8,128)S(1)}, f32[2,2,32,256]{3,2,1,0:T(8,128)S(1)}, u32[]{:S(2)}, u32[]{:S(2)}) collective-permute-start(f32[2,2,32,256]{3,2,1,0:T(8,128)S(1)} %collective-permute-done.10.refs_12_), channel_id=1, source_target_pairs={{0,8},{4,12},{8,0},{12,4},{1,9},{5,13},{9,1},{13,5},{2,10},{6,14},... | collective-permute-start | bytes 393224 | tf_op jit(solution)/shard_map/ppermute | solution.py:469
  16.7 2.3 %collective-permute-done.1.refs_3_ = f32[2,128,128]{2,1,0:T(8,128)S(1)} collective-permute-done((f32[2,128,128]{2,1,0:T(8,128)S(1)}, f32[2,128,128]{2,1,0:T(8,128)S(1)}, u32[]{:S(2)}, u32[]{:S(2)}) %collective-permute-start.1) | collective-permute-done | bytes 131104 | tf_op jit(solution)/shard_map/ppermute | solution.py:54
  19.1 1.5 collective-permute-start.11
  20.6 1.8 %collective-permute-start.9 = (f32[2,2,32,256]{3,2,1,0:T(8,128)S(1)}, f32[2,2,32,256]{3,2,1,0:T(8,128)S(1)}, u32[]{:S(2)}, u32[]{:S(2)}) collective-permute-start(f32[2,2,32,256]{3,2,1,0:T(8,128)S(1)} %collective-permute-done.6.refs_8_), channel_id=1, source_target_pairs={{0,12},{4,8},{8,4},{12,0},{1,13},{5,9},{9,5},{13,1},{2,14},{6,10},... | collective-permute-start | bytes 393224 | tf_op jit(solution)/shard_map/ppermute | solution.py:469
  22.9 1.2 collective-permute-start.7
  24.1 1.8 %collective-permute-start.5 = (f32[2,2,32,256]{3,2,1,0:T(8,128)S(1)}, f32[2,2,32,256]{3,2,1,0:T(8,128)S(1)}, u32[]{:S(2)}, u32[]{:S(2)}) collective-permute-start(f32[2,2,32,256]{3,2,1,0:T(8,128)S(1)} %collective-permute-done.2.refs_4_), channel_id=1, source_target_pairs={{0,12},{4,8},{8,4},{12,0},{1,13},{5,9},{9,5},{13,1},{2,14},{6,10},... | collective-permute-start | bytes 393224 | tf_op jit(solution)/shard_map/ppermute | solution.py:469
  26.4 1.5 collective-permute-done.9.refs_11_
  27.9 1.8 %collective-permute-start.3 = (f32[2,2,32,256]{3,2,1,0:T(8,128)S(1)}, f32[2,2,32,256]{3,2,1,0:T(8,128)S(1)}, u32[]{:S(2)}, u32[]{:S(2)}) collective-permute-start(f32[2,2,32,256]{3,2,1,0:T(8,128)S(1)} %collective-permute-done.2.refs_4_), channel_id=1, source_target_pairs={{0,4},{4,0},{8,12},{12,8},{1,5},{5,1},{9,13},{13,9},{2,6},{6,2},{1... | collective-permute-start | bytes 393224 | tf_op jit(solution)/shard_map/ppermute | solution.py:469
  29.7 1.9 %collective-permute-done.8.refs_10_ = f32[2,2,32,256]{3,2,1,0:T(8,128)S(1)} collective-permute-done((f32[2,2,32,256]{3,2,1,0:T(8,128)S(1)}, f32[2,2,32,256]{3,2,1,0:T(8,128)S(1)}, u32[]{:S(2)}, u32[]{:S(2)}) %collective-permute-start.8) | collective-permute-done | bytes 131104 | tf_op jit(solution)/shard_map/ppermute | solution.py:469
  31.6 1.9 %collective-permute-done.5.refs_7_ = f32[2,2,32,256]{3,2,1,0:T(8,128)S(1)} collective-permute-done((f32[2,2,32,256]{3,2,1,0:T(8,128)S(1)}, f32[2,2,32,256]{3,2,1,0:T(8,128)S(1)}, u32[]{:S(2)}, u32[]{:S(2)}) %collective-permute-start.5) | collective-permute-done | bytes 131104 | tf_op jit(solution)/shard_map/ppermute | solution.py:469
  33.5 1.0 collective-permute-done.4.refs_6_
  34.5 0.8 collective-permute-done.3.refs_5_
  35.3 0.9 copy-done.6
  37.5 3.6 %collective-permute-done.14.refs_4_ = f32[2,128,512]{2,1,0:T(8,128)S(1)} collective-permute-done((f32[2,128,512]{2,1,0:T(8,128)S(1)}, f32[2,128,512]{2,1,0:T(8,128)S(1)}, u32[]{:S(2)}, u32[]{:S(2)}) %collective-permute-start.14) | collective-permute-done | bytes 524320 | tf_op jit(solution)/shard_map/ppermute | solution.py:54
  41.2 1.0 copy-done
  42.2 1.0 copy-done.2
  43.2 1.2 copy-done.4
  44.5 1.0 copy-done.8
  46.2 18.1 %start.1 = (f32[16,256,512]{2,1,0:T(8,128)S(1)}, f32[2,256,256]{2,1,0:T(8,128)S(1)}, f32[8,2,256,256]{3,2,1,0:T(8,128)S(1)}, f32[2,128,512]{2,1,0:T(8,128)S(1)}, f32[2,128,512]{2,1,0:T(8,128)S(1)}) custom-call(s32[5]{0:T(128)S(1)} %stack.52.refs_0_, s32[2,2]{1,0:T(2,128)S(1)} %bitcast.18, f32[2]{0:T(128)S(1)} %get-tuple-element.36.refs_2_.refs_1_, ...), custom_call_target="tpu_custom_call" | custom-call | tf_op jit(solution)/shard_map/start/pallas_call | solution.py:82
  64.5 1.8 %collective-permute-done.16.refs_3_ = f32[2,128,512]{2,1,0:T(8,128)S(1)} collective-permute-done((f32[2,128,512]{2,1,0:T(8,128)S(1)}, f32[2,128,512]{2,1,0:T(8,128)S(1)}, u32[]{:S(2)}, u32[]{:S(2)}) %collective-permute-start.16) | collective-permute-done | bytes 524320 | tf_op jit(solution)/shard_map/ppermute | solution.py:54
  67.0 1.5 %collective-permute-start.17 = (f32[2,128,256]{2,1,0:T(8,128)S(1)}, f32[2,128,256]{2,1,0:T(8,128)S(1)}, u32[]{:S(2)}, u32[]{:S(2)}) collective-permute-start(f32[2,128,256]{2,1,0:T(8,128)S(1)} %get-tuple-element.47), channel_id=1, source_target_pairs={{0,4},{4,0},{8,12},{12,8},{1,5},{5,1},{9,13},{13,9},{2,6},{6,2},{1... | collective-permute-start | bytes 786440 | tf_op jit(solution)/shard_map/ppermute | solution.py:54
  68.8 7.5 %collective-permute-done.17.refs_3_ = f32[2,128,256]{2,1,0:T(8,128)S(1)} collective-permute-done((f32[2,128,256]{2,1,0:T(8,128)S(1)}, f32[2,128,256]{2,1,0:T(8,128)S(1)}, u32[]{:S(2)}, u32[]{:S(2)}) %collective-permute-start.17) | collective-permute-done | bytes 262176 | tf_op jit(solution)/shard_map/ppermute | solution.py:54
  76.3 4.5 %collective-permute-done.18.refs_4_ = f32[2,128,256]{2,1,0:T(8,128)S(1)} collective-permute-done((f32[2,128,256]{2,1,0:T(8,128)S(1)}, f32[2,128,256]{2,1,0:T(8,128)S(1)}, u32[]{:S(2)}, u32[]{:S(2)}) %collective-permute-start.18) | collective-permute-done | bytes 262176 | tf_op jit(solution)/shard_map/ppermute | solution.py:54
  81.6 1.9 %collective-permute-done.19.refs_4_ = f32[2,128,512]{2,1,0:T(8,128)S(1)} collective-permute-done((f32[2,128,512]{2,1,0:T(8,128)S(1)}, f32[2,128,512]{2,1,0:T(8,128)S(1)}, u32[]{:S(2)}, u32[]{:S(2)}) %collective-permute-start.19) | collective-permute-done | bytes 524320 | tf_op jit(solution)/shard_map/ppermute | solution.py:54
  83.5 10.2 %change.1 = (f32[2]{0:T(128)S(1)}, f32[16,256,512]{2,1,0:T(8,128)S(1)}, f32[2,256,256]{2,1,0:T(8,128)S(1)}, f32[2,256,256]{2,1,0:T(8,128)S(1)}) custom-call(s32[5]{0:T(128)S(1)} %stack.52.refs_0_, s32[2,2]{1,0:T(2,128)S(1)} %bitcast.19, f32[2]{0:T(128)S(1)} %get-tuple-element.36.refs_2_.refs_1_, f32[2,128,512]{2,1,0:T(8,128)S(1)} %halo.2.refs_3_.refs_6_, ...), custom_call_target="tpu_custom_call" | custom-call | tf_op jit(solution)/shard_map/change/pallas_call | solution.py:82
  93.9 1.0 collective-permute-done.20
  95.0 2.7 %collective-permute-start.23 = (f32[2]{0:T(128)S(1)}, f32[2]{0:T(128)S(1)}, u32[]{:S(2)}, u32[]{:S(2)}) collective-permute-start(f32[2]{0:T(128)S(1)} %add.26.refs_2_), channel_id=1, source_target_pairs={{0,12},{4,8},{8,4},{12,0},{1,13},{5,9},{9,5},{13,1},{2,14},{6,10},... | collective-permute-start | bytes 32 | tf_op jit(solution)/shard_map/ppermute | solution.py:405
  98.5 1.0 collective-permute-done.23.refs_5_
  99.4 1.8 %collective-permute-done.22.refs_4_ = f32[2]{0:T(128)S(1)} collective-permute-done((f32[2]{0:T(128)S(1)}, f32[2]{0:T(128)S(1)}, u32[]{:S(2)}, u32[]{:S(2)}) %collective-permute-start.22) | collective-permute-done | bytes 40 | tf_op jit(solution)/shard_map/ppermute | solution.py:405
  101.8 10.5 %image.1 = (f32[16,256,512]{2,1,0:T(8,128)S(1)}, f32[1]{0:T(128)}, f32[2,128,512]{2,1,0:T(8,128)S(1)}, f32[2,128,512]{2,1,0:T(8,128)S(1)}) custom-call(s32[5]{0:T(128)S(1)} %stack.52.refs_0_, s32[2,2]{1,0:T(2,128)S(1)} %bitcast.20, f32[2]{0:T(128)S(1)} %add.26.refs_2_, f32[2]{0:T(128)S(1)} %collective-permute-done.21.refs_3_, ...), custom_call_target="tpu_custom_call" | custom-call | tf_op jit(solution)/shard_map/image/pallas_call | solution.py:82
  112.4 1.9 %collective-permute-done.24.refs_3_ = f32[2,128,512]{2,1,0:T(8,128)S(1)} collective-permute-done((f32[2,128,512]{2,1,0:T(8,128)S(1)}, f32[2,128,512]{2,1,0:T(8,128)S(1)}, u32[]{:S(2)}, u32[]{:S(2)}) %collective-permute-start.24) | collective-permute-done | bytes 524320 | tf_op jit(solution)/shard_map/ppermute | solution.py:54
  115.4 2.7 %collective-permute-start.26 = (f32[2,128,256]{2,1,0:T(8,128)S(1)}, f32[2,128,256]{2,1,0:T(8,128)S(1)}, u32[]{:S(2)}, u32[]{:S(2)}) collective-permute-start(f32[2,128,256]{2,1,0:T(8,128)S(1)} %get-tuple-element.60), channel_id=1, source_target_pairs={{4,8},{12,0},{8,4},{0,12},{5,9},{13,1},{9,5},{1,13},{6,10},{14,2},... | collective-permute-start | bytes 786440 | tf_op jit(solution)/shard_map/ppermute | solution.py:54
  118.1 6.2 %collective-permute-done.25.refs_3_ = f32[2,128,256]{2,1,0:T(8,128)S(1)} collective-permute-done((f32[2,128,256]{2,1,0:T(8,128)S(1)}, f32[2,128,256]{2,1,0:T(8,128)S(1)}, u32[]{:S(2)}, u32[]{:S(2)}) %collective-permute-start.25) | collective-permute-done | bytes 262176 | tf_op jit(solution)/shard_map/ppermute | solution.py:54
  124.3 5.8 %collective-permute-done.26.refs_4_ = f32[2,128,256]{2,1,0:T(8,128)S(1)} collective-permute-done((f32[2,128,256]{2,1,0:T(8,128)S(1)}, f32[2,128,256]{2,1,0:T(8,128)S(1)}, u32[]{:S(2)}, u32[]{:S(2)}) %collective-permute-start.26) | collective-permute-done | bytes 262176 | tf_op jit(solution)/shard_map/ppermute | solution.py:54
  130.9 1.9 %collective-permute-done.27.refs_4_ = f32[2,128,512]{2,1,0:T(8,128)S(1)} collective-permute-done((f32[2,128,512]{2,1,0:T(8,128)S(1)}, f32[2,128,512]{2,1,0:T(8,128)S(1)}, u32[]{:S(2)}, u32[]{:S(2)}) %collective-permute-start.27) | collective-permute-done | bytes 524320 | tf_op jit(solution)/shard_map/ppermute | solution.py:54
  132.8 9.8 %last_change.1 = f32[2]{0:T(128)S(1)} custom-call(s32[5]{0:T(128)S(1)} %stack.52.refs_0_, s32[2,2]{1,0:T(2,128)S(1)} %bitcast.21, f32[2]{0:T(128)S(1)} %get-tuple-element.36.refs_2_.refs_1_, f32[2,128,512]{2,1,0:T(8,128)S(1)} %halo.3.refs_3_.refs_7_, f32[2,128,512]{2,1,0:T(8,128)S(1)} %collective-permute-done.27.refs_4_, ...), custom_call_target="tpu_custom_call" | custom-call | tf_op jit(solution)/shard_map/last_change/pallas_call | solution.py:82
  142.8 1.0 collective-permute-done.28
  144.0 1.8 %collective-permute-start.30 = (f32[2]{0:T(128)S(1)}, f32[2]{0:T(128)S(1)}, u32[]{:S(2)}, u32[]{:S(2)}) collective-permute-start(f32[2]{0:T(128)S(1)} %add.27.refs_0_), channel_id=1, source_target_pairs={{0,8},{4,12},{8,0},{12,4},{1,9},{5,13},{9,1},{13,5},{2,10},{6,14},... | collective-permute-start | bytes 32 | tf_op jit(solution)/shard_map/ppermute | solution.py:405
  145.8 1.5 collective-permute-start.29
  147.3 1.0 collective-permute-done.31.refs_3_
  148.3 1.1 collective-permute-done.29.refs_1_
  149.4 1.3 finish.1
  (55 shorter events, 11.3 us)
Async XLA Ops:
  0.0 83.5 %copy-start.1 = (bf16[512,512]{1,0:T(8,128)(2,1)S(1)}, bf16[512,512]{1,0:T(8,128)(2,1)}, u32[]{:S(2)}) copy-start(bf16[512,512]{1,0:T(8,128)(2,1)} %constant.43.clone.refs_10_.refs_8_.refs_14_) | copy-start | bytes 1572868
  1.0 1.2 copy-start.3
  2.2 0.9 copy-start.5
  3.1 80.4 %copy-start.10 = (s32[1,1,2,2]{3,2,1,0:T(2,128)S(1)}, s32[1,1,2,2]{3,2,1,0:T(2,128)}, u32[]{:S(2)}) copy-start(s32[1,1,2,2]{3,2,1,0:T(2,128)} %param.10) | copy-start | bytes 52
  3.7 8.9 %collective-permute-start.10 = (f32[2,2,32,256]{3,2,1,0:T(8,128)S(1)}, f32[2,2,32,256]{3,2,1,0:T(8,128)S(1)}, u32[]{:S(2)}, u32[]{:S(2)}) collective-permute-start(f32[2,2,32,256]{3,2,1,0:T(8,128)S(1)} %get-tuple-element.41), channel_id=1, source_target_pairs={{0,3},{1,2},{2,1},{3,0},{4,7},{5,6},{6,5},{7,4},{8,11},{9,10},{10,... | collective-permute-start | bytes 393224 | tf_op jit(solution)/shard_map/ppermute | solution.py:468
  8.9 6.3 %collective-permute-start = (f32[2,128,128]{2,1,0:T(8,128)S(1)}, f32[2,128,128]{2,1,0:T(8,128)S(1)}, u32[]{:S(2)}, u32[]{:S(2)}) collective-permute-start(f32[2,128,128]{2,1,0:T(8,128)S(1)} %get-tuple-element.39), channel_id=1, source_target_pairs={{0,4},{4,0},{8,12},{12,8},{1,5},{5,1},{9,13},{13,9},{2,6},{6,2},{1... | collective-permute-start | bytes 393224 | tf_op jit(solution)/shard_map/ppermute | solution.py:54
  10.4 8.7 %collective-permute-start.1 = (f32[2,128,128]{2,1,0:T(8,128)S(1)}, f32[2,128,128]{2,1,0:T(8,128)S(1)}, u32[]{:S(2)}, u32[]{:S(2)}) collective-permute-start(f32[2,128,128]{2,1,0:T(8,128)S(1)} %get-tuple-element.40), channel_id=1, source_target_pairs={{4,8},{12,0},{8,4},{0,12},{5,9},{13,1},{9,5},{1,13},{6,10},{14,2},... | collective-permute-start | bytes 393224 | tf_op jit(solution)/shard_map/ppermute | solution.py:54
  11.8 8.7 %collective-permute-start.6 = (f32[2,2,32,256]{3,2,1,0:T(8,128)S(1)}, f32[2,2,32,256]{3,2,1,0:T(8,128)S(1)}, u32[]{:S(2)}, u32[]{:S(2)}) collective-permute-start(f32[2,2,32,256]{3,2,1,0:T(8,128)S(1)} %get-tuple-element.41), channel_id=1, source_target_pairs={{0,2},{1,3},{2,0},{3,1},{4,6},{5,7},{6,4},{7,5},{8,10},{9,11},{10,... | collective-permute-start | bytes 393224 | tf_op jit(solution)/shard_map/ppermute | solution.py:468
  11.8 10.5 %collective-permute-start.2 = (f32[2,2,32,256]{3,2,1,0:T(8,128)S(1)}, f32[2,2,32,256]{3,2,1,0:T(8,128)S(1)}, u32[]{:S(2)}, u32[]{:S(2)}) collective-permute-start(f32[2,2,32,256]{3,2,1,0:T(8,128)S(1)} %get-tuple-element.41), channel_id=1, source_target_pairs={{0,1},{1,0},{2,3},{3,2},{4,5},{5,4},{6,7},{7,6},{8,9},{9,8},{10,11... | collective-permute-start | bytes 393224 | tf_op jit(solution)/shard_map/ppermute | solution.py:468
  12.6 10.3 %collective-permute-start.13 = (f32[2,2,32,256]{3,2,1,0:T(8,128)S(1)}, f32[2,2,32,256]{3,2,1,0:T(8,128)S(1)}, u32[]{:S(2)}, u32[]{:S(2)}) collective-permute-start(f32[2,2,32,256]{3,2,1,0:T(8,128)S(1)} %collective-permute-done.10.refs_12_), channel_id=1, source_target_pairs={{0,12},{4,8},{8,4},{12,0},{1,13},{5,9},{9,5},{13,1},{2,14},{6,10},... | collective-permute-start | bytes 393224 | tf_op jit(solution)/shard_map/ppermute | solution.py:469
  15.2 8.9 %collective-permute-start.12 = (f32[2,2,32,256]{3,2,1,0:T(8,128)S(1)}, f32[2,2,32,256]{3,2,1,0:T(8,128)S(1)}, u32[]{:S(2)}, u32[]{:S(2)}) collective-permute-start(f32[2,2,32,256]{3,2,1,0:T(8,128)S(1)} %collective-permute-done.10.refs_12_), channel_id=1, source_target_pairs={{0,8},{4,12},{8,0},{12,4},{1,9},{5,13},{9,1},{13,5},{2,10},{6,14},... | collective-permute-start | bytes 393224 | tf_op jit(solution)/shard_map/ppermute | solution.py:469
  19.1 6.8 %collective-permute-start.11 = (f32[2,2,32,256]{3,2,1,0:T(8,128)S(1)}, f32[2,2,32,256]{3,2,1,0:T(8,128)S(1)}, u32[]{:S(2)}, u32[]{:S(2)}) collective-permute-start(f32[2,2,32,256]{3,2,1,0:T(8,128)S(1)} %collective-permute-done.10.refs_12_), channel_id=1, source_target_pairs={{0,4},{4,0},{8,12},{12,8},{1,5},{5,1},{9,13},{13,9},{2,6},{6,2},{1... | collective-permute-start | bytes 393224 | tf_op jit(solution)/shard_map/ppermute | solution.py:469
  20.6 7.3 %collective-permute-start.9 = (f32[2,2,32,256]{3,2,1,0:T(8,128)S(1)}, f32[2,2,32,256]{3,2,1,0:T(8,128)S(1)}, u32[]{:S(2)}, u32[]{:S(2)}) collective-permute-start(f32[2,2,32,256]{3,2,1,0:T(8,128)S(1)} %collective-permute-done.6.refs_8_), channel_id=1, source_target_pairs={{0,12},{4,8},{8,4},{12,0},{1,13},{5,9},{9,5},{13,1},{2,14},{6,10},... | collective-permute-start | bytes 393224 | tf_op jit(solution)/shard_map/ppermute | solution.py:469
  22.4 9.2 %collective-permute-start.8 = (f32[2,2,32,256]{3,2,1,0:T(8,128)S(1)}, f32[2,2,32,256]{3,2,1,0:T(8,128)S(1)}, u32[]{:S(2)}, u32[]{:S(2)}) collective-permute-start(f32[2,2,32,256]{3,2,1,0:T(8,128)S(1)} %collective-permute-done.6.refs_8_), channel_id=1, source_target_pairs={{0,8},{4,12},{8,0},{12,4},{1,9},{5,13},{9,1},{13,5},{2,10},{6,14},... | collective-permute-start | bytes 393224 | tf_op jit(solution)/shard_map/ppermute | solution.py:469
  22.9 8.7 %collective-permute-start.7 = (f32[2,2,32,256]{3,2,1,0:T(8,128)S(1)}, f32[2,2,32,256]{3,2,1,0:T(8,128)S(1)}, u32[]{:S(2)}, u32[]{:S(2)}) collective-permute-start(f32[2,2,32,256]{3,2,1,0:T(8,128)S(1)} %collective-permute-done.6.refs_8_), channel_id=1, source_target_pairs={{0,4},{4,0},{8,12},{12,8},{1,5},{5,1},{9,13},{13,9},{2,6},{6,2},{1... | collective-permute-start | bytes 393224 | tf_op jit(solution)/shard_map/ppermute | solution.py:469
  24.1 9.4 %collective-permute-start.5 = (f32[2,2,32,256]{3,2,1,0:T(8,128)S(1)}, f32[2,2,32,256]{3,2,1,0:T(8,128)S(1)}, u32[]{:S(2)}, u32[]{:S(2)}) collective-permute-start(f32[2,2,32,256]{3,2,1,0:T(8,128)S(1)} %collective-permute-done.2.refs_4_), channel_id=1, source_target_pairs={{0,12},{4,8},{8,4},{12,0},{1,13},{5,9},{9,5},{13,1},{2,14},{6,10},... | collective-permute-start | bytes 393224 | tf_op jit(solution)/shard_map/ppermute | solution.py:469
  25.9 8.6 %collective-permute-start.4 = (f32[2,2,32,256]{3,2,1,0:T(8,128)S(1)}, f32[2,2,32,256]{3,2,1,0:T(8,128)S(1)}, u32[]{:S(2)}, u32[]{:S(2)}) collective-permute-start(f32[2,2,32,256]{3,2,1,0:T(8,128)S(1)} %collective-permute-done.2.refs_4_), channel_id=1, source_target_pairs={{0,8},{4,12},{8,0},{12,4},{1,9},{5,13},{9,1},{13,5},{2,10},{6,14},... | collective-permute-start | bytes 393224 | tf_op jit(solution)/shard_map/ppermute | solution.py:469
  27.9 7.4 %collective-permute-start.3 = (f32[2,2,32,256]{3,2,1,0:T(8,128)S(1)}, f32[2,2,32,256]{3,2,1,0:T(8,128)S(1)}, u32[]{:S(2)}, u32[]{:S(2)}) collective-permute-start(f32[2,2,32,256]{3,2,1,0:T(8,128)S(1)} %collective-permute-done.2.refs_4_), channel_id=1, source_target_pairs={{0,4},{4,0},{8,12},{12,8},{1,5},{5,1},{9,13},{13,9},{2,6},{6,2},{1... | collective-permute-start | bytes 393224 | tf_op jit(solution)/shard_map/ppermute | solution.py:469
  35.3 1.0 copy-start.6
  36.9 4.2 %collective-permute-start.15 = (f32[3,4,2,2,32,256]{5,4,3,2,1,0:T(8,128)S(1)}, f32[3,4,2,2,32,256]{5,4,3,2,1,0:T(8,128)S(1)}, u32[]{:S(2)}, u32[]{:S(2)}) collective-permute-start(f32[3,4,2,2,32,256]{5,4,3,2,1,0:T(8,128)S(1)} %get-tuple-element.43.refs_6_), channel_id=1, source_target_pairs={{0,16},{16,0},{1,17},{17,1},{2,18},{18,2},{3,19},{19,3},{4,20},{20... | collective-permute-start | bytes 4718600 | tf_op jit(solution)/shard_map/ppermute | solution.py:54
  37.0 4.1 %collective-permute-start.14 = (f32[2,128,512]{2,1,0:T(8,128)S(1)}, f32[2,128,512]{2,1,0:T(8,128)S(1)}, u32[]{:S(2)}, u32[]{:S(2)}) collective-permute-start(f32[2,128,512]{2,1,0:T(8,128)S(1)} %get-tuple-element.42.refs_3_), channel_id=1, source_target_pairs={{0,16},{16,0},{1,17},{17,1},{2,18},{18,2},{3,19},{19,3},{4,20},{20... | collective-permute-start | bytes 1572872 | tf_op jit(solution)/shard_map/ppermute | solution.py:54
  41.2 1.0 copy-start
  42.2 1.0 copy-start.2
  43.2 1.2 copy-start.4
  44.5 1.0 copy-start.8
  45.5 0.7 copy-start.9
  64.3 2.0 %collective-permute-start.16 = (f32[2,128,512]{2,1,0:T(8,128)S(1)}, f32[2,128,512]{2,1,0:T(8,128)S(1)}, u32[]{:S(2)}, u32[]{:S(2)}) collective-permute-start(f32[2,128,512]{2,1,0:T(8,128)S(1)} %get-tuple-element.45), channel_id=1, source_target_pairs={{0,16},{16,0},{1,17},{17,1},{2,18},{18,2},{3,19},{19,3},{4,20},{20... | collective-permute-start | bytes 1572872 | tf_op jit(solution)/shard_map/ppermute | solution.py:54
  67.0 9.2 %collective-permute-start.17 = (f32[2,128,256]{2,1,0:T(8,128)S(1)}, f32[2,128,256]{2,1,0:T(8,128)S(1)}, u32[]{:S(2)}, u32[]{:S(2)}) collective-permute-start(f32[2,128,256]{2,1,0:T(8,128)S(1)} %get-tuple-element.47), channel_id=1, source_target_pairs={{0,4},{4,0},{8,12},{12,8},{1,5},{5,1},{9,13},{13,9},{2,6},{6,2},{1... | collective-permute-start | bytes 786440 | tf_op jit(solution)/shard_map/ppermute | solution.py:54
  68.6 12.2 %collective-permute-start.18 = (f32[2,128,256]{2,1,0:T(8,128)S(1)}, f32[2,128,256]{2,1,0:T(8,128)S(1)}, u32[]{:S(2)}, u32[]{:S(2)}) collective-permute-start(f32[2,128,256]{2,1,0:T(8,128)S(1)} %get-tuple-element.48), channel_id=1, source_target_pairs={{4,8},{12,0},{8,4},{0,12},{5,9},{13,1},{9,5},{1,13},{6,10},{14,2},... | collective-permute-start | bytes 786440 | tf_op jit(solution)/shard_map/ppermute | solution.py:54
  81.5 2.0 %collective-permute-start.19 = (f32[2,128,512]{2,1,0:T(8,128)S(1)}, f32[2,128,512]{2,1,0:T(8,128)S(1)}, u32[]{:S(2)}, u32[]{:S(2)}) collective-permute-start(f32[2,128,512]{2,1,0:T(8,128)S(1)} %halo.2.refs_3_.refs_6_), channel_id=1, source_target_pairs={{0,16},{16,0},{1,17},{17,1},{2,18},{18,2},{3,19},{19,3},{4,20},{20... | collective-permute-start | bytes 1572872 | tf_op jit(solution)/shard_map/ppermute | solution.py:54
  93.8 1.2 collective-permute-start.20
  95.0 4.5 %collective-permute-start.23 = (f32[2]{0:T(128)S(1)}, f32[2]{0:T(128)S(1)}, u32[]{:S(2)}, u32[]{:S(2)}) collective-permute-start(f32[2]{0:T(128)S(1)} %add.26.refs_2_), channel_id=1, source_target_pairs={{0,12},{4,8},{8,4},{12,0},{1,13},{5,9},{9,5},{13,1},{2,14},{6,10},... | collective-permute-start | bytes 32 | tf_op jit(solution)/shard_map/ppermute | solution.py:405
  97.7 3.6 %collective-permute-start.22 = (f32[2]{0:T(128)S(1)}, f32[2]{0:T(128)S(1)}, u32[]{:S(2)}, u32[]{:S(2)}) collective-permute-start(f32[2]{0:T(128)S(1)} %add.26.refs_2_), channel_id=1, source_target_pairs={{0,8},{4,12},{8,0},{12,4},{1,9},{5,13},{9,1},{13,5},{2,10},{6,14},... | collective-permute-start | bytes 32 | tf_op jit(solution)/shard_map/ppermute | solution.py:405
  98.2 3.6 %collective-permute-start.21 = (f32[2]{0:T(128)S(1)}, f32[2]{0:T(128)S(1)}, u32[]{:S(2)}, u32[]{:S(2)}) collective-permute-start(f32[2]{0:T(128)S(1)} %add.26.refs_2_), channel_id=1, source_target_pairs={{0,4},{4,0},{8,12},{12,8},{1,5},{5,1},{9,13},{13,9},{2,6},{6,2},{1... | collective-permute-start | bytes 32 | tf_op jit(solution)/shard_map/ppermute | solution.py:405
  112.3 2.0 %collective-permute-start.24 = (f32[2,128,512]{2,1,0:T(8,128)S(1)}, f32[2,128,512]{2,1,0:T(8,128)S(1)}, u32[]{:S(2)}, u32[]{:S(2)}) collective-permute-start(f32[2,128,512]{2,1,0:T(8,128)S(1)} %get-tuple-element.57), channel_id=1, source_target_pairs={{0,16},{16,0},{1,17},{17,1},{2,18},{18,2},{3,19},{19,3},{4,20},{20... | collective-permute-start | bytes 1572872 | tf_op jit(solution)/shard_map/ppermute | solution.py:54
  115.1 34.3 %copy-start.7 = (f32[2,128,256]{2,1,0:T(8,128)S(1)}, f32[2,128,256]{2,1,0:T(8,128)}, u32[]{:S(2)}) copy-start(f32[2,128,256]{2,1,0:T(8,128)} %refs_5_.3) | copy-start | bytes 786436
  115.1 9.2 %collective-permute-start.25 = (f32[2,128,256]{2,1,0:T(8,128)S(1)}, f32[2,128,256]{2,1,0:T(8,128)S(1)}, u32[]{:S(2)}, u32[]{:S(2)}) collective-permute-start(f32[2,128,256]{2,1,0:T(8,128)S(1)} %get-tuple-element.59), channel_id=1, source_target_pairs={{0,4},{4,0},{8,12},{12,8},{1,5},{5,1},{9,13},{13,9},{2,6},{6,2},{1... | collective-permute-start | bytes 786440 | tf_op jit(solution)/shard_map/ppermute | solution.py:54
  115.4 14.6 %collective-permute-start.26 = (f32[2,128,256]{2,1,0:T(8,128)S(1)}, f32[2,128,256]{2,1,0:T(8,128)S(1)}, u32[]{:S(2)}, u32[]{:S(2)}) collective-permute-start(f32[2,128,256]{2,1,0:T(8,128)S(1)} %get-tuple-element.60), channel_id=1, source_target_pairs={{4,8},{12,0},{8,4},{0,12},{5,9},{13,1},{9,5},{1,13},{6,10},{14,2},... | collective-permute-start | bytes 786440 | tf_op jit(solution)/shard_map/ppermute | solution.py:54
  130.8 2.0 %collective-permute-start.27 = (f32[2,128,512]{2,1,0:T(8,128)S(1)}, f32[2,128,512]{2,1,0:T(8,128)S(1)}, u32[]{:S(2)}, u32[]{:S(2)}) collective-permute-start(f32[2,128,512]{2,1,0:T(8,128)S(1)} %halo.3.refs_3_.refs_7_), channel_id=1, source_target_pairs={{0,16},{16,0},{1,17},{17,1},{2,18},{18,2},{3,19},{19,3},{4,20},{20... | collective-permute-start | bytes 1572872 | tf_op jit(solution)/shard_map/ppermute | solution.py:54
  142.6 1.2 collective-permute-start.28
  143.8 4.5 %collective-permute-start.31 = (f32[2]{0:T(128)S(1)}, f32[2]{0:T(128)S(1)}, u32[]{:S(2)}, u32[]{:S(2)}) collective-permute-start(f32[2]{0:T(128)S(1)} %add.27.refs_0_), channel_id=1, source_target_pairs={{0,12},{4,8},{8,4},{12,0},{1,13},{5,9},{9,5},{13,1},{2,14},{6,10},... | collective-permute-start | bytes 32 | tf_op jit(solution)/shard_map/ppermute | solution.py:405
  144.0 4.2 %collective-permute-start.30 = (f32[2]{0:T(128)S(1)}, f32[2]{0:T(128)S(1)}, u32[]{:S(2)}, u32[]{:S(2)}) collective-permute-start(f32[2]{0:T(128)S(1)} %add.27.refs_0_), channel_id=1, source_target_pairs={{0,8},{4,12},{8,0},{12,4},{1,9},{5,13},{9,1},{13,5},{2,10},{6,14},... | collective-permute-start | bytes 32 | tf_op jit(solution)/shard_map/ppermute | solution.py:405
  145.8 3.6 %collective-permute-start.29 = (f32[2]{0:T(128)S(1)}, f32[2]{0:T(128)S(1)}, u32[]{:S(2)}, u32[]{:S(2)}) collective-permute-start(f32[2]{0:T(128)S(1)} %add.27.refs_0_), channel_id=1, source_target_pairs={{0,4},{4,0},{8,12},{12,8},{1,5},{5,1},{9,13},{13,9},{2,6},{6,2},{1... | collective-permute-start | bytes 32 | tf_op jit(solution)/shard_map/ppermute | solution.py:405

commit v3 on v2

--- a/solution.py
+++ b/solution.py
@@ -17,12 +17,15 @@
 
 def dft_tables(width):
     ladder = np.arange(width, dtype=np.int64)
-    angles = (ladder[:, None] * ladder[None, :] % width) * (2.0 * math.pi / width)
+    angles = (ladder[:, None] * ladder[None, : width // 2] % width) * (2.0 * math.pi / width)
     real_part = np.cos(angles) / math.sqrt(width)
     imag_part = -np.sin(angles) / math.sqrt(width)
-    table_one = np.block([[real_part, -imag_part], [imag_part, real_part]])
-    table_two = np.block([[real_part, imag_part], [-imag_part, real_part]])
-    return table_one.astype(ml_dtypes.bfloat16), table_two.astype(ml_dtypes.bfloat16)
+    blocks = [
+        np.block([[real_part[p::2], -imag_part[p::2]], [imag_part[p::2], real_part[p::2]]])
+        for p in range(2)
+    ]
+    one = np.stack(blocks).astype(ml_dtypes.bfloat16)
+    return one, np.ascontiguousarray(one.transpose(0, 2, 1))
 
 
 def pair_swaps(count):
@@ -72,24 +75,24 @@
     return jnp.dot(left, right, preferred_element_type=jnp.float32)
 
 
-def call(body, name, out_shapes, in_spaces, operands, out_spaces=None, scratch=()):
+def call(body, name, out_shapes, in_spaces, operands, out_spaces=None, scratch=(), pinned=True, dtypes={}):
     specs = [pl.BlockSpec(memory_space=space) for space in in_spaces]
     out_spaces = out_spaces or [pltpu.VMEM] * len(out_shapes)
     operands = [
-        pltpu.with_memory_space_constraint(operand, pltpu.VMEM) if space == pltpu.VMEM else operand
+        pltpu.with_memory_space_constraint(operand, pltpu.VMEM) if pinned and space == pltpu.VMEM else operand
         for operand, space in zip(operands, in_spaces)
     ]
     return pl.pallas_call(
         body,
         name=name,
         out_shape=[
-            pltpu.VMEM(shape, jnp.float32)
+            space(shape, dtypes.get(k, jnp.float32))
             if space == pltpu.VMEM
             else jax.ShapeDtypeStruct(shape, jnp.float32)
-            for shape, space in zip(out_shapes, out_spaces)
+            for k, (shape, space) in enumerate(zip(out_shapes, out_spaces))
         ],
         in_specs=specs,
-        out_specs=[pl.BlockSpec(memory_space=space) for space in out_spaces],
+        out_specs=[pl.BlockSpec(memory_space=space or pltpu.VMEM) for space in out_spaces],
         scratch_shapes=list(scratch),
         compiler_params=pltpu.CompilerParams(vmem_limit_bytes=16 * 2**20),
     )(*operands)
@@ -108,8 +111,8 @@
         return [
             pltpu.VMEM((2, self.rows, self.cols), jnp.float32),
             pltpu.VMEM((self.slots, 2, wide, wide), jnp.float32),
-            pltpu.VMEM((UNROLL, 2 * wide, wide), jnp.bfloat16),
-            pltpu.VMEM((UNROLL, 2 * wide, wide), jnp.bfloat16),
+            pltpu.VMEM((UNROLL, 2, wide, wide), jnp.bfloat16),
+            pltpu.VMEM((UNROLL, 2, wide, wide), jnp.bfloat16),
         ]
 
     def fill_region(self, region, middle, received, weights):
@@ -150,36 +153,69 @@
         lax.fori_loop(0, self.modes // UNROLL, step, 0)
 
     def spectra(self, slot, modes, probes, windows, wave, half, tables):
+        mid = self.rim
+        low, high = slice(0, mid), slice(mid, 2 * mid)
+        for j, mode in enumerate(modes):
+            ends = []
+            for rows in (low, high):
+                p_real, p_imag = probes[mode, 0, rows], probes[mode, 1, rows]
+                x_real, x_imag = windows[slot, 0, rows], windows[slot, 1, rows]
+                ends.append((p_real * x_real - p_imag * x_imag, p_real * x_imag + p_imag * x_real))
+            for part, rows in enumerate((low, high)):
+                wave[j, 0, rows] = (ends[0][part] + ends[1][part]).astype(jnp.bfloat16)
+                wave[j, 1, rows] = (ends[0][part] - ends[1][part]).astype(jnp.bfloat16)
+        for j in range(len(modes)):
+            for k, rows in enumerate((low, high)):
+                strip = dot(tables[0][k], wave[j, k])
+                for part, source in enumerate((low, high)):
+                    left, right = strip[source, low], strip[source, high]
+                    target = slice(part * mid, (part + 1) * mid)
+                    half[j, 0, rows, target] = (left + right).astype(jnp.bfloat16)
+                    half[j, 1, rows, target] = (left - right).astype(jnp.bfloat16)
+        return [[dot(half[j, k], tables[1][k]) for k in range(2)] for j in range(len(modes))]
+
+    def paired(self, first, second):
+        mid = self.rim
+        products = [a * b for a, b in zip(first, second)]
+        return jnp.concatenate([p[:, :mid] + p[:, mid:] for p in products], 1)
+
+    def load(self, spectra, unit):
         wide = self.patch
-        x_real, x_imag = windows[slot, 0], windows[slot, 1]
+        return [spectra[unit, :, :wide], spectra[unit, :, wide:]]
+
+    def store(self, spectra, unit, field):
+        wide = self.patch
+        spectra[unit, :, :wide], spectra[unit, :, wide:] = field
+
+    def images(self, fields, weight, modes, probes, wave, half, tables):
+        mid = self.rim
+        low, high = slice(0, mid), slice(mid, 2 * mid)
+        doubled = 2.0 * weight
+        for j, field in enumerate(fields):
+            for k, columns in enumerate((low, high)):
+                factor = jnp.concatenate([doubled[:, columns]] * 2, 1)
+                half[j, k] = (field[k] * factor).astype(jnp.bfloat16)
+        for j in range(len(modes)):
+            even, odd = (dot(half[j, k], tables[0][k]) for k in range(2))
+            for columns, turned in ((low, even + odd), (high, even - odd)):
+                turned = turned.astype(jnp.bfloat16)
+                for k, rows in enumerate((low, high)):
+                    wave[j, k, low, columns] = turned[rows, low]
+                    wave[j, k, high, columns] = turned[rows, high]
+        sums = [[0.0, 0.0], [0.0, 0.0]]
         for j, mode in enumerate(modes):
-            p_real, p_imag = probes[mode, 0], probes[mode, 1]
-            wave[j, :wide] = (p_real * x_real - p_imag * x_imag).astype(jnp.bfloat16)
-            wave[j, wide:] = (p_real * x_imag + p_imag * x_real).astype(jnp.bfloat16)
-        for j in range(len(modes)):
-            half[j] = dot(tables[0][...], wave[j]).astype(jnp.bfloat16)
-        return [
-            dot(half[j, :wide], tables[1][:wide]) + dot(half[j, wide:], tables[1][wide:])
-            for j in range(len(modes))
-        ]
-
-    def images(self, fields, weight, modes, probes, wave, half, tables):
-        wide = self.patch
-        for j, field in enumerate(fields):
-            half[j, :wide] = (2.0 * field[:, :wide] * weight).astype(jnp.bfloat16)
-            half[j, wide:] = (2.0 * field[:, wide:] * weight).astype(jnp.bfloat16)
-        for j in range(len(modes)):
-            turned = dot(half[j, :wide], tables[0][:wide]) + dot(half[j, wide:], tables[0][wide:])
-            turned = turned.astype(jnp.bfloat16)
-            wave[j, :wide] = turned[:, :wide]
-            wave[j, wide:] = turned[:, wide:]
-        real_sum = imag_sum = 0.0
-        for j, mode in enumerate(modes):
-            back = dot(tables[1][...], wave[j])
-            p_real, p_imag = probes[mode, 0], probes[mode, 1]
-            real_sum = real_sum + (p_real * back[:wide] + p_imag * back[wide:])
-            imag_sum = imag_sum + (p_real * back[wide:] - p_imag * back[:wide])
-        return real_sum, imag_sum
+            even, odd = (dot(tables[1][k], wave[j, k]) for k in range(2))
+            for side, (rows, back) in enumerate(((low, even + odd), (high, even - odd))):
+                p_real, p_imag = probes[mode, 0, rows], probes[mode, 1, rows]
+                sums[side][0] = sums[side][0] + (p_real * back[low] + p_imag * back[high])
+                sums[side][1] = sums[side][1] + (p_real * back[high] - p_imag * back[low])
+        return sums
+
+    def add_images(self, image, sums):
+        mid = self.rim
+        for side in range(2):
+            for part in range(2):
+                image[part, side * mid : (side + 1) * mid] += sums[side][part]
 
     def send(self, canvas, parity, middle_out, sends):
         rim, rows = self.rim, self.tile_rows
@@ -224,8 +260,8 @@
             fields = plan.spectra(slot, modes, probes, windows, wave, half, tables)
             power = 0.0
             for mode, field in zip(modes, fields):
-                spectra[slot * plan.modes + mode] = field
-                power = power + (field[:, :wide] * field[:, :wide] + field[:, wide:] * field[:, wide:])
+                plan.store(spectra, slot * plan.modes + mode, field)
+                power = power + plan.paired(field, field)
             intensity[slot] += power
 
         plan.each_modes(slot, forward)
@@ -234,10 +270,9 @@
         image[...] = jnp.zeros_like(image)
 
         def backward(modes):
-            fields = [spectra[slot * plan.modes + mode] for mode in modes]
-            real_sum, imag_sum = plan.images(fields, windows[slot, 0], modes, probes, wave, half, tables)
-            image[0] += real_sum
-            image[1] += imag_sum
+            fields = [plan.load(spectra, slot * plan.modes + mode) for mode in modes]
+            sums = plan.images(fields, windows[slot, 0], modes, probes, wave, half, tables)
+            plan.add_images(image, sums)
 
         plan.each_modes(slot, backward)
         for part in range(2):
@@ -271,13 +306,10 @@
             fields = plan.spectra(slot, modes, probes, windows, wave, half, tables)
             cross = square = 0.0
             for mode, field in zip(modes, fields):
-                base = spectra[slot * plan.modes + mode]
-                cross = cross + (base[:, :wide] * field[:, :wide] + base[:, wide:] * field[:, wide:])
+                cross = cross + plan.paired(plan.load(spectra, slot * plan.modes + mode), field)
                 if not last:
-                    moved[slot * plan.modes + mode] = field
-                    square = square + (
-                        field[:, :wide] * field[:, :wide] + field[:, wide:] * field[:, wide:]
-                    )
+                    plan.store(moved, slot * plan.modes + mode, field)
+                    square = square + plan.paired(field, field)
             change[slot] += 2.0 * cross
             if not last:
                 power[slot] += square
@@ -309,12 +341,12 @@
         def backward(modes):
             fields = []
             for mode in modes:
-                field = spectra[slot * plan.modes + mode] + step * moved[slot * plan.modes + mode]
-                fresh[slot * plan.modes + mode] = field
-                fields.append(field)
-            real_sum, imag_sum = plan.images(fields, windows[slot, 0], modes, probes, wave, half, tables)
-            image[0] += real_sum
-            image[1] += imag_sum
+                unit = slot * plan.modes + mode
+                pairs = zip(plan.load(spectra, unit), plan.load(moved, unit))
+                fields.append([base + step * shift for base, shift in pairs])
+                plan.store(fresh, unit, fields[-1])
+            sums = plan.images(fields, windows[slot, 0], modes, probes, wave, half, tables)
+            plan.add_images(image, sums)
 
         plan.each_modes(slot, backward)
         for part in range(2):
@@ -339,6 +371,31 @@
     low, high = tile[:, :, : plan.rim], tile[:, :, plan.tile_cols - plan.rim :]
     for k, rim in enumerate(rims):
         rim[...] = jnp.where((info[SIDE_Y] == 0) == (k == 0), high, low)
+
+
+def stage_body(plan, *refs):
+    targets, one, two, shard, _, ordered, *copies = refs
+    wide = plan.patch
+    place = lax.broadcasted_iota(jnp.int32, (wide, wide), 0)
+    source = jnp.where(place < plan.rim, 2 * place, 2 * (place - plan.rim) + 1)
+    pick = jnp.where(source == lax.broadcasted_iota(jnp.int32, (wide, wide), 1), 1.0, 0.0)
+    pick = pick.astype(jnp.bfloat16)
+
+    def parts_of(block):
+        parts = []
+        for _ in range(3):
+            parts.append(block.astype(jnp.bfloat16))
+            block = block - parts[-1].astype(jnp.float32)
+        return parts
+
+    for slot in range(plan.slots):
+        rows = sum(dot(pick, part) for part in parts_of(targets[slot]))
+        ordered[slot] = sum(
+            lax.dot_general(part, pick, (((1,), (1,)), ((), ())), preferred_element_type=jnp.float32)
+            for part in parts_of(rows)
+        )
+    for source, copy in zip((one, two, shard), copies):
+        copy[...] = source[...]
 
 
 def join_body(plan, swaps, columns, shards, *refs):
@@ -462,6 +519,16 @@
         [(lead, 2, span, patch)] + [(2, tile_rows, rim)] * swaps_y,
         [smem] + [vmem] * 2,
         [info, probe_shard, object_field],
+        pinned=False,
+    )
+    targets, one, two, own_shard = call(
+        functools.partial(stage_body, plan),
+        "stage",
+        [targets.shape, one.shape, two.shape, probe_shard.shape],
+        [vmem] * 4 + [pl.ANY],
+        [targets, one, two, probe_shard, mine],
+        pinned=False,
+        dtypes={1: jnp.bfloat16, 2: jnp.bfloat16},
     )
     parts = []
     for pairs in exchanges(groups):
@@ -482,7 +549,7 @@
         [(units, patch, 2 * patch), (slots, patch, patch), (modes, 2, patch, patch), tall]
         + [fold] * swaps_x,
         [smem] * 3 + [vmem] * (7 + swaps_x),
-        [info, centres, weights_x, middle, *rows_around(middle), probe_shard, packed, crossed]
+        [info, centres, weights_x, middle, *rows_around(middle), own_shard, packed, crossed]
         + [targets, one, two],
         scratch=plan.scratch() + [image_scratch],
     )
@@ -524,6 +591,7 @@
         [(2, tile_rows, tile_cols)],
         [smem] * (len(totals) + 1) + [vmem] * 3,
         [*totals, first_step, object_field, first_way, last_way],
+        [None],
     )
     return current
 

time: 152 us -> 141 us (0.928)
  Pallas kernels: 54.2 us -> 48.1 us
  waiting for transfers between devices: 51.9 us -> 48.3 us
    pallas_call x11 -> x12, Pallas kernels: 54.2 us -> 48.1 us  [call(): pl.pallas_call(body, name=name, out_shape=[space(shape, dtypes.get(k, jnp...]
    ppermute x14, waiting for transfers between devices: 39.4 us -> 35.8 us  [swap(): lax.ppermute(block, axis, pairs)]
    unnamed x23 -> x20, local copies, waits for them, and re-layouts: 8.87 us -> 7.97 us
  transfers between devices with their start and end apart: 32 -> 32, of which waited for: 22 -> 21; matrix products, arithmetic and copies ran while one was open for 0% -> 0% of each run, Pallas kernels for 0% -> 1%
where the time goes in v3:
time: 141 us
  waiting for transfers between devices  48.3 us (34%)
  Pallas kernels  48.1 us (34%)
  starting transfers between devices  35.2 us (25%)
  local copies, waits for them, and re-layouts  8.06 us (6%)
    pallas_call x12, Pallas kernels, call(): pl.pallas_call(body, name=name, out_shape=[space(shape, dtypes.get(k, jnp...  48.1 us
    ppermute x14, waiting for transfers between devices, swap(): lax.ppermute(block, axis, pairs)  35.8 us
    ppermute x9, starting transfers between devices, shards(): lax.ppermute(block, 'gy', others)  13.2 us
    ppermute x14, starting transfers between devices, swap(): lax.ppermute(block, axis, pairs)  9.09 us
    unnamed x20, local copies, waits for them, and re-layouts  7.97 us
    ppermute x9, waiting for transfers between devices, shards(): lax.ppermute(block, 'gy', others)  7.09 us
    ppermute x6, starting transfers between devices, totals_of(): lax.ppermute(sums, 'gy', pairs)  6.98 us
    ppermute x3, starting transfers between devices, shards(): block = lax.ppermute(mine, 'ma', pairs)  5.93 us
  transfers between devices with their start and end apart: 32, of which 21 were waited for; matrix products, arithmetic and copies ran while one was open for 0% of the time, Pallas kernels for 1%

profile of v3, /device:TPU:0, one launch (start us, length us, event | category | flops | bytes accessed | tf_op | source)
XLA Modules:
  0.0 140.6 jit_solution(18297657595770505360)
XLA Ops:
  0.9 1.2 copy-done
  2.1 0.9 copy-done.2
  3.7 5.1 %collective-permute-start.10 = (f32[2,2,32,256]{3,2,1,0:T(8,128)S(1)}, f32[2,2,32,256]{3,2,1,0:T(8,128)S(1)}, u32[]{:S(2)}, u32[]{:S(2)}) collective-permute-start(f32[2,2,32,256]{3,2,1,0:T(8,128)S(1)} %get-tuple-element.45.refs_4_), channel_id=1, source_target_pairs={{0,3},{1,2},{2,1},{3,0},{4,7},{5,6},{6,5},{7,4},{8,11},{9,10},{10,... | collective-permute-start | bytes 393224 | tf_op jit(solution)/shard_map/ppermute | solution.py:535
  8.8 1.5 %collective-permute-start = (f32[2,128,128]{2,1,0:T(8,128)S(1)}, f32[2,128,128]{2,1,0:T(8,128)S(1)}, u32[]{:S(2)}, u32[]{:S(2)}) collective-permute-start(f32[2,128,128]{2,1,0:T(8,128)S(1)} %get-tuple-element.43), channel_id=1, source_target_pairs={{0,4},{4,0},{8,12},{12,8},{1,5},{5,1},{9,13},{13,9},{2,6},{6,2},{1... | collective-permute-start | bytes 393224 | tf_op jit(solution)/shard_map/ppermute | solution.py:57
  10.3 1.5 %collective-permute-start.1 = (f32[2,128,128]{2,1,0:T(8,128)S(1)}, f32[2,128,128]{2,1,0:T(8,128)S(1)}, u32[]{:S(2)}, u32[]{:S(2)}) collective-permute-start(f32[2,128,128]{2,1,0:T(8,128)S(1)} %get-tuple-element.44), channel_id=1, source_target_pairs={{4,8},{12,0},{8,4},{0,12},{5,9},{13,1},{9,5},{1,13},{6,10},{14,2},... | collective-permute-start | bytes 393224 | tf_op jit(solution)/shard_map/ppermute | solution.py:57
  12.6 2.6 %collective-permute-start.13 = (f32[2,2,32,256]{3,2,1,0:T(8,128)S(1)}, f32[2,2,32,256]{3,2,1,0:T(8,128)S(1)}, u32[]{:S(2)}, u32[]{:S(2)}) collective-permute-start(f32[2,2,32,256]{3,2,1,0:T(8,128)S(1)} %collective-permute-done.10.refs_12_), channel_id=1, source_target_pairs={{0,12},{4,8},{8,4},{12,0},{1,13},{5,9},{9,5},{13,1},{2,14},{6,10},... | collective-permute-start | bytes 393224 | tf_op jit(solution)/shard_map/ppermute | solution.py:536
  15.2 1.5 %collective-permute-start.12 = (f32[2,2,32,256]{3,2,1,0:T(8,128)S(1)}, f32[2,2,32,256]{3,2,1,0:T(8,128)S(1)}, u32[]{:S(2)}, u32[]{:S(2)}) collective-permute-start(f32[2,2,32,256]{3,2,1,0:T(8,128)S(1)} %collective-permute-done.10.refs_12_), channel_id=1, source_target_pairs={{0,8},{4,12},{8,0},{12,4},{1,9},{5,13},{9,1},{13,5},{2,10},{6,14},... | collective-permute-start | bytes 393224 | tf_op jit(solution)/shard_map/ppermute | solution.py:536
  16.7 2.3 %collective-permute-done.1.refs_3_ = f32[2,128,128]{2,1,0:T(8,128)S(1)} collective-permute-done((f32[2,128,128]{2,1,0:T(8,128)S(1)}, f32[2,128,128]{2,1,0:T(8,128)S(1)}, u32[]{:S(2)}, u32[]{:S(2)}) %collective-permute-start.1) | collective-permute-done | bytes 131104 | tf_op jit(solution)/shard_map/ppermute | solution.py:57
  19.0 1.5 %collective-permute-start.11 = (f32[2,2,32,256]{3,2,1,0:T(8,128)S(1)}, f32[2,2,32,256]{3,2,1,0:T(8,128)S(1)}, u32[]{:S(2)}, u32[]{:S(2)}) collective-permute-start(f32[2,2,32,256]{3,2,1,0:T(8,128)S(1)} %collective-permute-done.10.refs_12_), channel_id=1, source_target_pairs={{0,4},{4,0},{8,12},{12,8},{1,5},{5,1},{9,13},{13,9},{2,6},{6,2},{1... | collective-permute-start | bytes 393224 | tf_op jit(solution)/shard_map/ppermute | solution.py:536
  20.5 1.8 %collective-permute-start.9 = (f32[2,2,32,256]{3,2,1,0:T(8,128)S(1)}, f32[2,2,32,256]{3,2,1,0:T(8,128)S(1)}, u32[]{:S(2)}, u32[]{:S(2)}) collective-permute-start(f32[2,2,32,256]{3,2,1,0:T(8,128)S(1)} %collective-permute-done.6.refs_8_), channel_id=1, source_target_pairs={{0,12},{4,8},{8,4},{12,0},{1,13},{5,9},{9,5},{13,1},{2,14},{6,10},... | collective-permute-start | bytes 393224 | tf_op jit(solution)/shard_map/ppermute | solution.py:536
  22.8 1.2 collective-permute-start.7
  24.0 1.8 %collective-permute-start.5 = (f32[2,2,32,256]{3,2,1,0:T(8,128)S(1)}, f32[2,2,32,256]{3,2,1,0:T(8,128)S(1)}, u32[]{:S(2)}, u32[]{:S(2)}) collective-permute-start(f32[2,2,32,256]{3,2,1,0:T(8,128)S(1)} %collective-permute-done.2.refs_4_), channel_id=1, source_target_pairs={{0,12},{4,8},{8,4},{12,0},{1,13},{5,9},{9,5},{13,1},{2,14},{6,10},... | collective-permute-start | bytes 393224 | tf_op jit(solution)/shard_map/ppermute | solution.py:536
  26.3 1.5 %collective-permute-done.9.refs_11_ = f32[2,2,32,256]{3,2,1,0:T(8,128)S(1)} collective-permute-done((f32[2,2,32,256]{3,2,1,0:T(8,128)S(1)}, f32[2,2,32,256]{3,2,1,0:T(8,128)S(1)}, u32[]{:S(2)}, u32[]{:S(2)}) %collective-permute-start.9) | collective-permute-done | bytes 131104 | tf_op jit(solution)/shard_map/ppermute | solution.py:536
  27.8 1.8 %collective-permute-start.3 = (f32[2,2,32,256]{3,2,1,0:T(8,128)S(1)}, f32[2,2,32,256]{3,2,1,0:T(8,128)S(1)}, u32[]{:S(2)}, u32[]{:S(2)}) collective-permute-start(f32[2,2,32,256]{3,2,1,0:T(8,128)S(1)} %collective-permute-done.2.refs_4_), channel_id=1, source_target_pairs={{0,4},{4,0},{8,12},{12,8},{1,5},{5,1},{9,13},{13,9},{2,6},{6,2},{1... | collective-permute-start | bytes 393224 | tf_op jit(solution)/shard_map/ppermute | solution.py:536
  29.6 1.9 %collective-permute-done.8.refs_10_ = f32[2,2,32,256]{3,2,1,0:T(8,128)S(1)} collective-permute-done((f32[2,2,32,256]{3,2,1,0:T(8,128)S(1)}, f32[2,2,32,256]{3,2,1,0:T(8,128)S(1)}, u32[]{:S(2)}, u32[]{:S(2)}) %collective-permute-start.8) | collective-permute-done | bytes 131104 | tf_op jit(solution)/shard_map/ppermute | solution.py:536
  31.5 1.9 %collective-permute-done.5.refs_7_ = f32[2,2,32,256]{3,2,1,0:T(8,128)S(1)} collective-permute-done((f32[2,2,32,256]{3,2,1,0:T(8,128)S(1)}, f32[2,2,32,256]{3,2,1,0:T(8,128)S(1)}, u32[]{:S(2)}, u32[]{:S(2)}) %collective-permute-start.5) | collective-permute-done | bytes 131104 | tf_op jit(solution)/shard_map/ppermute | solution.py:536
  33.4 1.0 collective-permute-done.4.refs_6_
  34.4 0.8 collective-permute-done.3.refs_5_
  35.2 0.9 copy-done.3
  37.5 1.2 copy-done.1
  38.7 1.0 copy-done.5
  39.7 0.9 copy-done.6
  40.7 0.9 copy-done.7
  41.6 0.8 stage.1
  43.2 15.3 %start.1 = (f32[16,256,512]{2,1,0:T(8,128)S(1)}, f32[2,256,256]{2,1,0:T(8,128)S(1)}, f32[8,2,256,256]{3,2,1,0:T(8,128)S(1)}, f32[2,128,512]{2,1,0:T(8,128)S(1)}, f32[2,128,512]{2,1,0:T(8,128)S(1)}) custom-call(s32[5]{0:T(128)S(1)} %stack.52.refs_0_, s32[2,2]{1,0:T(2,128)S(1)} %bitcast.17, f32[2]{0:T(128)S(1)} %get-tuple-element.40.refs_2_.refs_1_, ...), custom_call_target="tpu_custom_call" | custom-call | tf_op jit(solution)/shard_map/start/pallas_call | solution.py:85
  58.6 1.8 %collective-permute-done.16.refs_3_ = f32[2,128,512]{2,1,0:T(8,128)S(1)} collective-permute-done((f32[2,128,512]{2,1,0:T(8,128)S(1)}, f32[2,128,512]{2,1,0:T(8,128)S(1)}, u32[]{:S(2)}, u32[]{:S(2)}) %collective-permute-start.16) | collective-permute-done | bytes 524320 | tf_op jit(solution)/shard_map/ppermute | solution.py:57
  61.2 1.6 %collective-permute-start.17 = (f32[2,128,256]{2,1,0:T(8,128)S(1)}, f32[2,128,256]{2,1,0:T(8,128)S(1)}, u32[]{:S(2)}, u32[]{:S(2)}) collective-permute-start(f32[2,128,256]{2,1,0:T(8,128)S(1)} %get-tuple-element.55), channel_id=1, source_target_pairs={{0,4},{4,0},{8,12},{12,8},{1,5},{5,1},{9,13},{13,9},{2,6},{6,2},{1... | collective-permute-start | bytes 786440 | tf_op jit(solution)/shard_map/ppermute | solution.py:57
  62.9 7.5 %collective-permute-done.17.refs_3_ = f32[2,128,256]{2,1,0:T(8,128)S(1)} collective-permute-done((f32[2,128,256]{2,1,0:T(8,128)S(1)}, f32[2,128,256]{2,1,0:T(8,128)S(1)}, u32[]{:S(2)}, u32[]{:S(2)}) %collective-permute-start.17) | collective-permute-done | bytes 262176 | tf_op jit(solution)/shard_map/ppermute | solution.py:57
  70.4 4.5 %collective-permute-done.18.refs_4_ = f32[2,128,256]{2,1,0:T(8,128)S(1)} collective-permute-done((f32[2,128,256]{2,1,0:T(8,128)S(1)}, f32[2,128,256]{2,1,0:T(8,128)S(1)}, u32[]{:S(2)}, u32[]{:S(2)}) %collective-permute-start.18) | collective-permute-done | bytes 262176 | tf_op jit(solution)/shard_map/ppermute | solution.py:57
  75.8 1.9 %collective-permute-done.19.refs_4_ = f32[2,128,512]{2,1,0:T(8,128)S(1)} collective-permute-done((f32[2,128,512]{2,1,0:T(8,128)S(1)}, f32[2,128,512]{2,1,0:T(8,128)S(1)}, u32[]{:S(2)}, u32[]{:S(2)}) %collective-permute-start.19) | collective-permute-done | bytes 524320 | tf_op jit(solution)/shard_map/ppermute | solution.py:57
  77.7 8.6 %change.1 = (f32[2]{0:T(128)S(1)}, f32[16,256,512]{2,1,0:T(8,128)S(1)}, f32[2,256,256]{2,1,0:T(8,128)S(1)}, f32[2,256,256]{2,1,0:T(8,128)S(1)}) custom-call(s32[5]{0:T(128)S(1)} %stack.52.refs_0_, s32[2,2]{1,0:T(2,128)S(1)} %bitcast.18, f32[2]{0:T(128)S(1)} %get-tuple-element.40.refs_2_.refs_1_, f32[2,128,512]{2,1,0:T(8,128)S(1)} %halo.2.refs_3_.refs_6_, ...), custom_call_target="tpu_custom_call" | custom-call | tf_op jit(solution)/shard_map/change/pallas_call | solution.py:85
  86.5 1.0 collective-permute-done.20
  87.5 2.7 %collective-permute-start.23 = (f32[2]{0:T(128)S(1)}, f32[2]{0:T(128)S(1)}, u32[]{:S(2)}, u32[]{:S(2)}) collective-permute-start(f32[2]{0:T(128)S(1)} %add.26.refs_2_), channel_id=1, source_target_pairs={{0,12},{4,8},{8,4},{12,0},{1,13},{5,9},{9,5},{13,1},{2,14},{6,10},... | collective-permute-start | bytes 32 | tf_op jit(solution)/shard_map/ppermute | solution.py:462
  91.0 1.0 collective-permute-done.23.refs_5_
  92.0 1.8 %collective-permute-done.22.refs_4_ = f32[2]{0:T(128)S(1)} collective-permute-done((f32[2]{0:T(128)S(1)}, f32[2]{0:T(128)S(1)}, u32[]{:S(2)}, u32[]{:S(2)}) %collective-permute-start.22) | collective-permute-done | bytes 40 | tf_op jit(solution)/shard_map/ppermute | solution.py:462
  94.3 8.8 %image.1 = (f32[16,256,512]{2,1,0:T(8,128)S(1)}, f32[1]{0:T(128)}, f32[2,128,512]{2,1,0:T(8,128)S(1)}, f32[2,128,512]{2,1,0:T(8,128)S(1)}) custom-call(s32[5]{0:T(128)S(1)} %stack.52.refs_0_, s32[2,2]{1,0:T(2,128)S(1)} %bitcast.19, f32[2]{0:T(128)S(1)} %add.26.refs_2_, f32[2]{0:T(128)S(1)} %collective-permute-done.21.refs_3_, ...), custom_call_target="tpu_custom_call" | custom-call | tf_op jit(solution)/shard_map/image/pallas_call | solution.py:85
  103.1 1.9 %collective-permute-done.24.refs_3_ = f32[2,128,512]{2,1,0:T(8,128)S(1)} collective-permute-done((f32[2,128,512]{2,1,0:T(8,128)S(1)}, f32[2,128,512]{2,1,0:T(8,128)S(1)}, u32[]{:S(2)}, u32[]{:S(2)}) %collective-permute-start.24) | collective-permute-done | bytes 524320 | tf_op jit(solution)/shard_map/ppermute | solution.py:57
  106.2 2.7 %collective-permute-start.26 = (f32[2,128,256]{2,1,0:T(8,128)S(1)}, f32[2,128,256]{2,1,0:T(8,128)S(1)}, u32[]{:S(2)}, u32[]{:S(2)}) collective-permute-start(f32[2,128,256]{2,1,0:T(8,128)S(1)} %get-tuple-element.68), channel_id=1, source_target_pairs={{4,8},{12,0},{8,4},{0,12},{5,9},{13,1},{9,5},{1,13},{6,10},{14,2},... | collective-permute-start | bytes 786440 | tf_op jit(solution)/shard_map/ppermute | solution.py:57
  108.9 6.2 %collective-permute-done.25.refs_3_ = f32[2,128,256]{2,1,0:T(8,128)S(1)} collective-permute-done((f32[2,128,256]{2,1,0:T(8,128)S(1)}, f32[2,128,256]{2,1,0:T(8,128)S(1)}, u32[]{:S(2)}, u32[]{:S(2)}) %collective-permute-start.25) | collective-permute-done | bytes 262176 | tf_op jit(solution)/shard_map/ppermute | solution.py:57
  115.0 5.7 %collective-permute-done.26.refs_4_ = f32[2,128,256]{2,1,0:T(8,128)S(1)} collective-permute-done((f32[2,128,256]{2,1,0:T(8,128)S(1)}, f32[2,128,256]{2,1,0:T(8,128)S(1)}, u32[]{:S(2)}, u32[]{:S(2)}) %collective-permute-start.26) | collective-permute-done | bytes 262176 | tf_op jit(solution)/shard_map/ppermute | solution.py:57
  121.6 1.9 %collective-permute-done.27.refs_4_ = f32[2,128,512]{2,1,0:T(8,128)S(1)} collective-permute-done((f32[2,128,512]{2,1,0:T(8,128)S(1)}, f32[2,128,512]{2,1,0:T(8,128)S(1)}, u32[]{:S(2)}, u32[]{:S(2)}) %collective-permute-start.27) | collective-permute-done | bytes 524320 | tf_op jit(solution)/shard_map/ppermute | solution.py:57
  123.5 8.3 %last_change.1 = f32[2]{0:T(128)S(1)} custom-call(s32[5]{0:T(128)S(1)} %stack.52.refs_0_, s32[2,2]{1,0:T(2,128)S(1)} %bitcast.20, f32[2]{0:T(128)S(1)} %get-tuple-element.40.refs_2_.refs_1_, f32[2,128,512]{2,1,0:T(8,128)S(1)} %halo.3.refs_3_.refs_7_, f32[2,128,512]{2,1,0:T(8,128)S(1)} %collective-permute-done.27.refs_4_, ...), custom_call_target="tpu_custom_call" | custom-call | tf_op jit(solution)/shard_map/last_change/pallas_call | solution.py:85
  132.0 1.0 collective-permute-done.28
  133.3 1.8 %collective-permute-start.30 = (f32[2]{0:T(128)S(1)}, f32[2]{0:T(128)S(1)}, u32[]{:S(2)}, u32[]{:S(2)}) collective-permute-start(f32[2]{0:T(128)S(1)} %add.27.refs_0_), channel_id=1, source_target_pairs={{0,8},{4,12},{8,0},{12,4},{1,9},{5,13},{9,1},{13,5},{2,10},{6,14},... | collective-permute-start | bytes 32 | tf_op jit(solution)/shard_map/ppermute | solution.py:462
  135.1 1.5 %collective-permute-start.29 = (f32[2]{0:T(128)S(1)}, f32[2]{0:T(128)S(1)}, u32[]{:S(2)}, u32[]{:S(2)}) collective-permute-start(f32[2]{0:T(128)S(1)} %add.27.refs_0_), channel_id=1, source_target_pairs={{0,4},{4,0},{8,12},{12,8},{1,5},{5,1},{9,13},{13,9},{2,6},{6,2},{1... | collective-permute-start | bytes 32 | tf_op jit(solution)/shard_map/ppermute | solution.py:462
  136.6 1.0 collective-permute-done.31.refs_3_
  137.5 1.1 collective-permute-done.29.refs_1_
  138.7 2.0 %finish.1 = f32[2,128,256]{2,1,0:T(8,128)} custom-call(f32[2]{0:T(128)S(1)} %add.27.refs_0_, f32[2]{0:T(128)S(1)} %collective-permute-done.29.refs_1_, f32[2]{0:T(128)S(1)} %collective-permute-done.30.refs_2_, f32[2]{0:T(128)S(1)} %collective-permute-done.31.refs_3_, f32[1]{0:T(128)} %get-tuple-element.70.refs_4_, f32[2,128,256]{2,1,0:T(8,128)S(1)} %copy-done.4, ...), custom_call_target="tpu_custom_call" | custom-call | tf_op jit(solution)/shard_map/finish/pallas_call | solution.py:85
  (53 shorter events, 10.5 us)
Async XLA Ops:
  0.0 77.7 %copy-start.9 = (s32[1,1,2,2]{3,2,1,0:T(2,128)S(1)}, s32[1,1,2,2]{3,2,1,0:T(2,128)}, u32[]{:S(2)}) copy-start(s32[1,1,2,2]{3,2,1,0:T(2,128)} %param.10) | copy-start | bytes 52
  0.9 1.2 copy-start
  2.1 0.9 copy-start.2
  3.7 8.9 %collective-permute-start.10 = (f32[2,2,32,256]{3,2,1,0:T(8,128)S(1)}, f32[2,2,32,256]{3,2,1,0:T(8,128)S(1)}, u32[]{:S(2)}, u32[]{:S(2)}) collective-permute-start(f32[2,2,32,256]{3,2,1,0:T(8,128)S(1)} %get-tuple-element.45.refs_4_), channel_id=1, source_target_pairs={{0,3},{1,2},{2,1},{3,0},{4,7},{5,6},{6,5},{7,4},{8,11},{9,10},{10,... | collective-permute-start | bytes 393224 | tf_op jit(solution)/shard_map/ppermute | solution.py:535
  8.8 6.3 %collective-permute-start = (f32[2,128,128]{2,1,0:T(8,128)S(1)}, f32[2,128,128]{2,1,0:T(8,128)S(1)}, u32[]{:S(2)}, u32[]{:S(2)}) collective-permute-start(f32[2,128,128]{2,1,0:T(8,128)S(1)} %get-tuple-element.43), channel_id=1, source_target_pairs={{0,4},{4,0},{8,12},{12,8},{1,5},{5,1},{9,13},{13,9},{2,6},{6,2},{1... | collective-permute-start | bytes 393224 | tf_op jit(solution)/shard_map/ppermute | solution.py:57
  10.3 8.7 %collective-permute-start.1 = (f32[2,128,128]{2,1,0:T(8,128)S(1)}, f32[2,128,128]{2,1,0:T(8,128)S(1)}, u32[]{:S(2)}, u32[]{:S(2)}) collective-permute-start(f32[2,128,128]{2,1,0:T(8,128)S(1)} %get-tuple-element.44), channel_id=1, source_target_pairs={{4,8},{12,0},{8,4},{0,12},{5,9},{13,1},{9,5},{1,13},{6,10},{14,2},... | collective-permute-start | bytes 393224 | tf_op jit(solution)/shard_map/ppermute | solution.py:57
  11.8 8.7 %collective-permute-start.6 = (f32[2,2,32,256]{3,2,1,0:T(8,128)S(1)}, f32[2,2,32,256]{3,2,1,0:T(8,128)S(1)}, u32[]{:S(2)}, u32[]{:S(2)}) collective-permute-start(f32[2,2,32,256]{3,2,1,0:T(8,128)S(1)} %get-tuple-element.45.refs_4_), channel_id=1, source_target_pairs={{0,2},{1,3},{2,0},{3,1},{4,6},{5,7},{6,4},{7,5},{8,10},{9,11},{10,... | collective-permute-start | bytes 393224 | tf_op jit(solution)/shard_map/ppermute | solution.py:535
  11.8 10.5 %collective-permute-start.2 = (f32[2,2,32,256]{3,2,1,0:T(8,128)S(1)}, f32[2,2,32,256]{3,2,1,0:T(8,128)S(1)}, u32[]{:S(2)}, u32[]{:S(2)}) collective-permute-start(f32[2,2,32,256]{3,2,1,0:T(8,128)S(1)} %get-tuple-element.45.refs_4_), channel_id=1, source_target_pairs={{0,1},{1,0},{2,3},{3,2},{4,5},{5,4},{6,7},{7,6},{8,9},{9,8},{10,11... | collective-permute-start | bytes 393224 | tf_op jit(solution)/shard_map/ppermute | solution.py:535
  12.6 10.3 %collective-permute-start.13 = (f32[2,2,32,256]{3,2,1,0:T(8,128)S(1)}, f32[2,2,32,256]{3,2,1,0:T(8,128)S(1)}, u32[]{:S(2)}, u32[]{:S(2)}) collective-permute-start(f32[2,2,32,256]{3,2,1,0:T(8,128)S(1)} %collective-permute-done.10.refs_12_), channel_id=1, source_target_pairs={{0,12},{4,8},{8,4},{12,0},{1,13},{5,9},{9,5},{13,1},{2,14},{6,10},... | collective-permute-start | bytes 393224 | tf_op jit(solution)/shard_map/ppermute | solution.py:536
  15.2 8.9 %collective-permute-start.12 = (f32[2,2,32,256]{3,2,1,0:T(8,128)S(1)}, f32[2,2,32,256]{3,2,1,0:T(8,128)S(1)}, u32[]{:S(2)}, u32[]{:S(2)}) collective-permute-start(f32[2,2,32,256]{3,2,1,0:T(8,128)S(1)} %collective-permute-done.10.refs_12_), channel_id=1, source_target_pairs={{0,8},{4,12},{8,0},{12,4},{1,9},{5,13},{9,1},{13,5},{2,10},{6,14},... | collective-permute-start | bytes 393224 | tf_op jit(solution)/shard_map/ppermute | solution.py:536
  19.0 6.8 %collective-permute-start.11 = (f32[2,2,32,256]{3,2,1,0:T(8,128)S(1)}, f32[2,2,32,256]{3,2,1,0:T(8,128)S(1)}, u32[]{:S(2)}, u32[]{:S(2)}) collective-permute-start(f32[2,2,32,256]{3,2,1,0:T(8,128)S(1)} %collective-permute-done.10.refs_12_), channel_id=1, source_target_pairs={{0,4},{4,0},{8,12},{12,8},{1,5},{5,1},{9,13},{13,9},{2,6},{6,2},{1... | collective-permute-start | bytes 393224 | tf_op jit(solution)/shard_map/ppermute | solution.py:536
  20.5 7.3 %collective-permute-start.9 = (f32[2,2,32,256]{3,2,1,0:T(8,128)S(1)}, f32[2,2,32,256]{3,2,1,0:T(8,128)S(1)}, u32[]{:S(2)}, u32[]{:S(2)}) collective-permute-start(f32[2,2,32,256]{3,2,1,0:T(8,128)S(1)} %collective-permute-done.6.refs_8_), channel_id=1, source_target_pairs={{0,12},{4,8},{8,4},{12,0},{1,13},{5,9},{9,5},{13,1},{2,14},{6,10},... | collective-permute-start | bytes 393224 | tf_op jit(solution)/shard_map/ppermute | solution.py:536
  22.3 9.2 %collective-permute-start.8 = (f32[2,2,32,256]{3,2,1,0:T(8,128)S(1)}, f32[2,2,32,256]{3,2,1,0:T(8,128)S(1)}, u32[]{:S(2)}, u32[]{:S(2)}) collective-permute-start(f32[2,2,32,256]{3,2,1,0:T(8,128)S(1)} %collective-permute-done.6.refs_8_), channel_id=1, source_target_pairs={{0,8},{4,12},{8,0},{12,4},{1,9},{5,13},{9,1},{13,5},{2,10},{6,14},... | collective-permute-start | bytes 393224 | tf_op jit(solution)/shard_map/ppermute | solution.py:536
  22.8 8.7 %collective-permute-start.7 = (f32[2,2,32,256]{3,2,1,0:T(8,128)S(1)}, f32[2,2,32,256]{3,2,1,0:T(8,128)S(1)}, u32[]{:S(2)}, u32[]{:S(2)}) collective-permute-start(f32[2,2,32,256]{3,2,1,0:T(8,128)S(1)} %collective-permute-done.6.refs_8_), channel_id=1, source_target_pairs={{0,4},{4,0},{8,12},{12,8},{1,5},{5,1},{9,13},{13,9},{2,6},{6,2},{1... | collective-permute-start | bytes 393224 | tf_op jit(solution)/shard_map/ppermute | solution.py:536
  24.0 9.4 %collective-permute-start.5 = (f32[2,2,32,256]{3,2,1,0:T(8,128)S(1)}, f32[2,2,32,256]{3,2,1,0:T(8,128)S(1)}, u32[]{:S(2)}, u32[]{:S(2)}) collective-permute-start(f32[2,2,32,256]{3,2,1,0:T(8,128)S(1)} %collective-permute-done.2.refs_4_), channel_id=1, source_target_pairs={{0,12},{4,8},{8,4},{12,0},{1,13},{5,9},{9,5},{13,1},{2,14},{6,10},... | collective-permute-start | bytes 393224 | tf_op jit(solution)/shard_map/ppermute | solution.py:536
  25.8 8.6 %collective-permute-start.4 = (f32[2,2,32,256]{3,2,1,0:T(8,128)S(1)}, f32[2,2,32,256]{3,2,1,0:T(8,128)S(1)}, u32[]{:S(2)}, u32[]{:S(2)}) collective-permute-start(f32[2,2,32,256]{3,2,1,0:T(8,128)S(1)} %collective-permute-done.2.refs_4_), channel_id=1, source_target_pairs={{0,8},{4,12},{8,0},{12,4},{1,9},{5,13},{9,1},{13,5},{2,10},{6,14},... | collective-permute-start | bytes 393224 | tf_op jit(solution)/shard_map/ppermute | solution.py:536
  27.8 7.4 %collective-permute-start.3 = (f32[2,2,32,256]{3,2,1,0:T(8,128)S(1)}, f32[2,2,32,256]{3,2,1,0:T(8,128)S(1)}, u32[]{:S(2)}, u32[]{:S(2)}) collective-permute-start(f32[2,2,32,256]{3,2,1,0:T(8,128)S(1)} %collective-permute-done.2.refs_4_), channel_id=1, source_target_pairs={{0,4},{4,0},{8,12},{12,8},{1,5},{5,1},{9,13},{13,9},{2,6},{6,2},{1... | collective-permute-start | bytes 393224 | tf_op jit(solution)/shard_map/ppermute | solution.py:536
  35.2 1.0 copy-start.3
  36.9 5.6 %collective-permute-start.15 = (f32[3,4,2,2,32,256]{5,4,3,2,1,0:T(8,128)S(1)}, f32[3,4,2,2,32,256]{5,4,3,2,1,0:T(8,128)S(1)}, u32[]{:S(2)}, u32[]{:S(2)}) collective-permute-start(f32[3,4,2,2,32,256]{5,4,3,2,1,0:T(8,128)S(1)} %get-tuple-element.48.refs_6_), channel_id=1, source_target_pairs={{0,16},{16,0},{1,17},{17,1},{2,18},{18,2},{3,19},{19,3},{4,20},{20... | collective-permute-start | bytes 4718600 | tf_op jit(solution)/shard_map/ppermute | solution.py:57
  37.0 5.5 %collective-permute-start.14 = (f32[2,128,512]{2,1,0:T(8,128)S(1)}, f32[2,128,512]{2,1,0:T(8,128)S(1)}, u32[]{:S(2)}, u32[]{:S(2)}) collective-permute-start(f32[2,128,512]{2,1,0:T(8,128)S(1)} %get-tuple-element.46.refs_3_), channel_id=1, source_target_pairs={{0,16},{16,0},{1,17},{17,1},{2,18},{18,2},{3,19},{19,3},{4,20},{20... | collective-permute-start | bytes 1572872 | tf_op jit(solution)/shard_map/ppermute | solution.py:57
  37.5 1.2 copy-start.1
  38.7 1.0 copy-start.5
  39.7 0.9 copy-start.6
  40.7 0.9 copy-start.7
  42.5 0.7 copy-start.8
  58.4 2.0 %collective-permute-start.16 = (f32[2,128,512]{2,1,0:T(8,128)S(1)}, f32[2,128,512]{2,1,0:T(8,128)S(1)}, u32[]{:S(2)}, u32[]{:S(2)}) collective-permute-start(f32[2,128,512]{2,1,0:T(8,128)S(1)} %get-tuple-element.53), channel_id=1, source_target_pairs={{0,16},{16,0},{1,17},{17,1},{2,18},{18,2},{3,19},{19,3},{4,20},{20... | collective-permute-start | bytes 1572872 | tf_op jit(solution)/shard_map/ppermute | solution.py:57
  61.2 9.2 %collective-permute-start.17 = (f32[2,128,256]{2,1,0:T(8,128)S(1)}, f32[2,128,256]{2,1,0:T(8,128)S(1)}, u32[]{:S(2)}, u32[]{:S(2)}) collective-permute-start(f32[2,128,256]{2,1,0:T(8,128)S(1)} %get-tuple-element.55), channel_id=1, source_target_pairs={{0,4},{4,0},{8,12},{12,8},{1,5},{5,1},{9,13},{13,9},{2,6},{6,2},{1... | collective-permute-start | bytes 786440 | tf_op jit(solution)/shard_map/ppermute | solution.py:57
  62.8 12.2 %collective-permute-start.18 = (f32[2,128,256]{2,1,0:T(8,128)S(1)}, f32[2,128,256]{2,1,0:T(8,128)S(1)}, u32[]{:S(2)}, u32[]{:S(2)}) collective-permute-start(f32[2,128,256]{2,1,0:T(8,128)S(1)} %get-tuple-element.56), channel_id=1, source_target_pairs={{4,8},{12,0},{8,4},{0,12},{5,9},{13,1},{9,5},{1,13},{6,10},{14,2},... | collective-permute-start | bytes 786440 | tf_op jit(solution)/shard_map/ppermute | solution.py:57
  75.7 2.0 %collective-permute-start.19 = (f32[2,128,512]{2,1,0:T(8,128)S(1)}, f32[2,128,512]{2,1,0:T(8,128)S(1)}, u32[]{:S(2)}, u32[]{:S(2)}) collective-permute-start(f32[2,128,512]{2,1,0:T(8,128)S(1)} %halo.2.refs_3_.refs_6_), channel_id=1, source_target_pairs={{0,16},{16,0},{1,17},{17,1},{2,18},{18,2},{3,19},{19,3},{4,20},{20... | collective-permute-start | bytes 1572872 | tf_op jit(solution)/shard_map/ppermute | solution.py:57
  86.3 1.2 collective-permute-start.20
  87.5 4.5 %collective-permute-start.23 = (f32[2]{0:T(128)S(1)}, f32[2]{0:T(128)S(1)}, u32[]{:S(2)}, u32[]{:S(2)}) collective-permute-start(f32[2]{0:T(128)S(1)} %add.26.refs_2_), channel_id=1, source_target_pairs={{0,12},{4,8},{8,4},{12,0},{1,13},{5,9},{9,5},{13,1},{2,14},{6,10},... | collective-permute-start | bytes 32 | tf_op jit(solution)/shard_map/ppermute | solution.py:462
  90.2 3.6 %collective-permute-start.22 = (f32[2]{0:T(128)S(1)}, f32[2]{0:T(128)S(1)}, u32[]{:S(2)}, u32[]{:S(2)}) collective-permute-start(f32[2]{0:T(128)S(1)} %add.26.refs_2_), channel_id=1, source_target_pairs={{0,8},{4,12},{8,0},{12,4},{1,9},{5,13},{9,1},{13,5},{2,10},{6,14},... | collective-permute-start | bytes 32 | tf_op jit(solution)/shard_map/ppermute | solution.py:462
  90.7 3.6 %collective-permute-start.21 = (f32[2]{0:T(128)S(1)}, f32[2]{0:T(128)S(1)}, u32[]{:S(2)}, u32[]{:S(2)}) collective-permute-start(f32[2]{0:T(128)S(1)} %add.26.refs_2_), channel_id=1, source_target_pairs={{0,4},{4,0},{8,12},{12,8},{1,5},{5,1},{9,13},{13,9},{2,6},{6,2},{1... | collective-permute-start | bytes 32 | tf_op jit(solution)/shard_map/ppermute | solution.py:462
  103.0 2.0 %collective-permute-start.24 = (f32[2,128,512]{2,1,0:T(8,128)S(1)}, f32[2,128,512]{2,1,0:T(8,128)S(1)}, u32[]{:S(2)}, u32[]{:S(2)}) collective-permute-start(f32[2,128,512]{2,1,0:T(8,128)S(1)} %get-tuple-element.65), channel_id=1, source_target_pairs={{0,16},{16,0},{1,17},{17,1},{2,18},{18,2},{3,19},{19,3},{4,20},{20... | collective-permute-start | bytes 1572872 | tf_op jit(solution)/shard_map/ppermute | solution.py:57
  105.0 33.6 %copy-start.4 = (f32[2,128,256]{2,1,0:T(8,128)S(1)}, f32[2,128,256]{2,1,0:T(8,128)}, u32[]{:S(2)}) copy-start(f32[2,128,256]{2,1,0:T(8,128)} %refs_5_.1) | copy-start | bytes 786436
  105.8 9.2 %collective-permute-start.25 = (f32[2,128,256]{2,1,0:T(8,128)S(1)}, f32[2,128,256]{2,1,0:T(8,128)S(1)}, u32[]{:S(2)}, u32[]{:S(2)}) collective-permute-start(f32[2,128,256]{2,1,0:T(8,128)S(1)} %get-tuple-element.67), channel_id=1, source_target_pairs={{0,4},{4,0},{8,12},{12,8},{1,5},{5,1},{9,13},{13,9},{2,6},{6,2},{1... | collective-permute-start | bytes 786440 | tf_op jit(solution)/shard_map/ppermute | solution.py:57
  106.2 14.6 %collective-permute-start.26 = (f32[2,128,256]{2,1,0:T(8,128)S(1)}, f32[2,128,256]{2,1,0:T(8,128)S(1)}, u32[]{:S(2)}, u32[]{:S(2)}) collective-permute-start(f32[2,128,256]{2,1,0:T(8,128)S(1)} %get-tuple-element.68), channel_id=1, source_target_pairs={{4,8},{12,0},{8,4},{0,12},{5,9},{13,1},{9,5},{1,13},{6,10},{14,2},... | collective-permute-start | bytes 786440 | tf_op jit(solution)/shard_map/ppermute | solution.py:57
  121.5 2.0 %collective-permute-start.27 = (f32[2,128,512]{2,1,0:T(8,128)S(1)}, f32[2,128,512]{2,1,0:T(8,128)S(1)}, u32[]{:S(2)}, u32[]{:S(2)}) collective-permute-start(f32[2,128,512]{2,1,0:T(8,128)S(1)} %halo.3.refs_3_.refs_7_), channel_id=1, source_target_pairs={{0,16},{16,0},{1,17},{17,1},{2,18},{18,2},{3,19},{19,3},{4,20},{20... | collective-permute-start | bytes 1572872 | tf_op jit(solution)/shard_map/ppermute | solution.py:57
  131.8 1.2 collective-permute-start.28
  133.1 4.5 %collective-permute-start.31 = (f32[2]{0:T(128)S(1)}, f32[2]{0:T(128)S(1)}, u32[]{:S(2)}, u32[]{:S(2)}) collective-permute-start(f32[2]{0:T(128)S(1)} %add.27.refs_0_), channel_id=1, source_target_pairs={{0,12},{4,8},{8,4},{12,0},{1,13},{5,9},{9,5},{13,1},{2,14},{6,10},... | collective-permute-start | bytes 32 | tf_op jit(solution)/shard_map/ppermute | solution.py:462
  133.3 4.2 %collective-permute-start.30 = (f32[2]{0:T(128)S(1)}, f32[2]{0:T(128)S(1)}, u32[]{:S(2)}, u32[]{:S(2)}) collective-permute-start(f32[2]{0:T(128)S(1)} %add.27.refs_0_), channel_id=1, source_target_pairs={{0,8},{4,12},{8,0},{12,4},{1,9},{5,13},{9,1},{13,5},{2,10},{6,14},... | collective-permute-start | bytes 32 | tf_op jit(solution)/shard_map/ppermute | solution.py:462
  135.1 3.6 %collective-permute-start.29 = (f32[2]{0:T(128)S(1)}, f32[2]{0:T(128)S(1)}, u32[]{:S(2)}, u32[]{:S(2)}) collective-permute-start(f32[2]{0:T(128)S(1)} %add.27.refs_0_), channel_id=1, source_target_pairs={{0,4},{4,0},{8,12},{12,8},{1,5},{5,1},{9,13},{13,9},{2,6},{6,2},{1... | collective-permute-start | bytes 32 | tf_op jit(solution)/shard_map/ppermute | solution.py:462

commit v4 on v3

--- a/solution.py
+++ b/solution.py
@@ -10,8 +10,10 @@
 from jax.experimental.pallas import tpu as pltpu
 from jax.sharding import PartitionSpec as P
 
+
 DAMPING = 1.0
 UNROLL = 2
+BROAD = 2
 USED, PLACE_MA, SIDE, PLACE_Y, SIDE_Y = range(5)
 
 
@@ -53,10 +55,7 @@
 
 
 def swap(axis, blocks):
-    return [
-        lax.ppermute(block, axis, pairs)
-        for block, pairs in zip(blocks, pair_swaps(lax.axis_size(axis)))
-    ]
+    return [lax.ppermute(block, axis, pairs) for block, pairs in zip(blocks, pair_swaps(lax.axis_size(axis)))]
 
 
 def exchanges(count):
@@ -75,16 +74,19 @@
     return jnp.dot(left, right, preferred_element_type=jnp.float32)
 
 
-def call(body, name, out_shapes, in_spaces, operands, out_spaces=None, scratch=(), pinned=True, dtypes={}):
+def call(body, out_shapes, in_spaces, operands, out_spaces=None, scratch=(), aliases={}, dtypes={}):
     specs = [pl.BlockSpec(memory_space=space) for space in in_spaces]
     out_spaces = out_spaces or [pltpu.VMEM] * len(out_shapes)
     operands = [
-        pltpu.with_memory_space_constraint(operand, pltpu.VMEM) if pinned and space == pltpu.VMEM else operand
+        operand if space == pltpu.SMEM else pltpu.with_memory_space_constraint(operand, space)
         for operand, space in zip(operands, in_spaces)
     ]
+    return kernel_of(body, out_shapes, specs, operands, out_spaces, scratch, aliases, dtypes)
+
+
+def kernel_of(body, out_shapes, specs, operands, out_spaces, scratch, aliases, dtypes):
     return pl.pallas_call(
         body,
-        name=name,
         out_shape=[
             space(shape, dtypes.get(k, jnp.float32))
             if space == pltpu.VMEM
@@ -94,26 +96,38 @@
         in_specs=specs,
         out_specs=[pl.BlockSpec(memory_space=space or pltpu.VMEM) for space in out_spaces],
         scratch_shapes=list(scratch),
+        input_output_aliases=aliases,
         compiler_params=pltpu.CompilerParams(vmem_limit_bytes=16 * 2**20),
     )(*operands)
 
 
 class Plan:
-    def __init__(self, tile_rows, tile_cols, patch, modes, slots):
+    def __init__(self, tile_rows, tile_cols, patch, modes, slots, lead):
         self.tile_rows, self.tile_cols = tile_rows, tile_cols
         self.patch, self.modes, self.slots = patch, modes, slots
         self.rim = patch // 2
         self.rows = tile_rows + patch
         self.cols = tile_cols + patch
-
-    def scratch(self):
+        self.narrow = math.gcd(lead, UNROLL)
+        self.broad = math.gcd(modes, BROAD)
+
+    def scratch(self, width, windows=True):
         wide = self.patch
-        return [
-            pltpu.VMEM((2, self.rows, self.cols), jnp.float32),
-            pltpu.VMEM((self.slots, 2, wide, wide), jnp.float32),
-            pltpu.VMEM((UNROLL, 2, wide, wide), jnp.bfloat16),
-            pltpu.VMEM((UNROLL, 2, wide, wide), jnp.bfloat16),
-        ]
+        return (
+            [pltpu.VMEM((2, self.rows, self.cols), jnp.float32)]
+            + [pltpu.VMEM((self.slots, 2, wide, wide), jnp.float32)] * windows
+            + [pltpu.VMEM((width, 2, wide, wide), jnp.bfloat16)] * 2
+        )
+
+    def each_unit(self, count, width, body):
+        groups = count // width
+
+        def step(index, carry):
+            first = lax.rem(index, groups) * width
+            body(lax.div(index, groups), [first + j for j in range(width)])
+            return carry
+
+        lax.fori_loop(0, self.slots * groups, step, 0)
 
     def fill_region(self, region, middle, received, weights):
         rim, rows = self.rim, self.tile_rows
@@ -145,25 +159,27 @@
         turned = pltpu.roll(pltpu.roll(strip, centres[slot, 1], 1), shift, 0)
         canvas[part, pl.ds(base, self.patch + 8), :] += turned
 
-    def each_modes(self, slot, body):
+    def each_modes(self, body):
         def step(index, carry):
-            body([index * UNROLL + j for j in range(UNROLL)])
+            body([index * self.broad + j for j in range(self.broad)])
             return carry
 
-        lax.fori_loop(0, self.modes // UNROLL, step, 0)
+        lax.fori_loop(0, self.modes // self.broad, step, 0)
 
     def spectra(self, slot, modes, probes, windows, wave, half, tables):
         mid = self.rim
         low, high = slice(0, mid), slice(mid, 2 * mid)
-        for j, mode in enumerate(modes):
-            ends = []
-            for rows in (low, high):
-                p_real, p_imag = probes[mode, 0, rows], probes[mode, 1, rows]
-                x_real, x_imag = windows[slot, 0, rows], windows[slot, 1, rows]
-                ends.append((p_real * x_real - p_imag * x_imag, p_real * x_imag + p_imag * x_real))
-            for part, rows in enumerate((low, high)):
-                wave[j, 0, rows] = (ends[0][part] + ends[1][part]).astype(jnp.bfloat16)
-                wave[j, 1, rows] = (ends[0][part] - ends[1][part]).astype(jnp.bfloat16)
+        for top in range(0, mid, 16):
+            bands = [slice(top, top + 16), slice(mid + top, mid + top + 16)]
+            fields = [[windows[slot, part, band] for part in range(2)] for band in bands]
+            for j, mode in enumerate(modes):
+                ends = []
+                for band, (x_real, x_imag) in zip(bands, fields):
+                    p_real, p_imag = probes[mode, 0, band], probes[mode, 1, band]
+                    ends.append((p_real * x_real - p_imag * x_imag, p_real * x_imag + p_imag * x_real))
+                for part, band in enumerate(bands):
+                    wave[j, 0, band] = (ends[0][part] + ends[1][part]).astype(jnp.bfloat16)
+                    wave[j, 1, band] = (ends[0][part] - ends[1][part]).astype(jnp.bfloat16)
         for j in range(len(modes)):
             for k, rows in enumerate((low, high)):
                 strip = dot(tables[0][k], wave[j, k])
@@ -227,54 +243,57 @@
 
 
 def start_body(plan, swaps, grid, *refs):
-    refs = list(refs)
-    info, centres, weights, middle = refs[:4]
-    received = refs[4 : 4 + swaps]
-    shard, packed, crossed, targets, one, two = refs[4 + swaps : 10 + swaps]
-    spectra, intensity, probes, middle_out, *tail = refs[10 + swaps :]
+    columns, shards = grid
+    info, centres, _, _, windows = refs[:5]
+    packed, crossed = refs[5 : 4 + shards], refs[4 + shards : 3 + 2 * shards]
+    targets, one, two, probes, spectra, intensity, middle_out, *tail = refs[3 + 2 * shards :]
     sends = tail[:swaps]
-    region, windows, wave, half, image = tail[swaps:]
+    region, wave, half, image, weight = tail[swaps:]
     wide = plan.patch
-    columns, shards = grid
     lead = plan.modes // shards
     tables = (one, two)
     span = wide // (2 * columns)
 
-    probes[pl.ds(info[PLACE_MA] * lead, lead)] = shard[...]
     for k in range(1, shards):
         home = source_of(info[PLACE_MA], k, shards) * lead
         for c in range(columns):
             column = source_of(info[PLACE_Y], c, columns) * span
             near = pl.multiple_of(info[SIDE] * (wide // 2) + column, 8)
             far = pl.multiple_of((1 - info[SIDE]) * (wide // 2) + column, 8)
-            probes[pl.ds(home, lead), :, pl.ds(near, span), :] = packed[k - 1, c]
-            probes[pl.ds(home, lead), :, pl.ds(far, span), :] = crossed[k - 1, c]
-
-    plan.fill_region(region, middle, received, weights)
-    plan.take_windows(windows, region, centres)
+            probes[pl.ds(home, lead), :, pl.ds(near, span), :] = packed[k - 1][c]
+            probes[pl.ds(home, lead), :, pl.ds(far, span), :] = crossed[k - 1][c]
+
+    def forward(slot, modes):
+        modes = [lax.rem((info[PLACE_MA] + 1) * lead + m, plan.modes) for m in modes]
+        fields = plan.spectra(slot, modes, probes, windows, wave, half, tables)
+        for mode, field in zip(modes, fields):
+            plan.store(spectra, slot * plan.modes + mode, field)
+
+    plan.each_unit(plan.modes - lead, plan.narrow, forward)
     region[...] = jnp.zeros_like(region)
     for slot in range(plan.slots):
-        intensity[slot] = jnp.zeros((wide, wide), jnp.float32)
-
-        def forward(modes):
-            fields = plan.spectra(slot, modes, probes, windows, wave, half, tables)
+        live = jnp.where(slot < info[USED], 1.0, 0.0)
+
+        def brighten(band, carry):
+            rows = pl.ds(pl.multiple_of(band * 8, 8), 8)
             power = 0.0
-            for mode, field in zip(modes, fields):
-                plan.store(spectra, slot * plan.modes + mode, field)
-                power = power + plan.paired(field, field)
-            intensity[slot] += power
-
-        plan.each_modes(slot, forward)
-        live = jnp.where(slot < info[USED], 1.0, 0.0)
-        windows[slot, 0] = live * (intensity[slot] - targets[slot])
+            for mode in range(plan.modes):
+                field = spectra[slot * plan.modes + mode, rows]
+                pair = [field[:, :wide], field[:, wide:]]
+                power = power + plan.paired(pair, pair)
+            intensity[slot, rows] = power
+            weight[rows] = live * (power - targets[slot, rows])
+            return carry
+
+        lax.fori_loop(0, wide // 8, brighten, 0, unroll=4)
         image[...] = jnp.zeros_like(image)
 
         def backward(modes):
             fields = [plan.load(spectra, slot * plan.modes + mode) for mode in modes]
-            sums = plan.images(fields, windows[slot, 0], modes, probes, wave, half, tables)
+            sums = plan.images(fields, weight[...], modes, probes, wave, half, tables)
             plan.add_images(image, sums)
 
-        plan.each_modes(slot, backward)
+        plan.each_modes(backward)
         for part in range(2):
             plan.place(region, slot, part, image[part], centres)
     plan.send(region, info[SIDE], middle_out, sends)
@@ -314,7 +333,7 @@
             if not last:
                 power[slot] += square
 
-        plan.each_modes(slot, forward)
+        plan.each_modes(forward)
         live = jnp.where(slot < info[USED], 1.0, 0.0)
         bend = bend + live * jnp.sum(change[slot] * change[slot])
     sums[1] = bend
@@ -348,7 +367,7 @@
             sums = plan.images(fields, windows[slot, 0], modes, probes, wave, half, tables)
             plan.add_images(image, sums)
 
-        plan.each_modes(slot, backward)
+        plan.each_modes(backward)
         for part in range(2):
             plan.place(region, slot, part, image[part], centres)
     plan.send(region, info[SIDE], middle_out, sends)
@@ -364,18 +383,48 @@
 
 
 def pack_body(plan, swaps, columns, *refs):
-    info, shard, tile, mine, *rims = refs
+    info, shard, tile, mine, *rims = refs[: 4 + swaps]
+    sems = refs[4 + swaps]
     span = plan.patch // (2 * columns)
     start = pl.multiple_of(info[SIDE] * (plan.patch // 2) + info[PLACE_Y] * span, 8)
-    mine[...] = shard[:, :, pl.ds(start, span), :]
-    low, high = tile[:, :, : plan.rim], tile[:, :, plan.tile_cols - plan.rim :]
+    copies = [pltpu.make_async_copy(shard.at[:, :, pl.ds(start, span), :], mine, sems.at[0])]
     for k, rim in enumerate(rims):
-        rim[...] = jnp.where((info[SIDE_Y] == 0) == (k == 0), high, low)
-
-
-def stage_body(plan, *refs):
-    targets, one, two, shard, _, ordered, *copies = refs
-    wide = plan.patch
+        first = jnp.where((info[SIDE_Y] == 0) == (k == 0), plan.tile_cols - plan.rim, 0)
+        first = pl.multiple_of(first, 128)
+        source = tile.at[:, :, pl.ds(first, plan.rim)]
+        copies.append(pltpu.make_async_copy(source, rim, sems.at[1 + k]))
+    for copy in copies:
+        copy.start()
+    for copy in copies:
+        copy.wait()
+
+
+def early_body(plan, swaps, shards, *refs):
+    info, centres, weights, middle = refs[:4]
+    received = refs[4 : 4 + swaps]
+    far_targets, far_one, far_two, far_shard = refs[4 + swaps : 8 + swaps]
+    probes, spectra, windows, ordered, one, two = refs[8 + swaps : 14 + swaps]
+    region, wave, half, sems = refs[14 + swaps :]
+    wide, lead = plan.patch, plan.modes // shards
+    home = info[PLACE_MA] * lead
+    copies = [
+        pltpu.make_async_copy(source, target, sems.at[k])
+        for k, (source, target) in enumerate(
+            (
+                (far_one, one),
+                (far_two, two),
+                (far_targets, ordered),
+                (far_shard, probes.at[pl.ds(home, lead)]),
+            )
+        )
+    ]
+    for copy in copies:
+        copy.start()
+    plan.fill_region(region, middle, received, weights)
+    plan.take_windows(windows, region, centres)
+    for copy in copies:
+        copy.wait()
+
     place = lax.broadcasted_iota(jnp.int32, (wide, wide), 0)
     source = jnp.where(place < plan.rim, 2 * place, 2 * (place - plan.rim) + 1)
     pick = jnp.where(source == lax.broadcasted_iota(jnp.int32, (wide, wide), 1), 1.0, 0.0)
@@ -389,27 +438,33 @@
         return parts
 
     for slot in range(plan.slots):
-        rows = sum(dot(pick, part) for part in parts_of(targets[slot]))
+        rows = sum(dot(pick, part) for part in parts_of(ordered[slot]))
         ordered[slot] = sum(
             lax.dot_general(part, pick, (((1,), (1,)), ((), ())), preferred_element_type=jnp.float32)
             for part in parts_of(rows)
         )
-    for source, copy in zip((one, two, shard), copies):
-        copy[...] = source[...]
-
-
-def join_body(plan, swaps, columns, shards, *refs):
+
+    def forward(slot, modes):
+        fields = plan.spectra(slot, modes, probes, windows, wave, half, (one, two))
+        for mode, field in zip(modes, fields):
+            plan.store(spectra, slot * plan.modes + mode, field)
+
+    plan.each_unit(lead, plan.narrow, lambda slot, modes: forward(slot, [home + m for m in modes]))
+
+
+def widen_body(plan, swaps, *refs):
     weights, tile = refs[:2]
     received = refs[2 : 2 + swaps]
-    parts = refs[2 + swaps : -2]
-    middle, packed = refs[-2:]
+    middle = refs[2 + swaps]
     low, high = sides_of(received, weights)
     middle[:, :, : plan.rim] = low
     middle[:, :, plan.rim : plan.rim + plan.tile_cols] = tile[...]
     middle[:, :, plan.rim + plan.tile_cols :] = high
-    for k in range(shards - 1):
-        for c in range(columns):
-            packed[k, c] = parts[k * columns + c][...]
+
+
+def join_body(*refs):
+    for c, part in enumerate(refs[:-2]):
+        refs[-1][c] = part[...]
 
 
 def sides_of(received, weights):
@@ -469,7 +524,7 @@
     lead = probe_shard.shape[0]
     modes = lead * groups
     slots = measured.shape[2]
-    plan = Plan(tile_rows, tile_cols, patch, modes, slots)
+    plan = Plan(tile_rows, tile_cols, patch, modes, slots, lead)
     rim, units = plan.rim, slots * modes
     one, two = (jnp.asarray(table) for table in dft_tables(patch))
     targets = measured[0, 0]
@@ -499,95 +554,96 @@
     def descent(middle, sends):
         merged, *blocks = call(
             functools.partial(fold_body, plan, swaps_x),
-            "fold",
             [tall] + [(2, tile_rows, patch)] * swaps_y,
             [smem] * 2 + [vmem] * (1 + swaps_x),
             [info, weights_x, middle, *swap("gx", sends)],
         )
         (middle,) = call(
             functools.partial(halo_body, plan, swaps_y),
-            "halo",
             [tall],
             [smem] * 2 + [vmem] * (1 + swaps_y),
             [weights_y, inside, merged, *swap("gy", blocks)],
         )
         return middle
 
+    hbm, dma = pltpu.HBM, pltpu.SemaphoreType.DMA
     mine, *rims = call(
         functools.partial(pack_body, plan, swaps_y, columns),
-        "pack",
         [(lead, 2, span, patch)] + [(2, tile_rows, rim)] * swaps_y,
-        [smem] + [vmem] * 2,
+        [smem] + [hbm] * 2,
         [info, probe_shard, object_field],
-        pinned=False,
-    )
-    targets, one, two, own_shard = call(
-        functools.partial(stage_body, plan),
-        "stage",
-        [targets.shape, one.shape, two.shape, probe_shard.shape],
-        [vmem] * 4 + [pl.ANY],
-        [targets, one, two, probe_shard, mine],
-        pinned=False,
-        dtypes={1: jnp.bfloat16, 2: jnp.bfloat16},
+        scratch=[dma((1 + swaps_y,))],
     )
     parts = []
     for pairs in exchanges(groups):
         block = lax.ppermute(mine, "ma", pairs)
-        parts += [block] + [lax.ppermute(block, "gy", others) for others in exchanges(columns)]
-    middle, packed = call(
-        functools.partial(join_body, plan, swaps_y, columns, groups),
-        "join",
-        [tall, (groups - 1, columns, lead, 2, span, patch)],
-        [smem] + [vmem] * (1 + swaps_y + len(parts)),
-        [weights_y, object_field, *swap("gy", rims), *parts],
-    )
-    (crossed,) = swap("gx", [packed])[:1]
-
-    spectra, intensity, probes, middle, *sends = call(
+        across = [lax.ppermute(block, "gy", p) for p in exchanges(columns)]
+        parts.append([block, *across])
+    (middle,) = call(
+        functools.partial(widen_body, plan, swaps_y),
+        [tall],
+        [smem, vmem] + [vmem] * swaps_y,
+        [weights_y, object_field, *swap("gy", rims)],
+    )
+    probes, spectra, windows, targets, one, two = call(
+        functools.partial(early_body, plan, swaps_x, groups),
+        [
+            (modes, 2, patch, patch),
+            (units, patch, 2 * patch),
+            (slots, 2, patch, patch),
+            targets.shape,
+            one.shape,
+            two.shape,
+        ],
+        [smem] * 3 + [vmem] * (1 + swaps_x) + [hbm] * 4,
+        [info, centres, weights_x, middle, *rows_around(middle), targets, one, two, probe_shard],
+        scratch=plan.scratch(plan.narrow, False) + [dma((4,))],
+        dtypes={4: jnp.bfloat16, 5: jnp.bfloat16},
+    )
+    packed, crossed = [], []
+    for blocks in parts:
+        packed += call(join_body, [(columns, lead, 2, span, patch)], [vmem] * (columns + 1), [*blocks, windows])
+        crossed += swap("gx", packed[-1:])
+    probes, spectra, intensity, middle, *sends = call(
         functools.partial(start_body, plan, swaps_x, (columns, groups)),
-        "start",
-        [(units, patch, 2 * patch), (slots, patch, patch), (modes, 2, patch, patch), tall]
-        + [fold] * swaps_x,
-        [smem] * 3 + [vmem] * (7 + swaps_x),
-        [info, centres, weights_x, middle, *rows_around(middle), own_shard, packed, crossed]
-        + [targets, one, two],
-        scratch=plan.scratch() + [image_scratch],
+        [probes.shape, spectra.shape, (slots, patch, patch), tall] + [fold] * swaps_x,
+        [smem] * 2 + [vmem] * (6 + 2 * (groups - 1)),
+        [info, centres, probes, spectra, windows, *packed, *crossed, targets, one, two],
+        scratch=plan.scratch(max(plan.broad, plan.narrow), False)
+        + [image_scratch, pltpu.VMEM((patch, patch), jnp.float32)],
+        aliases={2: 0, 3: 1},
     )
     first_way = descent(middle, sends)
     sums, moved, change, power = call(
         functools.partial(change_body, plan, swaps_x, False),
-        "change",
         [(2,), (units, patch, 2 * patch), (slots, patch, patch), (slots, patch, patch)],
         [smem] * 3 + [vmem] * (5 + swaps_x),
         [info, centres, weights_x, first_way, *rows_around(first_way), spectra, probes, one, two],
         [smem] + [vmem] * 3,
-        scratch=plan.scratch(),
+        scratch=plan.scratch(plan.broad),
     )
     totals = totals_of(sums)
     spectra, first_step, middle, *sends = call(
         functools.partial(image_body, plan, swaps_x, len(totals)),
-        "image",
         [(units, patch, 2 * patch), (1,), tall] + [fold] * swaps_x,
         [smem] * (2 + len(totals)) + [vmem] * 9,
         [info, centres, *totals, spectra, moved, intensity, change, power, probes, targets, one, two],
         [vmem, smem] + [vmem] * (1 + swaps_x),
-        scratch=plan.scratch() + [image_scratch],
+        scratch=plan.scratch(plan.broad) + [image_scratch],
     )
     last_way = descent(middle, sends)
     (sums,) = call(
         functools.partial(change_body, plan, swaps_x, True),
-        "last_change",
         [(2,)],
         [smem] * 3 + [vmem] * (5 + swaps_x),
         [info, centres, weights_x, last_way, *rows_around(last_way), spectra, probes, one, two],
         [smem],
-        scratch=plan.scratch()
+        scratch=plan.scratch(plan.broad)
         + [pltpu.VMEM((slots, patch, patch), jnp.float32), pltpu.VMEM((1, 8, 128), jnp.float32)],
     )
     totals = totals_of(sums)
     (current,) = call(
         functools.partial(finish_body, plan, len(totals)),
-        "finish",
         [(2, tile_rows, tile_cols)],
         [smem] * (len(totals) + 1) + [vmem] * 3,
         [*totals, first_step, object_field, first_way, last_way],

time: 141 us -> 145 us (1.028)
  waiting for transfers between devices: 48.3 us -> 58 us
  local copies, waits for them, and re-layouts: 8.06 us -> 1.72 us
  Pallas kernels: 48.1 us -> 51.3 us
  starting transfers between devices: 35.2 us -> 32.6 us
    unnamed x20 -> x8, local copies, waits for them, and re-layouts: 7.97 us -> 1.64 us
    ppermute x14 -> x16, waiting for transfers between devices: 35.8 us -> 42 us  [swap(): lax.ppermute(block, axis, pairs)]
    ppermute x3, waiting for transfers between devices: 0.01 us -> 5.95 us  [shards(): block = lax.ppermute(mine, 'ma', pairs)]
    pallas_call x12 -> x15, Pallas kernels: 48.1 us -> 51.3 us  [kernel_of(): pl.pallas_call(body, out_shape=[space(shape, dtypes.get(k, jnp.float32))...]
    ppermute x9, starting transfers between devices: 13.2 us -> 10.2 us  [shards(): across = [lax.ppermute(block, 'gy', p) for p in exchanges(columns)]]
    ppermute x9, waiting for transfers between devices: 7.09 us -> 4.66 us  [shards(): across = [lax.ppermute(block, 'gy', p) for p in exchanges(columns)]]
    ppermute x14 -> x16, starting transfers between devices: 9.09 us -> 11 us  [swap(): lax.ppermute(block, axis, pairs)]
    ppermute x3, starting transfers between devices: 5.93 us -> 4.45 us  [shards(): block = lax.ppermute(mine, 'ma', pairs)]
  transfers between devices with their start and end apart: 32 -> 34, of which waited for: 21 -> 24; matrix products, arithmetic and copies ran while one was open for 0% -> 0% of each run, Pallas kernels for 1% -> 4%
where the time goes in v4:
time: 145 us
  waiting for transfers between devices  58 us (40%)
  Pallas kernels  51.3 us (35%)
  starting transfers between devices  32.6 us (22%)
  local copies, waits for them, and re-layouts  1.72 us (1%)
    pallas_call x15, Pallas kernels, kernel_of(): pl.pallas_call(body, out_shape=[space(shape, dtypes.get(k, jnp.float32))...  51.3 us
    ppermute x16, waiting for transfers between devices, swap(): lax.ppermute(block, axis, pairs)  42 us
    ppermute x16, starting transfers between devices, swap(): lax.ppermute(block, axis, pairs)  11 us
    ppermute x9, starting transfers between devices, shards(): across = [lax.ppermute(block, 'gy', p) for p in exchanges(columns)]  10.2 us
    ppermute x6, starting transfers between devices, totals_of(): lax.ppermute(sums, 'gy', pairs)  6.98 us
    ppermute x3, waiting for transfers between devices, shards(): block = lax.ppermute(mine, 'ma', pairs)  5.95 us
    ppermute x6, waiting for transfers between devices, totals_of(): lax.ppermute(sums, 'gy', pairs)  5.34 us
    ppermute x9, waiting for transfers between devices, shards(): across = [lax.ppermute(block, 'gy', p) for p in exchanges(columns)]  4.66 us
  transfers between devices with their start and end apart: 34, of which 24 were waited for; matrix products, arithmetic and copies ran while one was open for 0% of the time, Pallas kernels for 4%

profile of v4, /device:TPU:0, one launch (start us, length us, event | category | flops | bytes accessed | tf_op | source)
XLA Modules:
  0.0 144.7 jit_solution(15161022069904868683)
XLA Ops:
  0.9 1.6 %shard_map.73 = (f32[2,2,32,256]{3,2,1,0:T(8,128)S(1)}, f32[2,128,128]{2,1,0:T(8,128)S(1)}, f32[2,128,128]{2,1,0:T(8,128)S(1)}) custom-call(s32[5]{0:T(128)S(1)} %stack.52.refs_0_, f32[2,2,256,256]{3,2,1,0:T(8,128)} %refs_8_.1, f32[2,128,256]{2,1,0:T(8,128)} %refs_5_.1), custom_call_target="tpu_custom_call" | custom-call | tf_op jit(solution)/shard_map/pallas_call | solution.py:88
  2.5 3.0 %collective-permute-start = (f32[2,128,128]{2,1,0:T(8,128)S(1)}, f32[2,128,128]{2,1,0:T(8,128)S(1)}, u32[]{:S(2)}, u32[]{:S(2)}) collective-permute-start(f32[2,128,128]{2,1,0:T(8,128)S(1)} %get-tuple-element.43), channel_id=1, source_target_pairs={{0,4},{4,0},{8,12},{12,8},{1,5},{5,1},{9,13},{13,9},{2,6},{6,2},{1... | collective-permute-start | bytes 393224 | tf_op jit(solution)/shard_map/ppermute | solution.py:58
  5.5 1.5 %collective-permute-start.1 = (f32[2,128,128]{2,1,0:T(8,128)S(1)}, f32[2,128,128]{2,1,0:T(8,128)S(1)}, u32[]{:S(2)}, u32[]{:S(2)}) collective-permute-start(f32[2,128,128]{2,1,0:T(8,128)S(1)} %get-tuple-element.44), channel_id=1, source_target_pairs={{4,8},{12,0},{8,4},{0,12},{5,9},{13,1},{9,5},{1,13},{6,10},{14,2},... | collective-permute-start | bytes 393224 | tf_op jit(solution)/shard_map/ppermute | solution.py:58
  7.0 2.4 %collective-permute-done.refs_2_ = f32[2,128,128]{2,1,0:T(8,128)S(1)} collective-permute-done((f32[2,128,128]{2,1,0:T(8,128)S(1)}, f32[2,128,128]{2,1,0:T(8,128)S(1)}, u32[]{:S(2)}, u32[]{:S(2)}) %collective-permute-start) | collective-permute-done | bytes 131104 | tf_op jit(solution)/shard_map/ppermute | solution.py:58
  9.4 3.6 %collective-permute-done.1.refs_3_ = f32[2,128,128]{2,1,0:T(8,128)S(1)} collective-permute-done((f32[2,128,128]{2,1,0:T(8,128)S(1)}, f32[2,128,128]{2,1,0:T(8,128)S(1)}, u32[]{:S(2)}, u32[]{:S(2)}) %collective-permute-start.1) | collective-permute-done | bytes 131104 | tf_op jit(solution)/shard_map/ppermute | solution.py:58
  13.1 0.9 copy-done
  14.7 2.7 %collective-permute-start.7 = (f32[2,2,32,256]{3,2,1,0:T(8,128)S(1)}, f32[2,2,32,256]{3,2,1,0:T(8,128)S(1)}, u32[]{:S(2)}, u32[]{:S(2)}) collective-permute-start(f32[2,2,32,256]{3,2,1,0:T(8,128)S(1)} %get-tuple-element.48), channel_id=1, source_target_pairs={{0,2},{1,3},{2,0},{3,1},{4,6},{5,7},{6,4},{7,5},{8,10},{9,11},{10,... | collective-permute-start | bytes 393224 | tf_op jit(solution)/shard_map/ppermute | solution.py:579
  17.3 1.6 %collective-permute-start.3 = (f32[2,2,32,256]{3,2,1,0:T(8,128)S(1)}, f32[2,2,32,256]{3,2,1,0:T(8,128)S(1)}, u32[]{:S(2)}, u32[]{:S(2)}) collective-permute-start(f32[2,2,32,256]{3,2,1,0:T(8,128)S(1)} %get-tuple-element.48), channel_id=1, source_target_pairs={{0,1},{1,0},{2,3},{3,2},{4,5},{5,4},{6,7},{7,6},{8,9},{9,8},{10,11... | collective-permute-start | bytes 393224 | tf_op jit(solution)/shard_map/ppermute | solution.py:579
  19.1 5.7 %collective-permute-done.7.refs_0_ = f32[2,2,32,256]{3,2,1,0:T(8,128)S(1)} collective-permute-done((f32[2,2,32,256]{3,2,1,0:T(8,128)S(1)}, f32[2,2,32,256]{3,2,1,0:T(8,128)S(1)}, u32[]{:S(2)}, u32[]{:S(2)}) %collective-permute-start.7) | collective-permute-done | bytes 131104 | tf_op jit(solution)/shard_map/ppermute | solution.py:579
  24.8 1.4 collective-permute-start.10
  26.3 1.5 %collective-permute-start.6 = (f32[2,2,32,256]{3,2,1,0:T(8,128)S(1)}, f32[2,2,32,256]{3,2,1,0:T(8,128)S(1)}, u32[]{:S(2)}, u32[]{:S(2)}) collective-permute-start(f32[2,2,32,256]{3,2,1,0:T(8,128)S(1)} %collective-permute-done.3.refs_0_), channel_id=1, source_target_pairs={{0,12},{4,8},{8,4},{12,0},{1,13},{5,9},{9,5},{13,1},{2,14},{6,10},... | collective-permute-start | bytes 393224 | tf_op jit(solution)/shard_map/ppermute | solution.py:580
  28.2 1.5 %collective-permute-start.4 = (f32[2,2,32,256]{3,2,1,0:T(8,128)S(1)}, f32[2,2,32,256]{3,2,1,0:T(8,128)S(1)}, u32[]{:S(2)}, u32[]{:S(2)}) collective-permute-start(f32[2,2,32,256]{3,2,1,0:T(8,128)S(1)} %collective-permute-done.3.refs_0_), channel_id=1, source_target_pairs={{0,4},{4,0},{8,12},{12,8},{1,5},{5,1},{9,13},{13,9},{2,6},{6,2},{1... | collective-permute-start | bytes 393224 | tf_op jit(solution)/shard_map/ppermute | solution.py:580
  29.8 2.4 %collective-permute-done.10.refs_3_ = f32[2,2,32,256]{3,2,1,0:T(8,128)S(1)} collective-permute-done((f32[2,2,32,256]{3,2,1,0:T(8,128)S(1)}, f32[2,2,32,256]{3,2,1,0:T(8,128)S(1)}, u32[]{:S(2)}, u32[]{:S(2)}) %collective-permute-start.10) | collective-permute-done | bytes 131104 | tf_op jit(solution)/shard_map/ppermute | solution.py:580
  32.1 2.3 %collective-permute-done.6.refs_3_ = f32[2,2,32,256]{3,2,1,0:T(8,128)S(1)} collective-permute-done((f32[2,2,32,256]{3,2,1,0:T(8,128)S(1)}, f32[2,2,32,256]{3,2,1,0:T(8,128)S(1)}, u32[]{:S(2)}, u32[]{:S(2)}) %collective-permute-start.6) | collective-permute-done | bytes 131104 | tf_op jit(solution)/shard_map/ppermute | solution.py:580
  34.4 2.0 %collective-permute-start.8 = (f32[2,2,32,256]{3,2,1,0:T(8,128)S(1)}, f32[2,2,32,256]{3,2,1,0:T(8,128)S(1)}, u32[]{:S(2)}, u32[]{:S(2)}) collective-permute-start(f32[2,2,32,256]{3,2,1,0:T(8,128)S(1)} %collective-permute-done.7.refs_0_), channel_id=1, source_target_pairs={{0,4},{4,0},{8,12},{12,8},{1,5},{5,1},{9,13},{13,9},{2,6},{6,2},{1... | collective-permute-start | bytes 393224 | tf_op jit(solution)/shard_map/ppermute | solution.py:580
  36.5 0.8 collective-permute-start.14
  37.3 1.6 %collective-permute-start.13 = (f32[2,2,32,256]{3,2,1,0:T(8,128)S(1)}, f32[2,2,32,256]{3,2,1,0:T(8,128)S(1)}, u32[]{:S(2)}, u32[]{:S(2)}) collective-permute-start(f32[2,2,32,256]{3,2,1,0:T(8,128)S(1)} %collective-permute-done.11.refs_0_), channel_id=1, source_target_pairs={{0,8},{4,12},{8,0},{12,4},{1,9},{5,13},{9,1},{13,5},{2,10},{6,14},... | collective-permute-start | bytes 393224 | tf_op jit(solution)/shard_map/ppermute | solution.py:580
  38.9 1.0 collective-permute-start.12
  40.6 5.3 %shard_map.75 = (f32[8,2,256,256]{3,2,1,0:T(8,128)S(1)}, f32[16,256,512]{2,1,0:T(8,128)S(1)}, f32[2,2,256,256]{3,2,1,0:T(8,128)S(1)}, f32[2,256,256]{2,1,0:T(8,1...) custom-call(s32[5]{0:T(128)S(1)} %stack.52.refs_0_, s32[2,2]{1,0:T(2,128)S(1)} %bitcast.16, ...), custom_call_target="tpu_custom_call" | custom-call | tf_op jit(solution)/shard_map/pallas_call | solution.py:88
  46.8 1.1 collective-permute-done.15.refs_8_
  49.4 13.2 %shard_map.79 = (f32[8,2,256,256]{3,2,1,0:T(8,128)S(1)}, f32[16,256,512]{2,1,0:T(8,128)S(1)}, f32[2,256,256]{2,1,0:T(8,128)S(1)}, f32[2,128,512]{2,1,0:T(8,128)S(1)}, f32[2,128,512]{2,1,0:T(8,128)S(1)}) custom-call(s32[5]{0:T(128)S(1)} %stack.52.refs_0_, s32[2,2]{1,0:T(2,128)S(1)} %bitcast.17, ...), custom_call_target="tpu_custom_call", output_to_operand_aliasing={{0}: (2, {}), {1}: (3, {})} | custom-call | tf_op jit(solution)/shard_map/pallas_call | solution.py:88
  62.9 1.8 %collective-permute-done.18.refs_3_ = f32[2,128,512]{2,1,0:T(8,128)S(1)} collective-permute-done((f32[2,128,512]{2,1,0:T(8,128)S(1)}, f32[2,128,512]{2,1,0:T(8,128)S(1)}, u32[]{:S(2)}, u32[]{:S(2)}) %collective-permute-start.18) | collective-permute-done | bytes 524320 | tf_op jit(solution)/shard_map/ppermute | solution.py:58
  64.6 0.8 shard_map.80
  65.4 1.0 collective-permute-start.19
  67.1 7.5 %collective-permute-done.19.refs_3_ = f32[2,128,256]{2,1,0:T(8,128)S(1)} collective-permute-done((f32[2,128,256]{2,1,0:T(8,128)S(1)}, f32[2,128,256]{2,1,0:T(8,128)S(1)}, u32[]{:S(2)}, u32[]{:S(2)}) %collective-permute-start.19) | collective-permute-done | bytes 262176 | tf_op jit(solution)/shard_map/ppermute | solution.py:58
  74.7 4.4 %collective-permute-done.20.refs_4_ = f32[2,128,256]{2,1,0:T(8,128)S(1)} collective-permute-done((f32[2,128,256]{2,1,0:T(8,128)S(1)}, f32[2,128,256]{2,1,0:T(8,128)S(1)}, u32[]{:S(2)}, u32[]{:S(2)}) %collective-permute-start.20) | collective-permute-done | bytes 262176 | tf_op jit(solution)/shard_map/ppermute | solution.py:58
  79.9 1.9 %collective-permute-done.21.refs_4_ = f32[2,128,512]{2,1,0:T(8,128)S(1)} collective-permute-done((f32[2,128,512]{2,1,0:T(8,128)S(1)}, f32[2,128,512]{2,1,0:T(8,128)S(1)}, u32[]{:S(2)}, u32[]{:S(2)}) %collective-permute-start.21) | collective-permute-done | bytes 524320 | tf_op jit(solution)/shard_map/ppermute | solution.py:58
  81.8 8.6 %shard_map.82 = (f32[2]{0:T(128)S(1)}, f32[16,256,512]{2,1,0:T(8,128)S(1)}, f32[2,256,256]{2,1,0:T(8,128)S(1)}, f32[2,256,256]{2,1,0:T(8,128)S(1)}) custom-call(s32[5]{0:T(128)S(1)} %stack.52.refs_0_, s32[2,2]{1,0:T(2,128)S(1)} %bitcast.18, f32[2]{0:T(128)S(1)} %get-tuple-element.40.refs_2_.refs_1_, f32[2,128,512]{2,1,0:T(8,128)S(1)} %shard_map.81.refs_3_.refs_6_, ...), custom_call_target="tpu_custom_call" | custom-call | tf_op jit(solution)/shard_map/pallas_call | solution.py:88
  90.6 1.0 collective-permute-done.22
  91.7 2.2 %collective-permute-start.25 = (f32[2]{0:T(128)S(1)}, f32[2]{0:T(128)S(1)}, u32[]{:S(2)}, u32[]{:S(2)}) collective-permute-start(f32[2]{0:T(128)S(1)} %add.26.refs_2_), channel_id=1, source_target_pairs={{0,12},{4,8},{8,4},{12,0},{1,13},{5,9},{9,5},{13,1},{2,14},{6,10},... | collective-permute-start | bytes 32 | tf_op jit(solution)/shard_map/ppermute | solution.py:517
  94.3 0.8 collective-permute-start.23
  95.2 1.0 collective-permute-done.25.refs_5_
  96.1 1.4 collective-permute-done.24.refs_4_
  97.9 8.6 %shard_map.83 = (f32[16,256,512]{2,1,0:T(8,128)S(1)}, f32[1]{0:T(128)}, f32[2,128,512]{2,1,0:T(8,128)S(1)}, f32[2,128,512]{2,1,0:T(8,128)S(1)}) custom-call(s32[5]{0:T(128)S(1)} %stack.52.refs_0_, s32[2,2]{1,0:T(2,128)S(1)} %bitcast.19, f32[2]{0:T(128)S(1)} %add.26.refs_2_, f32[2]{0:T(128)S(1)} %collective-permute-done.23.refs_3_, ...), custom_call_target="tpu_custom_call" | custom-call | tf_op jit(solution)/shard_map/pallas_call | solution.py:88
  106.6 1.9 %collective-permute-done.26.refs_3_ = f32[2,128,512]{2,1,0:T(8,128)S(1)} collective-permute-done((f32[2,128,512]{2,1,0:T(8,128)S(1)}, f32[2,128,512]{2,1,0:T(8,128)S(1)}, u32[]{:S(2)}, u32[]{:S(2)}) %collective-permute-start.26) | collective-permute-done | bytes 524320 | tf_op jit(solution)/shard_map/ppermute | solution.py:58
  108.5 0.8 shard_map.84
  109.3 0.9 collective-permute-start.27
  110.2 2.2 %collective-permute-start.28 = (f32[2,128,256]{2,1,0:T(8,128)S(1)}, f32[2,128,256]{2,1,0:T(8,128)S(1)}, u32[]{:S(2)}, u32[]{:S(2)}) collective-permute-start(f32[2,128,256]{2,1,0:T(8,128)S(1)} %get-tuple-element.68), channel_id=1, source_target_pairs={{4,8},{12,0},{8,4},{0,12},{5,9},{13,1},{9,5},{1,13},{6,10},{14,2},... | collective-permute-start | bytes 786440 | tf_op jit(solution)/shard_map/ppermute | solution.py:58
  112.4 6.1 %collective-permute-done.27.refs_3_ = f32[2,128,256]{2,1,0:T(8,128)S(1)} collective-permute-done((f32[2,128,256]{2,1,0:T(8,128)S(1)}, f32[2,128,256]{2,1,0:T(8,128)S(1)}, u32[]{:S(2)}, u32[]{:S(2)}) %collective-permute-start.27) | collective-permute-done | bytes 262176 | tf_op jit(solution)/shard_map/ppermute | solution.py:58
  118.5 5.8 %collective-permute-done.28.refs_4_ = f32[2,128,256]{2,1,0:T(8,128)S(1)} collective-permute-done((f32[2,128,256]{2,1,0:T(8,128)S(1)}, f32[2,128,256]{2,1,0:T(8,128)S(1)}, u32[]{:S(2)}, u32[]{:S(2)}) %collective-permute-start.28) | collective-permute-done | bytes 262176 | tf_op jit(solution)/shard_map/ppermute | solution.py:58
  125.2 1.9 %collective-permute-done.29.refs_4_ = f32[2,128,512]{2,1,0:T(8,128)S(1)} collective-permute-done((f32[2,128,512]{2,1,0:T(8,128)S(1)}, f32[2,128,512]{2,1,0:T(8,128)S(1)}, u32[]{:S(2)}, u32[]{:S(2)}) %collective-permute-start.29) | collective-permute-done | bytes 524320 | tf_op jit(solution)/shard_map/ppermute | solution.py:58
  127.1 8.2 %shard_map.86 = f32[2]{0:T(128)S(1)} custom-call(s32[5]{0:T(128)S(1)} %stack.52.refs_0_, s32[2,2]{1,0:T(2,128)S(1)} %bitcast.20, f32[2]{0:T(128)S(1)} %get-tuple-element.40.refs_2_.refs_1_, f32[2,128,512]{2,1,0:T(8,128)S(1)} %shard_map.85.refs_3_.refs_7_, f32[2,128,512]{2,1,0:T(8,128)S(1)} %collective-permute-done.29.refs_4_, ...), custom_call_target="tpu_custom_call" | custom-call | tf_op jit(solution)/shard_map/pallas_call | solution.py:88
  135.6 1.0 collective-permute-done.30
  137.3 1.8 %collective-permute-start.32 = (f32[2]{0:T(128)S(1)}, f32[2]{0:T(128)S(1)}, u32[]{:S(2)}, u32[]{:S(2)}) collective-permute-start(f32[2]{0:T(128)S(1)} %add.27.refs_0_), channel_id=1, source_target_pairs={{0,8},{4,12},{8,0},{12,4},{1,9},{5,13},{9,1},{13,5},{2,10},{6,14},... | collective-permute-start | bytes 32 | tf_op jit(solution)/shard_map/ppermute | solution.py:517
  139.1 1.0 collective-permute-start.31
  140.1 1.0 collective-permute-done.33.refs_3_
  141.1 1.6 %collective-permute-done.31.refs_1_ = f32[2]{0:T(128)S(1)} collective-permute-done((f32[2]{0:T(128)S(1)}, f32[2]{0:T(128)S(1)}, u32[]{:S(2)}, u32[]{:S(2)}) %collective-permute-start.31) | collective-permute-done | bytes 40 | tf_op jit(solution)/shard_map/ppermute | solution.py:517
  142.7 2.0 %shard_map.87 = f32[2,128,256]{2,1,0:T(8,128)} custom-call(f32[2]{0:T(128)S(1)} %add.27.refs_0_, f32[2]{0:T(128)S(1)} %collective-permute-done.31.refs_1_, f32[2]{0:T(128)S(1)} %collective-permute-done.32.refs_2_, f32[2]{0:T(128)S(1)} %collective-permute-done.33.refs_3_, f32[1]{0:T(128)} %get-tuple-element.70.refs_4_, f32[2,128,256]{2,1,0:T(8,128)S(1)} %copy-done.1, ...), custom_call_target="tpu_custom_call" | custom-call | tf_op jit(solution)/shard_map/pallas_call | solution.py:88
  (48 shorter events, 9.2 us)
Async XLA Ops:
  2.5 6.9 %collective-permute-start = (f32[2,128,128]{2,1,0:T(8,128)S(1)}, f32[2,128,128]{2,1,0:T(8,128)S(1)}, u32[]{:S(2)}, u32[]{:S(2)}) collective-permute-start(f32[2,128,128]{2,1,0:T(8,128)S(1)} %get-tuple-element.43), channel_id=1, source_target_pairs={{0,4},{4,0},{8,12},{12,8},{1,5},{5,1},{9,13},{13,9},{2,6},{6,2},{1... | collective-permute-start | bytes 393224 | tf_op jit(solution)/shard_map/ppermute | solution.py:58
  5.5 7.5 %collective-permute-start.1 = (f32[2,128,128]{2,1,0:T(8,128)S(1)}, f32[2,128,128]{2,1,0:T(8,128)S(1)}, u32[]{:S(2)}, u32[]{:S(2)}) collective-permute-start(f32[2,128,128]{2,1,0:T(8,128)S(1)} %get-tuple-element.44), channel_id=1, source_target_pairs={{4,8},{12,0},{8,4},{0,12},{5,9},{13,1},{9,5},{1,13},{6,10},{14,2},... | collective-permute-start | bytes 393224 | tf_op jit(solution)/shard_map/ppermute | solution.py:58
  13.1 1.0 copy-start
  14.6 24.3 %collective-permute-start.2 = (f32[2,128,512]{2,1,0:T(8,128)S(1)}, f32[2,128,512]{2,1,0:T(8,128)S(1)}, u32[]{:S(2)}, u32[]{:S(2)}) collective-permute-start(f32[2,128,512]{2,1,0:T(8,128)S(1)} %shard_map.74.refs_3_), channel_id=1, source_target_pairs={{0,16},{16,0},{1,17},{17,1},{2,18},{18,2},{3,19},{19,3},{4,20},{20... | collective-permute-start | bytes 1572872 | tf_op jit(solution)/shard_map/ppermute | solution.py:58
  14.7 10.2 %collective-permute-start.7 = (f32[2,2,32,256]{3,2,1,0:T(8,128)S(1)}, f32[2,2,32,256]{3,2,1,0:T(8,128)S(1)}, u32[]{:S(2)}, u32[]{:S(2)}) collective-permute-start(f32[2,2,32,256]{3,2,1,0:T(8,128)S(1)} %get-tuple-element.48), channel_id=1, source_target_pairs={{0,2},{1,3},{2,0},{3,1},{4,6},{5,7},{6,4},{7,5},{8,10},{9,11},{10,... | collective-permute-start | bytes 393224 | tf_op jit(solution)/shard_map/ppermute | solution.py:579
  17.3 8.9 %collective-permute-start.3 = (f32[2,2,32,256]{3,2,1,0:T(8,128)S(1)}, f32[2,2,32,256]{3,2,1,0:T(8,128)S(1)}, u32[]{:S(2)}, u32[]{:S(2)}) collective-permute-start(f32[2,2,32,256]{3,2,1,0:T(8,128)S(1)} %get-tuple-element.48), channel_id=1, source_target_pairs={{0,1},{1,0},{2,3},{3,2},{4,5},{5,4},{6,7},{7,6},{8,9},{9,8},{10,11... | collective-permute-start | bytes 393224 | tf_op jit(solution)/shard_map/ppermute | solution.py:579
  18.9 9.3 %collective-permute-start.11 = (f32[2,2,32,256]{3,2,1,0:T(8,128)S(1)}, f32[2,2,32,256]{3,2,1,0:T(8,128)S(1)}, u32[]{:S(2)}, u32[]{:S(2)}) collective-permute-start(f32[2,2,32,256]{3,2,1,0:T(8,128)S(1)} %get-tuple-element.48), channel_id=1, source_target_pairs={{0,3},{1,2},{2,1},{3,0},{4,7},{5,6},{6,5},{7,4},{8,11},{9,10},{10,... | collective-permute-start | bytes 393224 | tf_op jit(solution)/shard_map/ppermute | solution.py:579
  24.8 7.3 %collective-permute-start.10 = (f32[2,2,32,256]{3,2,1,0:T(8,128)S(1)}, f32[2,2,32,256]{3,2,1,0:T(8,128)S(1)}, u32[]{:S(2)}, u32[]{:S(2)}) collective-permute-start(f32[2,2,32,256]{3,2,1,0:T(8,128)S(1)} %collective-permute-done.7.refs_0_), channel_id=1, source_target_pairs={{0,12},{4,8},{8,4},{12,0},{1,13},{5,9},{9,5},{13,1},{2,14},{6,10},... | collective-permute-start | bytes 393224 | tf_op jit(solution)/shard_map/ppermute | solution.py:580
  26.3 8.1 %collective-permute-start.6 = (f32[2,2,32,256]{3,2,1,0:T(8,128)S(1)}, f32[2,2,32,256]{3,2,1,0:T(8,128)S(1)}, u32[]{:S(2)}, u32[]{:S(2)}) collective-permute-start(f32[2,2,32,256]{3,2,1,0:T(8,128)S(1)} %collective-permute-done.3.refs_0_), channel_id=1, source_target_pairs={{0,12},{4,8},{8,4},{12,0},{1,13},{5,9},{9,5},{13,1},{2,14},{6,10},... | collective-permute-start | bytes 393224 | tf_op jit(solution)/shard_map/ppermute | solution.py:580
  27.8 8.7 %collective-permute-start.5 = (f32[2,2,32,256]{3,2,1,0:T(8,128)S(1)}, f32[2,2,32,256]{3,2,1,0:T(8,128)S(1)}, u32[]{:S(2)}, u32[]{:S(2)}) collective-permute-start(f32[2,2,32,256]{3,2,1,0:T(8,128)S(1)} %collective-permute-done.3.refs_0_), channel_id=1, source_target_pairs={{0,8},{4,12},{8,0},{12,4},{1,9},{5,13},{9,1},{13,5},{2,10},{6,14},... | collective-permute-start | bytes 393224 | tf_op jit(solution)/shard_map/ppermute | solution.py:580
  28.2 9.1 %collective-permute-start.4 = (f32[2,2,32,256]{3,2,1,0:T(8,128)S(1)}, f32[2,2,32,256]{3,2,1,0:T(8,128)S(1)}, u32[]{:S(2)}, u32[]{:S(2)}) collective-permute-start(f32[2,2,32,256]{3,2,1,0:T(8,128)S(1)} %collective-permute-done.3.refs_0_), channel_id=1, source_target_pairs={{0,4},{4,0},{8,12},{12,8},{1,5},{5,1},{9,13},{13,9},{2,6},{6,2},{1... | collective-permute-start | bytes 393224 | tf_op jit(solution)/shard_map/ppermute | solution.py:580
  32.1 13.8 %collective-permute-start.9 = (f32[2,2,32,256]{3,2,1,0:T(8,128)S(1)}, f32[2,2,32,256]{3,2,1,0:T(8,128)S(1)}, u32[]{:S(2)}, u32[]{:S(2)}) collective-permute-start(f32[2,2,32,256]{3,2,1,0:T(8,128)S(1)} %collective-permute-done.7.refs_0_), channel_id=1, source_target_pairs={{0,8},{4,12},{8,0},{12,4},{1,9},{5,13},{9,1},{13,5},{2,10},{6,14},... | collective-permute-start | bytes 393224 | tf_op jit(solution)/shard_map/ppermute | solution.py:580
  34.4 11.6 %collective-permute-start.8 = (f32[2,2,32,256]{3,2,1,0:T(8,128)S(1)}, f32[2,2,32,256]{3,2,1,0:T(8,128)S(1)}, u32[]{:S(2)}, u32[]{:S(2)}) collective-permute-start(f32[2,2,32,256]{3,2,1,0:T(8,128)S(1)} %collective-permute-done.7.refs_0_), channel_id=1, source_target_pairs={{0,4},{4,0},{8,12},{12,8},{1,5},{5,1},{9,13},{13,9},{2,6},{6,2},{1... | collective-permute-start | bytes 393224 | tf_op jit(solution)/shard_map/ppermute | solution.py:580
  36.5 10.2 %collective-permute-start.14 = (f32[2,2,32,256]{3,2,1,0:T(8,128)S(1)}, f32[2,2,32,256]{3,2,1,0:T(8,128)S(1)}, u32[]{:S(2)}, u32[]{:S(2)}) collective-permute-start(f32[2,2,32,256]{3,2,1,0:T(8,128)S(1)} %collective-permute-done.11.refs_0_), channel_id=1, source_target_pairs={{0,12},{4,8},{8,4},{12,0},{1,13},{5,9},{9,5},{13,1},{2,14},{6,10},... | collective-permute-start | bytes 393224 | tf_op jit(solution)/shard_map/ppermute | solution.py:580
  37.3 9.3 %collective-permute-start.13 = (f32[2,2,32,256]{3,2,1,0:T(8,128)S(1)}, f32[2,2,32,256]{3,2,1,0:T(8,128)S(1)}, u32[]{:S(2)}, u32[]{:S(2)}) collective-permute-start(f32[2,2,32,256]{3,2,1,0:T(8,128)S(1)} %collective-permute-done.11.refs_0_), channel_id=1, source_target_pairs={{0,8},{4,12},{8,0},{12,4},{1,9},{5,13},{9,1},{13,5},{2,10},{6,14},... | collective-permute-start | bytes 393224 | tf_op jit(solution)/shard_map/ppermute | solution.py:580
  38.9 7.7 %collective-permute-start.12 = (f32[2,2,32,256]{3,2,1,0:T(8,128)S(1)}, f32[2,2,32,256]{3,2,1,0:T(8,128)S(1)}, u32[]{:S(2)}, u32[]{:S(2)}) collective-permute-start(f32[2,2,32,256]{3,2,1,0:T(8,128)S(1)} %collective-permute-done.11.refs_0_), channel_id=1, source_target_pairs={{0,4},{4,0},{8,12},{12,8},{1,5},{5,1},{9,13},{13,9},{2,6},{6,2},{1... | collective-permute-start | bytes 393224 | tf_op jit(solution)/shard_map/ppermute | solution.py:580
  39.9 0.7 copy-start.2
  46.0 2.0 %collective-permute-start.15 = (f32[4,2,2,32,256]{4,3,2,1,0:T(8,128)S(1)}, f32[4,2,2,32,256]{4,3,2,1,0:T(8,128)S(1)}, u32[]{:S(2)}, u32[]{:S(2)}) collective-permute-start(f32[4,2,2,32,256]{4,3,2,1,0:T(8,128)S(1)} %shard_map.76.refs_5_), channel_id=1, source_target_pairs={{0,16},{16,0},{1,17},{17,1},{2,18},{18,2},{3,19},{19,3},{4,20},{20... | collective-permute-start | bytes 1572872 | tf_op jit(solution)/shard_map/ppermute | solution.py:58
  46.1 2.6 %collective-permute-start.16 = (f32[4,2,2,32,256]{4,3,2,1,0:T(8,128)S(1)}, f32[4,2,2,32,256]{4,3,2,1,0:T(8,128)S(1)}, u32[]{:S(2)}, u32[]{:S(2)}) collective-permute-start(f32[4,2,2,32,256]{4,3,2,1,0:T(8,128)S(1)} %shard_map.77.refs_6_), channel_id=1, source_target_pairs={{0,16},{16,0},{1,17},{17,1},{2,18},{18,2},{3,19},{19,3},{4,20},{20... | collective-permute-start | bytes 1572872 | tf_op jit(solution)/shard_map/ppermute | solution.py:58
  46.7 2.7 %collective-permute-start.17 = (f32[4,2,2,32,256]{4,3,2,1,0:T(8,128)S(1)}, f32[4,2,2,32,256]{4,3,2,1,0:T(8,128)S(1)}, u32[]{:S(2)}, u32[]{:S(2)}) collective-permute-start(f32[4,2,2,32,256]{4,3,2,1,0:T(8,128)S(1)} %shard_map.78.refs_7_), channel_id=1, source_target_pairs={{0,16},{16,0},{1,17},{17,1},{2,18},{18,2},{3,19},{19,3},{4,20},{20... | collective-permute-start | bytes 1572872 | tf_op jit(solution)/shard_map/ppermute | solution.py:58
  49.4 32.4 %copy-start.3 = (s32[1,1,2,2]{3,2,1,0:T(2,128)S(1)}, s32[1,1,2,2]{3,2,1,0:T(2,128)}, u32[]{:S(2)}) copy-start(s32[1,1,2,2]{3,2,1,0:T(2,128)} %param.10) | copy-start | bytes 52
  62.7 2.0 %collective-permute-start.18 = (f32[2,128,512]{2,1,0:T(8,128)S(1)}, f32[2,128,512]{2,1,0:T(8,128)S(1)}, u32[]{:S(2)}, u32[]{:S(2)}) collective-permute-start(f32[2,128,512]{2,1,0:T(8,128)S(1)} %get-tuple-element.53), channel_id=1, source_target_pairs={{0,16},{16,0},{1,17},{17,1},{2,18},{18,2},{3,19},{19,3},{4,20},{20... | collective-permute-start | bytes 1572872 | tf_op jit(solution)/shard_map/ppermute | solution.py:58
  65.4 9.2 %collective-permute-start.19 = (f32[2,128,256]{2,1,0:T(8,128)S(1)}, f32[2,128,256]{2,1,0:T(8,128)S(1)}, u32[]{:S(2)}, u32[]{:S(2)}) collective-permute-start(f32[2,128,256]{2,1,0:T(8,128)S(1)} %get-tuple-element.55), channel_id=1, source_target_pairs={{0,4},{4,0},{8,12},{12,8},{1,5},{5,1},{9,13},{13,9},{2,6},{6,2},{1... | collective-permute-start | bytes 786440 | tf_op jit(solution)/shard_map/ppermute | solution.py:58
  66.5 12.6 %collective-permute-start.20 = (f32[2,128,256]{2,1,0:T(8,128)S(1)}, f32[2,128,256]{2,1,0:T(8,128)S(1)}, u32[]{:S(2)}, u32[]{:S(2)}) collective-permute-start(f32[2,128,256]{2,1,0:T(8,128)S(1)} %get-tuple-element.56), channel_id=1, source_target_pairs={{4,8},{12,0},{8,4},{0,12},{5,9},{13,1},{9,5},{1,13},{6,10},{14,2},... | collective-permute-start | bytes 786440 | tf_op jit(solution)/shard_map/ppermute | solution.py:58
  79.8 2.0 %collective-permute-start.21 = (f32[2,128,512]{2,1,0:T(8,128)S(1)}, f32[2,128,512]{2,1,0:T(8,128)S(1)}, u32[]{:S(2)}, u32[]{:S(2)}) collective-permute-start(f32[2,128,512]{2,1,0:T(8,128)S(1)} %shard_map.81.refs_3_.refs_6_), channel_id=1, source_target_pairs={{0,16},{16,0},{1,17},{17,1},{2,18},{18,2},{3,19},{19,3},{4,20},{20... | collective-permute-start | bytes 1572872 | tf_op jit(solution)/shard_map/ppermute | solution.py:58
  90.4 1.2 collective-permute-start.22
  91.7 4.5 %collective-permute-start.25 = (f32[2]{0:T(128)S(1)}, f32[2]{0:T(128)S(1)}, u32[]{:S(2)}, u32[]{:S(2)}) collective-permute-start(f32[2]{0:T(128)S(1)} %add.26.refs_2_), channel_id=1, source_target_pairs={{0,12},{4,8},{8,4},{12,0},{1,13},{5,9},{9,5},{13,1},{2,14},{6,10},... | collective-permute-start | bytes 32 | tf_op jit(solution)/shard_map/ppermute | solution.py:517
  93.9 3.6 %collective-permute-start.24 = (f32[2]{0:T(128)S(1)}, f32[2]{0:T(128)S(1)}, u32[]{:S(2)}, u32[]{:S(2)}) collective-permute-start(f32[2]{0:T(128)S(1)} %add.26.refs_2_), channel_id=1, source_target_pairs={{0,8},{4,12},{8,0},{12,4},{1,9},{5,13},{9,1},{13,5},{2,10},{6,14},... | collective-permute-start | bytes 32 | tf_op jit(solution)/shard_map/ppermute | solution.py:517
  94.3 3.6 %collective-permute-start.23 = (f32[2]{0:T(128)S(1)}, f32[2]{0:T(128)S(1)}, u32[]{:S(2)}, u32[]{:S(2)}) collective-permute-start(f32[2]{0:T(128)S(1)} %add.26.refs_2_), channel_id=1, source_target_pairs={{0,4},{4,0},{8,12},{12,8},{1,5},{5,1},{9,13},{13,9},{2,6},{6,2},{1... | collective-permute-start | bytes 32 | tf_op jit(solution)/shard_map/ppermute | solution.py:517
  106.5 2.0 %collective-permute-start.26 = (f32[2,128,512]{2,1,0:T(8,128)S(1)}, f32[2,128,512]{2,1,0:T(8,128)S(1)}, u32[]{:S(2)}, u32[]{:S(2)}) collective-permute-start(f32[2,128,512]{2,1,0:T(8,128)S(1)} %get-tuple-element.65), channel_id=1, source_target_pairs={{0,16},{16,0},{1,17},{17,1},{2,18},{18,2},{3,19},{19,3},{4,20},{20... | collective-permute-start | bytes 1572872 | tf_op jit(solution)/shard_map/ppermute | solution.py:58
  108.5 34.2 %copy-start.1 = (f32[2,128,256]{2,1,0:T(8,128)S(1)}, f32[2,128,256]{2,1,0:T(8,128)}, u32[]{:S(2)}) copy-start(f32[2,128,256]{2,1,0:T(8,128)} %refs_5_.1) | copy-start | bytes 786436
  109.3 9.2 %collective-permute-start.27 = (f32[2,128,256]{2,1,0:T(8,128)S(1)}, f32[2,128,256]{2,1,0:T(8,128)S(1)}, u32[]{:S(2)}, u32[]{:S(2)}) collective-permute-start(f32[2,128,256]{2,1,0:T(8,128)S(1)} %get-tuple-element.67), channel_id=1, source_target_pairs={{0,4},{4,0},{8,12},{12,8},{1,5},{5,1},{9,13},{13,9},{2,6},{6,2},{1... | collective-permute-start | bytes 786440 | tf_op jit(solution)/shard_map/ppermute | solution.py:58
  110.2 14.2 %collective-permute-start.28 = (f32[2,128,256]{2,1,0:T(8,128)S(1)}, f32[2,128,256]{2,1,0:T(8,128)S(1)}, u32[]{:S(2)}, u32[]{:S(2)}) collective-permute-start(f32[2,128,256]{2,1,0:T(8,128)S(1)} %get-tuple-element.68), channel_id=1, source_target_pairs={{4,8},{12,0},{8,4},{0,12},{5,9},{13,1},{9,5},{1,13},{6,10},{14,2},... | collective-permute-start | bytes 786440 | tf_op jit(solution)/shard_map/ppermute | solution.py:58
  125.1 2.0 %collective-permute-start.29 = (f32[2,128,512]{2,1,0:T(8,128)S(1)}, f32[2,128,512]{2,1,0:T(8,128)S(1)}, u32[]{:S(2)}, u32[]{:S(2)}) collective-permute-start(f32[2,128,512]{2,1,0:T(8,128)S(1)} %shard_map.85.refs_3_.refs_7_), channel_id=1, source_target_pairs={{0,16},{16,0},{1,17},{17,1},{2,18},{18,2},{3,19},{19,3},{4,20},{20... | collective-permute-start | bytes 1572872 | tf_op jit(solution)/shard_map/ppermute | solution.py:58
  135.3 1.2 collective-permute-start.30
  136.6 4.5 %collective-permute-start.33 = (f32[2]{0:T(128)S(1)}, f32[2]{0:T(128)S(1)}, u32[]{:S(2)}, u32[]{:S(2)}) collective-permute-start(f32[2]{0:T(128)S(1)} %add.27.refs_0_), channel_id=1, source_target_pairs={{0,12},{4,8},{8,4},{12,0},{1,13},{5,9},{9,5},{13,1},{2,14},{6,10},... | collective-permute-start | bytes 32 | tf_op jit(solution)/shard_map/ppermute | solution.py:517
  137.3 3.8 %collective-permute-start.32 = (f32[2]{0:T(128)S(1)}, f32[2]{0:T(128)S(1)}, u32[]{:S(2)}, u32[]{:S(2)}) collective-permute-start(f32[2]{0:T(128)S(1)} %add.27.refs_0_), channel_id=1, source_target_pairs={{0,8},{4,12},{8,0},{12,4},{1,9},{5,13},{9,1},{13,5},{2,10},{6,14},... | collective-permute-start | bytes 32 | tf_op jit(solution)/shard_map/ppermute | solution.py:517
  139.1 3.6 %collective-permute-start.31 = (f32[2]{0:T(128)S(1)}, f32[2]{0:T(128)S(1)}, u32[]{:S(2)}, u32[]{:S(2)}) collective-permute-start(f32[2]{0:T(128)S(1)} %add.27.refs_0_), channel_id=1, source_target_pairs={{0,4},{4,0},{8,12},{12,8},{1,5},{5,1},{9,13},{13,9},{2,6},{6,2},{1... | collective-permute-start | bytes 32 | tf_op jit(solution)/shard_map/ppermute | solution.py:517

commit v5 on v4

--- a/solution.py
+++ b/solution.py
@@ -13,7 +13,7 @@
 
 DAMPING = 1.0
 UNROLL = 2
-BROAD = 2
+BROAD = 8
 USED, PLACE_MA, SIDE, PLACE_Y, SIDE_Y = range(5)
 
 
@@ -109,6 +109,8 @@
         self.rows = tile_rows + patch
         self.cols = tile_cols + patch
         self.narrow = math.gcd(lead, UNROLL)
+        others = modes - lead
+        self.foreign = others if 0 < others <= BROAD else self.narrow
         self.broad = math.gcd(modes, BROAD)
 
     def scratch(self, width, windows=True):
@@ -138,26 +140,28 @@
         region[:, rim : rim + rows] = middle[...]
         region[:, rim + rows :] = high
 
-    def row_split(self, row):
-        shift = lax.rem(row, 8)
-        return pl.multiple_of(row - shift, 8), shift
+    def split(self, place, step):
+        shift = lax.rem(place, step)
+        return pl.multiple_of(place - shift, step), shift
 
     def take_windows(self, windows, region, centres):
         wide = self.patch
         for slot in range(self.slots):
             for part in range(2):
-                base, shift = self.row_split(centres[slot, 0])
-                strip = region[part, pl.ds(base, wide + 8), :]
-                strip = pltpu.roll(strip, wide + 8 - shift, 0)[:wide]
-                turned = pltpu.roll(strip, self.cols - centres[slot, 1], 1)
-                windows[slot, part] = turned[:, :wide]
+                base, shift = self.split(centres[slot, 0], 8)
+                first, turn = self.split(centres[slot, 1], 128)
+                strip = region[part, pl.ds(base, wide + 8), pl.ds(first, wide + 128)]
+                strip = pltpu.roll(strip, wide + 128 - turn, 1)[:, :wide]
+                windows[slot, part] = pltpu.roll(strip, wide + 8 - shift, 0)[:wide]
 
     def place(self, canvas, slot, part, piece, centres):
-        strip = jnp.concatenate([piece, jnp.zeros((self.patch, self.cols - self.patch), jnp.float32)], 1)
-        strip = jnp.concatenate([strip, jnp.zeros((8, self.cols), jnp.float32)], 0)
-        base, shift = self.row_split(centres[slot, 0])
-        turned = pltpu.roll(pltpu.roll(strip, centres[slot, 1], 1), shift, 0)
-        canvas[part, pl.ds(base, self.patch + 8), :] += turned
+        wide = self.patch
+        base, shift = self.split(centres[slot, 0], 8)
+        first, turn = self.split(centres[slot, 1], 128)
+        strip = jnp.concatenate([piece, jnp.zeros((8, wide), jnp.float32)], 0)
+        strip = pltpu.roll(strip, shift, 0)
+        strip = jnp.concatenate([strip, jnp.zeros((wide + 8, 128), jnp.float32)], 1)
+        canvas[part, pl.ds(base, wide + 8), pl.ds(first, wide + 128)] += pltpu.roll(strip, turn, 1)
 
     def each_modes(self, body):
         def step(index, carry):
@@ -269,7 +273,7 @@
         for mode, field in zip(modes, fields):
             plan.store(spectra, slot * plan.modes + mode, field)
 
-    plan.each_unit(plan.modes - lead, plan.narrow, forward)
+    plan.each_unit(plan.modes - lead, plan.foreign, forward)
     region[...] = jnp.zeros_like(region)
     for slot in range(plan.slots):
         live = jnp.where(slot < info[USED], 1.0, 0.0)
@@ -609,7 +613,7 @@
         [probes.shape, spectra.shape, (slots, patch, patch), tall] + [fold] * swaps_x,
         [smem] * 2 + [vmem] * (6 + 2 * (groups - 1)),
         [info, centres, probes, spectra, windows, *packed, *crossed, targets, one, two],
-        scratch=plan.scratch(max(plan.broad, plan.narrow), False)
+        scratch=plan.scratch(max(plan.broad, plan.foreign), False)
         + [image_scratch, pltpu.VMEM((patch, patch), jnp.float32)],
         aliases={2: 0, 3: 1},
     )

time: 145 us -> 138 us (0.952)
  Pallas kernels: 51.3 us -> 44.3 us
    pallas_call x15, Pallas kernels: 51.3 us -> 44.3 us  [kernel_of(): pl.pallas_call(body, out_shape=[space(shape, dtypes.get(k, jnp.float32))...]
where the time goes in v5:
time: 138 us
  waiting for transfers between devices  58 us (42%)
  Pallas kernels  44.3 us (32%)
  starting transfers between devices  32.6 us (24%)
  local copies, waits for them, and re-layouts  1.72 us (1%)
    pallas_call x15, Pallas kernels, kernel_of(): pl.pallas_call(body, out_shape=[space(shape, dtypes.get(k, jnp.float32))...  44.3 us
    ppermute x16, waiting for transfers between devices, swap(): lax.ppermute(block, axis, pairs)  42 us
    ppermute x16, starting transfers between devices, swap(): lax.ppermute(block, axis, pairs)  11 us
    ppermute x9, starting transfers between devices, shards(): across = [lax.ppermute(block, 'gy', p) for p in exchanges(columns)]  10.2 us
    ppermute x6, starting transfers between devices, totals_of(): lax.ppermute(sums, 'gy', pairs)  6.98 us
    ppermute x3, waiting for transfers between devices, shards(): block = lax.ppermute(mine, 'ma', pairs)  5.95 us
    ppermute x6, waiting for transfers between devices, totals_of(): lax.ppermute(sums, 'gy', pairs)  5.4 us
    ppermute x9, waiting for transfers between devices, shards(): across = [lax.ppermute(block, 'gy', p) for p in exchanges(columns)]  4.66 us
  transfers between devices with their start and end apart: 34, of which 24 were waited for; matrix products, arithmetic and copies ran while one was open for 0% of the time, Pallas kernels for 4%

profile of v5, /device:TPU:0, one launch (start us, length us, event | category | flops | bytes accessed | tf_op | source)
XLA Modules:
  0.0 137.7 jit_solution(13742175290435509494)
XLA Ops:
  0.9 1.6 %shard_map.73 = (f32[2,2,32,256]{3,2,1,0:T(8,128)S(1)}, f32[2,128,128]{2,1,0:T(8,128)S(1)}, f32[2,128,128]{2,1,0:T(8,128)S(1)}) custom-call(s32[5]{0:T(128)S(1)} %stack.52.refs_0_, f32[2,2,256,256]{3,2,1,0:T(8,128)} %refs_8_.1, f32[2,128,256]{2,1,0:T(8,128)} %refs_5_.1), custom_call_target="tpu_custom_call" | custom-call | tf_op jit(solution)/shard_map/pallas_call | solution.py:88
  2.5 3.0 %collective-permute-start = (f32[2,128,128]{2,1,0:T(8,128)S(1)}, f32[2,128,128]{2,1,0:T(8,128)S(1)}, u32[]{:S(2)}, u32[]{:S(2)}) collective-permute-start(f32[2,128,128]{2,1,0:T(8,128)S(1)} %get-tuple-element.43), channel_id=1, source_target_pairs={{0,4},{4,0},{8,12},{12,8},{1,5},{5,1},{9,13},{13,9},{2,6},{6,2},{1... | collective-permute-start | bytes 393224 | tf_op jit(solution)/shard_map/ppermute | solution.py:58
  5.5 1.5 %collective-permute-start.1 = (f32[2,128,128]{2,1,0:T(8,128)S(1)}, f32[2,128,128]{2,1,0:T(8,128)S(1)}, u32[]{:S(2)}, u32[]{:S(2)}) collective-permute-start(f32[2,128,128]{2,1,0:T(8,128)S(1)} %get-tuple-element.44), channel_id=1, source_target_pairs={{4,8},{12,0},{8,4},{0,12},{5,9},{13,1},{9,5},{1,13},{6,10},{14,2},... | collective-permute-start | bytes 393224 | tf_op jit(solution)/shard_map/ppermute | solution.py:58
  7.0 2.4 %collective-permute-done.refs_2_ = f32[2,128,128]{2,1,0:T(8,128)S(1)} collective-permute-done((f32[2,128,128]{2,1,0:T(8,128)S(1)}, f32[2,128,128]{2,1,0:T(8,128)S(1)}, u32[]{:S(2)}, u32[]{:S(2)}) %collective-permute-start) | collective-permute-done | bytes 131104 | tf_op jit(solution)/shard_map/ppermute | solution.py:58
  9.4 3.6 %collective-permute-done.1.refs_3_ = f32[2,128,128]{2,1,0:T(8,128)S(1)} collective-permute-done((f32[2,128,128]{2,1,0:T(8,128)S(1)}, f32[2,128,128]{2,1,0:T(8,128)S(1)}, u32[]{:S(2)}, u32[]{:S(2)}) %collective-permute-start.1) | collective-permute-done | bytes 131104 | tf_op jit(solution)/shard_map/ppermute | solution.py:58
  13.1 0.9 copy-done
  14.7 2.7 %collective-permute-start.7 = (f32[2,2,32,256]{3,2,1,0:T(8,128)S(1)}, f32[2,2,32,256]{3,2,1,0:T(8,128)S(1)}, u32[]{:S(2)}, u32[]{:S(2)}) collective-permute-start(f32[2,2,32,256]{3,2,1,0:T(8,128)S(1)} %get-tuple-element.48), channel_id=1, source_target_pairs={{0,2},{1,3},{2,0},{3,1},{4,6},{5,7},{6,4},{7,5},{8,10},{9,11},{10,... | collective-permute-start | bytes 393224 | tf_op jit(solution)/shard_map/ppermute | solution.py:583
  17.3 1.6 %collective-permute-start.3 = (f32[2,2,32,256]{3,2,1,0:T(8,128)S(1)}, f32[2,2,32,256]{3,2,1,0:T(8,128)S(1)}, u32[]{:S(2)}, u32[]{:S(2)}) collective-permute-start(f32[2,2,32,256]{3,2,1,0:T(8,128)S(1)} %get-tuple-element.48), channel_id=1, source_target_pairs={{0,1},{1,0},{2,3},{3,2},{4,5},{5,4},{6,7},{7,6},{8,9},{9,8},{10,11... | collective-permute-start | bytes 393224 | tf_op jit(solution)/shard_map/ppermute | solution.py:583
  19.1 5.7 %collective-permute-done.7.refs_0_ = f32[2,2,32,256]{3,2,1,0:T(8,128)S(1)} collective-permute-done((f32[2,2,32,256]{3,2,1,0:T(8,128)S(1)}, f32[2,2,32,256]{3,2,1,0:T(8,128)S(1)}, u32[]{:S(2)}, u32[]{:S(2)}) %collective-permute-start.7) | collective-permute-done | bytes 131104 | tf_op jit(solution)/shard_map/ppermute | solution.py:583
  24.8 1.4 %collective-permute-start.10 = (f32[2,2,32,256]{3,2,1,0:T(8,128)S(1)}, f32[2,2,32,256]{3,2,1,0:T(8,128)S(1)}, u32[]{:S(2)}, u32[]{:S(2)}) collective-permute-start(f32[2,2,32,256]{3,2,1,0:T(8,128)S(1)} %collective-permute-done.7.refs_0_), channel_id=1, source_target_pairs={{0,12},{4,8},{8,4},{12,0},{1,13},{5,9},{9,5},{13,1},{2,14},{6,10},... | collective-permute-start | bytes 393224 | tf_op jit(solution)/shard_map/ppermute | solution.py:584
  26.3 1.5 %collective-permute-start.6 = (f32[2,2,32,256]{3,2,1,0:T(8,128)S(1)}, f32[2,2,32,256]{3,2,1,0:T(8,128)S(1)}, u32[]{:S(2)}, u32[]{:S(2)}) collective-permute-start(f32[2,2,32,256]{3,2,1,0:T(8,128)S(1)} %collective-permute-done.3.refs_0_), channel_id=1, source_target_pairs={{0,12},{4,8},{8,4},{12,0},{1,13},{5,9},{9,5},{13,1},{2,14},{6,10},... | collective-permute-start | bytes 393224 | tf_op jit(solution)/shard_map/ppermute | solution.py:584
  28.2 1.5 %collective-permute-start.4 = (f32[2,2,32,256]{3,2,1,0:T(8,128)S(1)}, f32[2,2,32,256]{3,2,1,0:T(8,128)S(1)}, u32[]{:S(2)}, u32[]{:S(2)}) collective-permute-start(f32[2,2,32,256]{3,2,1,0:T(8,128)S(1)} %collective-permute-done.3.refs_0_), channel_id=1, source_target_pairs={{0,4},{4,0},{8,12},{12,8},{1,5},{5,1},{9,13},{13,9},{2,6},{6,2},{1... | collective-permute-start | bytes 393224 | tf_op jit(solution)/shard_map/ppermute | solution.py:584
  29.8 2.4 %collective-permute-done.10.refs_3_ = f32[2,2,32,256]{3,2,1,0:T(8,128)S(1)} collective-permute-done((f32[2,2,32,256]{3,2,1,0:T(8,128)S(1)}, f32[2,2,32,256]{3,2,1,0:T(8,128)S(1)}, u32[]{:S(2)}, u32[]{:S(2)}) %collective-permute-start.10) | collective-permute-done | bytes 131104 | tf_op jit(solution)/shard_map/ppermute | solution.py:584
  32.1 2.3 %collective-permute-done.6.refs_3_ = f32[2,2,32,256]{3,2,1,0:T(8,128)S(1)} collective-permute-done((f32[2,2,32,256]{3,2,1,0:T(8,128)S(1)}, f32[2,2,32,256]{3,2,1,0:T(8,128)S(1)}, u32[]{:S(2)}, u32[]{:S(2)}) %collective-permute-start.6) | collective-permute-done | bytes 131104 | tf_op jit(solution)/shard_map/ppermute | solution.py:584
  34.4 2.0 %collective-permute-start.8 = (f32[2,2,32,256]{3,2,1,0:T(8,128)S(1)}, f32[2,2,32,256]{3,2,1,0:T(8,128)S(1)}, u32[]{:S(2)}, u32[]{:S(2)}) collective-permute-start(f32[2,2,32,256]{3,2,1,0:T(8,128)S(1)} %collective-permute-done.7.refs_0_), channel_id=1, source_target_pairs={{0,4},{4,0},{8,12},{12,8},{1,5},{5,1},{9,13},{13,9},{2,6},{6,2},{1... | collective-permute-start | bytes 393224 | tf_op jit(solution)/shard_map/ppermute | solution.py:584
  36.5 0.8 collective-permute-start.14
  37.3 1.6 %collective-permute-start.13 = (f32[2,2,32,256]{3,2,1,0:T(8,128)S(1)}, f32[2,2,32,256]{3,2,1,0:T(8,128)S(1)}, u32[]{:S(2)}, u32[]{:S(2)}) collective-permute-start(f32[2,2,32,256]{3,2,1,0:T(8,128)S(1)} %collective-permute-done.11.refs_0_), channel_id=1, source_target_pairs={{0,8},{4,12},{8,0},{12,4},{1,9},{5,13},{9,1},{13,5},{2,10},{6,14},... | collective-permute-start | bytes 393224 | tf_op jit(solution)/shard_map/ppermute | solution.py:584
  38.9 1.0 collective-permute-start.12
  40.6 4.9 %shard_map.75 = (f32[8,2,256,256]{3,2,1,0:T(8,128)S(1)}, f32[16,256,512]{2,1,0:T(8,128)S(1)}, f32[2,2,256,256]{3,2,1,0:T(8,128)S(1)}, f32[2,256,256]{2,1,0:T(8,1...) custom-call(s32[5]{0:T(128)S(1)} %stack.52.refs_0_, s32[2,2]{1,0:T(2,128)S(1)} %bitcast.16, ...), custom_call_target="tpu_custom_call" | custom-call | tf_op jit(solution)/shard_map/pallas_call | solution.py:88
  46.4 1.1 collective-permute-done.15.refs_8_
  49.1 10.5 %shard_map.79 = (f32[8,2,256,256]{3,2,1,0:T(8,128)S(1)}, f32[16,256,512]{2,1,0:T(8,128)S(1)}, f32[2,256,256]{2,1,0:T(8,128)S(1)}, f32[2,128,512]{2,1,0:T(8,128)S(1)}, f32[2,128,512]{2,1,0:T(8,128)S(1)}) custom-call(s32[5]{0:T(128)S(1)} %stack.52.refs_0_, s32[2,2]{1,0:T(2,128)S(1)} %bitcast.17, ...), custom_call_target="tpu_custom_call", output_to_operand_aliasing={{0}: (2, {}), {1}: (3, {})} | custom-call | tf_op jit(solution)/shard_map/pallas_call | solution.py:88
  59.8 1.8 %collective-permute-done.18.refs_3_ = f32[2,128,512]{2,1,0:T(8,128)S(1)} collective-permute-done((f32[2,128,512]{2,1,0:T(8,128)S(1)}, f32[2,128,512]{2,1,0:T(8,128)S(1)}, u32[]{:S(2)}, u32[]{:S(2)}) %collective-permute-start.18) | collective-permute-done | bytes 524320 | tf_op jit(solution)/shard_map/ppermute | solution.py:58
  61.5 0.8 shard_map.80
  62.3 1.0 collective-permute-start.19
  64.0 7.5 %collective-permute-done.19.refs_3_ = f32[2,128,256]{2,1,0:T(8,128)S(1)} collective-permute-done((f32[2,128,256]{2,1,0:T(8,128)S(1)}, f32[2,128,256]{2,1,0:T(8,128)S(1)}, u32[]{:S(2)}, u32[]{:S(2)}) %collective-permute-start.19) | collective-permute-done | bytes 262176 | tf_op jit(solution)/shard_map/ppermute | solution.py:58
  71.6 4.4 %collective-permute-done.20.refs_4_ = f32[2,128,256]{2,1,0:T(8,128)S(1)} collective-permute-done((f32[2,128,256]{2,1,0:T(8,128)S(1)}, f32[2,128,256]{2,1,0:T(8,128)S(1)}, u32[]{:S(2)}, u32[]{:S(2)}) %collective-permute-start.20) | collective-permute-done | bytes 262176 | tf_op jit(solution)/shard_map/ppermute | solution.py:58
  76.8 1.9 %collective-permute-done.21.refs_4_ = f32[2,128,512]{2,1,0:T(8,128)S(1)} collective-permute-done((f32[2,128,512]{2,1,0:T(8,128)S(1)}, f32[2,128,512]{2,1,0:T(8,128)S(1)}, u32[]{:S(2)}, u32[]{:S(2)}) %collective-permute-start.21) | collective-permute-done | bytes 524320 | tf_op jit(solution)/shard_map/ppermute | solution.py:58
  78.7 7.5 %shard_map.82 = (f32[2]{0:T(128)S(1)}, f32[16,256,512]{2,1,0:T(8,128)S(1)}, f32[2,256,256]{2,1,0:T(8,128)S(1)}, f32[2,256,256]{2,1,0:T(8,128)S(1)}) custom-call(s32[5]{0:T(128)S(1)} %stack.52.refs_0_, s32[2,2]{1,0:T(2,128)S(1)} %bitcast.18, f32[2]{0:T(128)S(1)} %get-tuple-element.40.refs_2_.refs_1_, f32[2,128,512]{2,1,0:T(8,128)S(1)} %shard_map.81.refs_3_.refs_6_, ...), custom_call_target="tpu_custom_call" | custom-call | tf_op jit(solution)/shard_map/pallas_call | solution.py:88
  86.4 1.0 collective-permute-done.22
  87.4 2.3 %collective-permute-start.25 = (f32[2]{0:T(128)S(1)}, f32[2]{0:T(128)S(1)}, u32[]{:S(2)}, u32[]{:S(2)}) collective-permute-start(f32[2]{0:T(128)S(1)} %add.26.refs_2_), channel_id=1, source_target_pairs={{0,12},{4,8},{8,4},{12,0},{1,13},{5,9},{9,5},{13,1},{2,14},{6,10},... | collective-permute-start | bytes 32 | tf_op jit(solution)/shard_map/ppermute | solution.py:521
  90.1 0.8 collective-permute-start.23
  90.9 1.0 collective-permute-done.25.refs_5_
  91.9 1.4 %collective-permute-done.24.refs_4_ = f32[2]{0:T(128)S(1)} collective-permute-done((f32[2]{0:T(128)S(1)}, f32[2]{0:T(128)S(1)}, u32[]{:S(2)}, u32[]{:S(2)}) %collective-permute-start.24) | collective-permute-done | bytes 40 | tf_op jit(solution)/shard_map/ppermute | solution.py:521
  93.7 7.0 %shard_map.83 = (f32[16,256,512]{2,1,0:T(8,128)S(1)}, f32[1]{0:T(128)}, f32[2,128,512]{2,1,0:T(8,128)S(1)}, f32[2,128,512]{2,1,0:T(8,128)S(1)}) custom-call(s32[5]{0:T(128)S(1)} %stack.52.refs_0_, s32[2,2]{1,0:T(2,128)S(1)} %bitcast.19, f32[2]{0:T(128)S(1)} %add.26.refs_2_, f32[2]{0:T(128)S(1)} %collective-permute-done.23.refs_3_, ...), custom_call_target="tpu_custom_call" | custom-call | tf_op jit(solution)/shard_map/pallas_call | solution.py:88
  100.8 1.9 %collective-permute-done.26.refs_3_ = f32[2,128,512]{2,1,0:T(8,128)S(1)} collective-permute-done((f32[2,128,512]{2,1,0:T(8,128)S(1)}, f32[2,128,512]{2,1,0:T(8,128)S(1)}, u32[]{:S(2)}, u32[]{:S(2)}) %collective-permute-start.26) | collective-permute-done | bytes 524320 | tf_op jit(solution)/shard_map/ppermute | solution.py:58
  102.7 0.8 shard_map.84
  103.5 0.8 collective-permute-start.27
  104.3 2.3 %collective-permute-start.28 = (f32[2,128,256]{2,1,0:T(8,128)S(1)}, f32[2,128,256]{2,1,0:T(8,128)S(1)}, u32[]{:S(2)}, u32[]{:S(2)}) collective-permute-start(f32[2,128,256]{2,1,0:T(8,128)S(1)} %get-tuple-element.68), channel_id=1, source_target_pairs={{4,8},{12,0},{8,4},{0,12},{5,9},{13,1},{9,5},{1,13},{6,10},{14,2},... | collective-permute-start | bytes 786440 | tf_op jit(solution)/shard_map/ppermute | solution.py:58
  106.6 6.1 %collective-permute-done.27.refs_3_ = f32[2,128,256]{2,1,0:T(8,128)S(1)} collective-permute-done((f32[2,128,256]{2,1,0:T(8,128)S(1)}, f32[2,128,256]{2,1,0:T(8,128)S(1)}, u32[]{:S(2)}, u32[]{:S(2)}) %collective-permute-start.27) | collective-permute-done | bytes 262176 | tf_op jit(solution)/shard_map/ppermute | solution.py:58
  112.7 5.8 %collective-permute-done.28.refs_4_ = f32[2,128,256]{2,1,0:T(8,128)S(1)} collective-permute-done((f32[2,128,256]{2,1,0:T(8,128)S(1)}, f32[2,128,256]{2,1,0:T(8,128)S(1)}, u32[]{:S(2)}, u32[]{:S(2)}) %collective-permute-start.28) | collective-permute-done | bytes 262176 | tf_op jit(solution)/shard_map/ppermute | solution.py:58
  119.4 1.9 %collective-permute-done.29.refs_4_ = f32[2,128,512]{2,1,0:T(8,128)S(1)} collective-permute-done((f32[2,128,512]{2,1,0:T(8,128)S(1)}, f32[2,128,512]{2,1,0:T(8,128)S(1)}, u32[]{:S(2)}, u32[]{:S(2)}) %collective-permute-start.29) | collective-permute-done | bytes 524320 | tf_op jit(solution)/shard_map/ppermute | solution.py:58
  121.3 7.0 %shard_map.86 = f32[2]{0:T(128)S(1)} custom-call(s32[5]{0:T(128)S(1)} %stack.52.refs_0_, s32[2,2]{1,0:T(2,128)S(1)} %bitcast.20, f32[2]{0:T(128)S(1)} %get-tuple-element.40.refs_2_.refs_1_, f32[2,128,512]{2,1,0:T(8,128)S(1)} %shard_map.85.refs_3_.refs_7_, f32[2,128,512]{2,1,0:T(8,128)S(1)} %collective-permute-done.29.refs_4_, ...), custom_call_target="tpu_custom_call" | custom-call | tf_op jit(solution)/shard_map/pallas_call | solution.py:88
  128.5 1.0 collective-permute-done.30
  130.2 1.8 %collective-permute-start.32 = (f32[2]{0:T(128)S(1)}, f32[2]{0:T(128)S(1)}, u32[]{:S(2)}, u32[]{:S(2)}) collective-permute-start(f32[2]{0:T(128)S(1)} %add.27.refs_0_), channel_id=1, source_target_pairs={{0,8},{4,12},{8,0},{12,4},{1,9},{5,13},{9,1},{13,5},{2,10},{6,14},... | collective-permute-start | bytes 32 | tf_op jit(solution)/shard_map/ppermute | solution.py:521
  132.1 1.0 collective-permute-start.31
  133.0 1.0 collective-permute-done.33.refs_3_
  134.0 1.6 %collective-permute-done.31.refs_1_ = f32[2]{0:T(128)S(1)} collective-permute-done((f32[2]{0:T(128)S(1)}, f32[2]{0:T(128)S(1)}, u32[]{:S(2)}, u32[]{:S(2)}) %collective-permute-start.31) | collective-permute-done | bytes 40 | tf_op jit(solution)/shard_map/ppermute | solution.py:521
  135.6 2.0 %shard_map.87 = f32[2,128,256]{2,1,0:T(8,128)} custom-call(f32[2]{0:T(128)S(1)} %add.27.refs_0_, f32[2]{0:T(128)S(1)} %collective-permute-done.31.refs_1_, f32[2]{0:T(128)S(1)} %collective-permute-done.32.refs_2_, f32[2]{0:T(128)S(1)} %collective-permute-done.33.refs_3_, f32[1]{0:T(128)} %get-tuple-element.70.refs_4_, f32[2,128,256]{2,1,0:T(8,128)S(1)} %copy-done.1, ...), custom_call_target="tpu_custom_call" | custom-call | tf_op jit(solution)/shard_map/pallas_call | solution.py:88
  (48 shorter events, 9.2 us)
Async XLA Ops:
  2.5 6.9 %collective-permute-start = (f32[2,128,128]{2,1,0:T(8,128)S(1)}, f32[2,128,128]{2,1,0:T(8,128)S(1)}, u32[]{:S(2)}, u32[]{:S(2)}) collective-permute-start(f32[2,128,128]{2,1,0:T(8,128)S(1)} %get-tuple-element.43), channel_id=1, source_target_pairs={{0,4},{4,0},{8,12},{12,8},{1,5},{5,1},{9,13},{13,9},{2,6},{6,2},{1... | collective-permute-start | bytes 393224 | tf_op jit(solution)/shard_map/ppermute | solution.py:58
  5.5 7.5 %collective-permute-start.1 = (f32[2,128,128]{2,1,0:T(8,128)S(1)}, f32[2,128,128]{2,1,0:T(8,128)S(1)}, u32[]{:S(2)}, u32[]{:S(2)}) collective-permute-start(f32[2,128,128]{2,1,0:T(8,128)S(1)} %get-tuple-element.44), channel_id=1, source_target_pairs={{4,8},{12,0},{8,4},{0,12},{5,9},{13,1},{9,5},{1,13},{6,10},{14,2},... | collective-permute-start | bytes 393224 | tf_op jit(solution)/shard_map/ppermute | solution.py:58
  13.1 1.0 copy-start
  14.6 24.3 %collective-permute-start.2 = (f32[2,128,512]{2,1,0:T(8,128)S(1)}, f32[2,128,512]{2,1,0:T(8,128)S(1)}, u32[]{:S(2)}, u32[]{:S(2)}) collective-permute-start(f32[2,128,512]{2,1,0:T(8,128)S(1)} %shard_map.74.refs_3_), channel_id=1, source_target_pairs={{0,16},{16,0},{1,17},{17,1},{2,18},{18,2},{3,19},{19,3},{4,20},{20... | collective-permute-start | bytes 1572872 | tf_op jit(solution)/shard_map/ppermute | solution.py:58
  14.7 10.2 %collective-permute-start.7 = (f32[2,2,32,256]{3,2,1,0:T(8,128)S(1)}, f32[2,2,32,256]{3,2,1,0:T(8,128)S(1)}, u32[]{:S(2)}, u32[]{:S(2)}) collective-permute-start(f32[2,2,32,256]{3,2,1,0:T(8,128)S(1)} %get-tuple-element.48), channel_id=1, source_target_pairs={{0,2},{1,3},{2,0},{3,1},{4,6},{5,7},{6,4},{7,5},{8,10},{9,11},{10,... | collective-permute-start | bytes 393224 | tf_op jit(solution)/shard_map/ppermute | solution.py:583
  17.3 8.9 %collective-permute-start.3 = (f32[2,2,32,256]{3,2,1,0:T(8,128)S(1)}, f32[2,2,32,256]{3,2,1,0:T(8,128)S(1)}, u32[]{:S(2)}, u32[]{:S(2)}) collective-permute-start(f32[2,2,32,256]{3,2,1,0:T(8,128)S(1)} %get-tuple-element.48), channel_id=1, source_target_pairs={{0,1},{1,0},{2,3},{3,2},{4,5},{5,4},{6,7},{7,6},{8,9},{9,8},{10,11... | collective-permute-start | bytes 393224 | tf_op jit(solution)/shard_map/ppermute | solution.py:583
  18.9 9.3 %collective-permute-start.11 = (f32[2,2,32,256]{3,2,1,0:T(8,128)S(1)}, f32[2,2,32,256]{3,2,1,0:T(8,128)S(1)}, u32[]{:S(2)}, u32[]{:S(2)}) collective-permute-start(f32[2,2,32,256]{3,2,1,0:T(8,128)S(1)} %get-tuple-element.48), channel_id=1, source_target_pairs={{0,3},{1,2},{2,1},{3,0},{4,7},{5,6},{6,5},{7,4},{8,11},{9,10},{10,... | collective-permute-start | bytes 393224 | tf_op jit(solution)/shard_map/ppermute | solution.py:583
  24.8 7.3 %collective-permute-start.10 = (f32[2,2,32,256]{3,2,1,0:T(8,128)S(1)}, f32[2,2,32,256]{3,2,1,0:T(8,128)S(1)}, u32[]{:S(2)}, u32[]{:S(2)}) collective-permute-start(f32[2,2,32,256]{3,2,1,0:T(8,128)S(1)} %collective-permute-done.7.refs_0_), channel_id=1, source_target_pairs={{0,12},{4,8},{8,4},{12,0},{1,13},{5,9},{9,5},{13,1},{2,14},{6,10},... | collective-permute-start | bytes 393224 | tf_op jit(solution)/shard_map/ppermute | solution.py:584
  26.3 8.1 %collective-permute-start.6 = (f32[2,2,32,256]{3,2,1,0:T(8,128)S(1)}, f32[2,2,32,256]{3,2,1,0:T(8,128)S(1)}, u32[]{:S(2)}, u32[]{:S(2)}) collective-permute-start(f32[2,2,32,256]{3,2,1,0:T(8,128)S(1)} %collective-permute-done.3.refs_0_), channel_id=1, source_target_pairs={{0,12},{4,8},{8,4},{12,0},{1,13},{5,9},{9,5},{13,1},{2,14},{6,10},... | collective-permute-start | bytes 393224 | tf_op jit(solution)/shard_map/ppermute | solution.py:584
  27.8 8.7 %collective-permute-start.5 = (f32[2,2,32,256]{3,2,1,0:T(8,128)S(1)}, f32[2,2,32,256]{3,2,1,0:T(8,128)S(1)}, u32[]{:S(2)}, u32[]{:S(2)}) collective-permute-start(f32[2,2,32,256]{3,2,1,0:T(8,128)S(1)} %collective-permute-done.3.refs_0_), channel_id=1, source_target_pairs={{0,8},{4,12},{8,0},{12,4},{1,9},{5,13},{9,1},{13,5},{2,10},{6,14},... | collective-permute-start | bytes 393224 | tf_op jit(solution)/shard_map/ppermute | solution.py:584
  28.2 9.1 %collective-permute-start.4 = (f32[2,2,32,256]{3,2,1,0:T(8,128)S(1)}, f32[2,2,32,256]{3,2,1,0:T(8,128)S(1)}, u32[]{:S(2)}, u32[]{:S(2)}) collective-permute-start(f32[2,2,32,256]{3,2,1,0:T(8,128)S(1)} %collective-permute-done.3.refs_0_), channel_id=1, source_target_pairs={{0,4},{4,0},{8,12},{12,8},{1,5},{5,1},{9,13},{13,9},{2,6},{6,2},{1... | collective-permute-start | bytes 393224 | tf_op jit(solution)/shard_map/ppermute | solution.py:584
  32.1 13.5 %collective-permute-start.9 = (f32[2,2,32,256]{3,2,1,0:T(8,128)S(1)}, f32[2,2,32,256]{3,2,1,0:T(8,128)S(1)}, u32[]{:S(2)}, u32[]{:S(2)}) collective-permute-start(f32[2,2,32,256]{3,2,1,0:T(8,128)S(1)} %collective-permute-done.7.refs_0_), channel_id=1, source_target_pairs={{0,8},{4,12},{8,0},{12,4},{1,9},{5,13},{9,1},{13,5},{2,10},{6,14},... | collective-permute-start | bytes 393224 | tf_op jit(solution)/shard_map/ppermute | solution.py:584
  34.4 11.3 %collective-permute-start.8 = (f32[2,2,32,256]{3,2,1,0:T(8,128)S(1)}, f32[2,2,32,256]{3,2,1,0:T(8,128)S(1)}, u32[]{:S(2)}, u32[]{:S(2)}) collective-permute-start(f32[2,2,32,256]{3,2,1,0:T(8,128)S(1)} %collective-permute-done.7.refs_0_), channel_id=1, source_target_pairs={{0,4},{4,0},{8,12},{12,8},{1,5},{5,1},{9,13},{13,9},{2,6},{6,2},{1... | collective-permute-start | bytes 393224 | tf_op jit(solution)/shard_map/ppermute | solution.py:584
  36.5 9.8 %collective-permute-start.14 = (f32[2,2,32,256]{3,2,1,0:T(8,128)S(1)}, f32[2,2,32,256]{3,2,1,0:T(8,128)S(1)}, u32[]{:S(2)}, u32[]{:S(2)}) collective-permute-start(f32[2,2,32,256]{3,2,1,0:T(8,128)S(1)} %collective-permute-done.11.refs_0_), channel_id=1, source_target_pairs={{0,12},{4,8},{8,4},{12,0},{1,13},{5,9},{9,5},{13,1},{2,14},{6,10},... | collective-permute-start | bytes 393224 | tf_op jit(solution)/shard_map/ppermute | solution.py:584
  37.3 9.0 %collective-permute-start.13 = (f32[2,2,32,256]{3,2,1,0:T(8,128)S(1)}, f32[2,2,32,256]{3,2,1,0:T(8,128)S(1)}, u32[]{:S(2)}, u32[]{:S(2)}) collective-permute-start(f32[2,2,32,256]{3,2,1,0:T(8,128)S(1)} %collective-permute-done.11.refs_0_), channel_id=1, source_target_pairs={{0,8},{4,12},{8,0},{12,4},{1,9},{5,13},{9,1},{13,5},{2,10},{6,14},... | collective-permute-start | bytes 393224 | tf_op jit(solution)/shard_map/ppermute | solution.py:584
  38.9 7.4 %collective-permute-start.12 = (f32[2,2,32,256]{3,2,1,0:T(8,128)S(1)}, f32[2,2,32,256]{3,2,1,0:T(8,128)S(1)}, u32[]{:S(2)}, u32[]{:S(2)}) collective-permute-start(f32[2,2,32,256]{3,2,1,0:T(8,128)S(1)} %collective-permute-done.11.refs_0_), channel_id=1, source_target_pairs={{0,4},{4,0},{8,12},{12,8},{1,5},{5,1},{9,13},{13,9},{2,6},{6,2},{1... | collective-permute-start | bytes 393224 | tf_op jit(solution)/shard_map/ppermute | solution.py:584
  39.9 0.7 copy-start.2
  45.6 2.0 %collective-permute-start.15 = (f32[4,2,2,32,256]{4,3,2,1,0:T(8,128)S(1)}, f32[4,2,2,32,256]{4,3,2,1,0:T(8,128)S(1)}, u32[]{:S(2)}, u32[]{:S(2)}) collective-permute-start(f32[4,2,2,32,256]{4,3,2,1,0:T(8,128)S(1)} %shard_map.76.refs_5_), channel_id=1, source_target_pairs={{0,16},{16,0},{1,17},{17,1},{2,18},{18,2},{3,19},{19,3},{4,20},{20... | collective-permute-start | bytes 1572872 | tf_op jit(solution)/shard_map/ppermute | solution.py:58
  45.7 2.6 %collective-permute-start.16 = (f32[4,2,2,32,256]{4,3,2,1,0:T(8,128)S(1)}, f32[4,2,2,32,256]{4,3,2,1,0:T(8,128)S(1)}, u32[]{:S(2)}, u32[]{:S(2)}) collective-permute-start(f32[4,2,2,32,256]{4,3,2,1,0:T(8,128)S(1)} %shard_map.77.refs_6_), channel_id=1, source_target_pairs={{0,16},{16,0},{1,17},{17,1},{2,18},{18,2},{3,19},{19,3},{4,20},{20... | collective-permute-start | bytes 1572872 | tf_op jit(solution)/shard_map/ppermute | solution.py:58
  46.3 2.7 %collective-permute-start.17 = (f32[4,2,2,32,256]{4,3,2,1,0:T(8,128)S(1)}, f32[4,2,2,32,256]{4,3,2,1,0:T(8,128)S(1)}, u32[]{:S(2)}, u32[]{:S(2)}) collective-permute-start(f32[4,2,2,32,256]{4,3,2,1,0:T(8,128)S(1)} %shard_map.78.refs_7_), channel_id=1, source_target_pairs={{0,16},{16,0},{1,17},{17,1},{2,18},{18,2},{3,19},{19,3},{4,20},{20... | collective-permute-start | bytes 1572872 | tf_op jit(solution)/shard_map/ppermute | solution.py:58
  49.1 29.6 %copy-start.3 = (s32[1,1,2,2]{3,2,1,0:T(2,128)S(1)}, s32[1,1,2,2]{3,2,1,0:T(2,128)}, u32[]{:S(2)}) copy-start(s32[1,1,2,2]{3,2,1,0:T(2,128)} %param.10) | copy-start | bytes 52
  59.6 2.0 %collective-permute-start.18 = (f32[2,128,512]{2,1,0:T(8,128)S(1)}, f32[2,128,512]{2,1,0:T(8,128)S(1)}, u32[]{:S(2)}, u32[]{:S(2)}) collective-permute-start(f32[2,128,512]{2,1,0:T(8,128)S(1)} %get-tuple-element.53), channel_id=1, source_target_pairs={{0,16},{16,0},{1,17},{17,1},{2,18},{18,2},{3,19},{19,3},{4,20},{20... | collective-permute-start | bytes 1572872 | tf_op jit(solution)/shard_map/ppermute | solution.py:58
  62.3 9.2 %collective-permute-start.19 = (f32[2,128,256]{2,1,0:T(8,128)S(1)}, f32[2,128,256]{2,1,0:T(8,128)S(1)}, u32[]{:S(2)}, u32[]{:S(2)}) collective-permute-start(f32[2,128,256]{2,1,0:T(8,128)S(1)} %get-tuple-element.55), channel_id=1, source_target_pairs={{0,4},{4,0},{8,12},{12,8},{1,5},{5,1},{9,13},{13,9},{2,6},{6,2},{1... | collective-permute-start | bytes 786440 | tf_op jit(solution)/shard_map/ppermute | solution.py:58
  63.4 12.6 %collective-permute-start.20 = (f32[2,128,256]{2,1,0:T(8,128)S(1)}, f32[2,128,256]{2,1,0:T(8,128)S(1)}, u32[]{:S(2)}, u32[]{:S(2)}) collective-permute-start(f32[2,128,256]{2,1,0:T(8,128)S(1)} %get-tuple-element.56), channel_id=1, source_target_pairs={{4,8},{12,0},{8,4},{0,12},{5,9},{13,1},{9,5},{1,13},{6,10},{14,2},... | collective-permute-start | bytes 786440 | tf_op jit(solution)/shard_map/ppermute | solution.py:58
  76.7 2.0 %collective-permute-start.21 = (f32[2,128,512]{2,1,0:T(8,128)S(1)}, f32[2,128,512]{2,1,0:T(8,128)S(1)}, u32[]{:S(2)}, u32[]{:S(2)}) collective-permute-start(f32[2,128,512]{2,1,0:T(8,128)S(1)} %shard_map.81.refs_3_.refs_6_), channel_id=1, source_target_pairs={{0,16},{16,0},{1,17},{17,1},{2,18},{18,2},{3,19},{19,3},{4,20},{20... | collective-permute-start | bytes 1572872 | tf_op jit(solution)/shard_map/ppermute | solution.py:58
  86.2 1.2 collective-permute-start.22
  87.4 4.5 %collective-permute-start.25 = (f32[2]{0:T(128)S(1)}, f32[2]{0:T(128)S(1)}, u32[]{:S(2)}, u32[]{:S(2)}) collective-permute-start(f32[2]{0:T(128)S(1)} %add.26.refs_2_), channel_id=1, source_target_pairs={{0,12},{4,8},{8,4},{12,0},{1,13},{5,9},{9,5},{13,1},{2,14},{6,10},... | collective-permute-start | bytes 32 | tf_op jit(solution)/shard_map/ppermute | solution.py:521
  89.7 3.6 %collective-permute-start.24 = (f32[2]{0:T(128)S(1)}, f32[2]{0:T(128)S(1)}, u32[]{:S(2)}, u32[]{:S(2)}) collective-permute-start(f32[2]{0:T(128)S(1)} %add.26.refs_2_), channel_id=1, source_target_pairs={{0,8},{4,12},{8,0},{12,4},{1,9},{5,13},{9,1},{13,5},{2,10},{6,14},... | collective-permute-start | bytes 32 | tf_op jit(solution)/shard_map/ppermute | solution.py:521
  90.1 3.6 %collective-permute-start.23 = (f32[2]{0:T(128)S(1)}, f32[2]{0:T(128)S(1)}, u32[]{:S(2)}, u32[]{:S(2)}) collective-permute-start(f32[2]{0:T(128)S(1)} %add.26.refs_2_), channel_id=1, source_target_pairs={{0,4},{4,0},{8,12},{12,8},{1,5},{5,1},{9,13},{13,9},{2,6},{6,2},{1... | collective-permute-start | bytes 32 | tf_op jit(solution)/shard_map/ppermute | solution.py:521
  100.7 2.0 %collective-permute-start.26 = (f32[2,128,512]{2,1,0:T(8,128)S(1)}, f32[2,128,512]{2,1,0:T(8,128)S(1)}, u32[]{:S(2)}, u32[]{:S(2)}) collective-permute-start(f32[2,128,512]{2,1,0:T(8,128)S(1)} %get-tuple-element.65), channel_id=1, source_target_pairs={{0,16},{16,0},{1,17},{17,1},{2,18},{18,2},{3,19},{19,3},{4,20},{20... | collective-permute-start | bytes 1572872 | tf_op jit(solution)/shard_map/ppermute | solution.py:58
  102.7 32.9 %copy-start.1 = (f32[2,128,256]{2,1,0:T(8,128)S(1)}, f32[2,128,256]{2,1,0:T(8,128)}, u32[]{:S(2)}) copy-start(f32[2,128,256]{2,1,0:T(8,128)} %refs_5_.1) | copy-start | bytes 786436
  103.5 9.2 %collective-permute-start.27 = (f32[2,128,256]{2,1,0:T(8,128)S(1)}, f32[2,128,256]{2,1,0:T(8,128)S(1)}, u32[]{:S(2)}, u32[]{:S(2)}) collective-permute-start(f32[2,128,256]{2,1,0:T(8,128)S(1)} %get-tuple-element.67), channel_id=1, source_target_pairs={{0,4},{4,0},{8,12},{12,8},{1,5},{5,1},{9,13},{13,9},{2,6},{6,2},{1... | collective-permute-start | bytes 786440 | tf_op jit(solution)/shard_map/ppermute | solution.py:58
  104.3 14.2 %collective-permute-start.28 = (f32[2,128,256]{2,1,0:T(8,128)S(1)}, f32[2,128,256]{2,1,0:T(8,128)S(1)}, u32[]{:S(2)}, u32[]{:S(2)}) collective-permute-start(f32[2,128,256]{2,1,0:T(8,128)S(1)} %get-tuple-element.68), channel_id=1, source_target_pairs={{4,8},{12,0},{8,4},{0,12},{5,9},{13,1},{9,5},{1,13},{6,10},{14,2},... | collective-permute-start | bytes 786440 | tf_op jit(solution)/shard_map/ppermute | solution.py:58
  119.3 2.0 %collective-permute-start.29 = (f32[2,128,512]{2,1,0:T(8,128)S(1)}, f32[2,128,512]{2,1,0:T(8,128)S(1)}, u32[]{:S(2)}, u32[]{:S(2)}) collective-permute-start(f32[2,128,512]{2,1,0:T(8,128)S(1)} %shard_map.85.refs_3_.refs_7_), channel_id=1, source_target_pairs={{0,16},{16,0},{1,17},{17,1},{2,18},{18,2},{3,19},{19,3},{4,20},{20... | collective-permute-start | bytes 1572872 | tf_op jit(solution)/shard_map/ppermute | solution.py:58
  128.3 1.2 collective-permute-start.30
  129.5 4.5 %collective-permute-start.33 = (f32[2]{0:T(128)S(1)}, f32[2]{0:T(128)S(1)}, u32[]{:S(2)}, u32[]{:S(2)}) collective-permute-start(f32[2]{0:T(128)S(1)} %add.27.refs_0_), channel_id=1, source_target_pairs={{0,12},{4,8},{8,4},{12,0},{1,13},{5,9},{9,5},{13,1},{2,14},{6,10},... | collective-permute-start | bytes 32 | tf_op jit(solution)/shard_map/ppermute | solution.py:521
  130.2 3.8 %collective-permute-start.32 = (f32[2]{0:T(128)S(1)}, f32[2]{0:T(128)S(1)}, u32[]{:S(2)}, u32[]{:S(2)}) collective-permute-start(f32[2]{0:T(128)S(1)} %add.27.refs_0_), channel_id=1, source_target_pairs={{0,8},{4,12},{8,0},{12,4},{1,9},{5,13},{9,1},{13,5},{2,10},{6,14},... | collective-permute-start | bytes 32 | tf_op jit(solution)/shard_map/ppermute | solution.py:521
  132.1 3.6 %collective-permute-start.31 = (f32[2]{0:T(128)S(1)}, f32[2]{0:T(128)S(1)}, u32[]{:S(2)}, u32[]{:S(2)}) collective-permute-start(f32[2]{0:T(128)S(1)} %add.27.refs_0_), channel_id=1, source_target_pairs={{0,4},{4,0},{8,12},{12,8},{1,5},{5,1},{9,13},{13,9},{2,6},{6,2},{1... | collective-permute-start | bytes 32 | tf_op jit(solution)/shard_map/ppermute | solution.py:521

commit v6 on v5

--- a/solution.py
+++ b/solution.py
@@ -13,6 +13,7 @@
 
 DAMPING = 1.0
 UNROLL = 2
+UNDER = 1
 BROAD = 8
 USED, PLACE_MA, SIDE, PLACE_Y, SIDE_Y = range(5)
 
@@ -387,8 +388,8 @@
 
 
 def pack_body(plan, swaps, columns, *refs):
-    info, shard, tile, mine, *rims = refs[: 4 + swaps]
-    sems = refs[4 + swaps]
+    info, shard, tile, mine, near_tile, *rims = refs[: 5 + swaps]
+    sems = refs[5 + swaps]
     span = plan.patch // (2 * columns)
     start = pl.multiple_of(info[SIDE] * (plan.patch // 2) + info[PLACE_Y] * span, 8)
     copies = [pltpu.make_async_copy(shard.at[:, :, pl.ds(start, span), :], mine, sems.at[0])]
@@ -397,6 +398,7 @@
         first = pl.multiple_of(first, 128)
         source = tile.at[:, :, pl.ds(first, plan.rim)]
         copies.append(pltpu.make_async_copy(source, rim, sems.at[1 + k]))
+    copies.append(pltpu.make_async_copy(tile, near_tile, sems.at[1 + swaps]))
     for copy in copies:
         copy.start()
     for copy in copies:
@@ -571,12 +573,12 @@
         return middle
 
     hbm, dma = pltpu.HBM, pltpu.SemaphoreType.DMA
-    mine, *rims = call(
+    mine, near_tile, *rims = call(
         functools.partial(pack_body, plan, swaps_y, columns),
-        [(lead, 2, span, patch)] + [(2, tile_rows, rim)] * swaps_y,
+        [(lead, 2, span, patch), object_field.shape] + [(2, tile_rows, rim)] * swaps_y,
         [smem] + [hbm] * 2,
         [info, probe_shard, object_field],
-        scratch=[dma((1 + swaps_y,))],
+        scratch=[dma((2 + swaps_y,))],
     )
     parts = []
     for pairs in exchanges(groups):
@@ -587,7 +589,7 @@
         functools.partial(widen_body, plan, swaps_y),
         [tall],
         [smem, vmem] + [vmem] * swaps_y,
-        [weights_y, object_field, *swap("gy", rims)],
+        [weights_y, near_tile, *swap("gy", rims)],
     )
     probes, spectra, windows, targets, one, two = call(
         functools.partial(early_body, plan, swaps_x, groups),
@@ -605,8 +607,13 @@
         dtypes={4: jnp.bfloat16, 5: jnp.bfloat16},
     )
     packed, crossed = [], []
-    for blocks in parts:
-        packed += call(join_body, [(columns, lead, 2, span, patch)], [vmem] * (columns + 1), [*blocks, windows])
+    for k, blocks in enumerate(parts):
+        packed += call(
+            join_body,
+            [(columns, lead, 2, span, patch)],
+            [vmem] * (columns + 1),
+            [*blocks, windows if k >= UNDER else mine],
+        )
         crossed += swap("gx", packed[-1:])
     probes, spectra, intensity, middle, *sends = call(
         functools.partial(start_body, plan, swaps_x, (columns, groups)),
@@ -650,7 +657,7 @@
         functools.partial(finish_body, plan, len(totals)),
         [(2, tile_rows, tile_cols)],
         [smem] * (len(totals) + 1) + [vmem] * 3,
-        [*totals, first_step, object_field, first_way, last_way],
+        [*totals, first_step, near_tile, first_way, last_way],
         [None],
     )
     return current

time: 138 us -> 137 us (level)
  no operation moved by 1% of the time
where the time goes in v6:
time: 137 us
  waiting for transfers between devices  58 us (42%)
  Pallas kernels  44.3 us (32%)
  starting transfers between devices  32.6 us (24%)
    pallas_call x15, Pallas kernels, kernel_of(): pl.pallas_call(body, out_shape=[space(shape, dtypes.get(k, jnp.float32))...  44.3 us
    ppermute x16, waiting for transfers between devices, swap(): lax.ppermute(block, axis, pairs)  42 us
    ppermute x16, starting transfers between devices, swap(): lax.ppermute(block, axis, pairs)  11 us
    ppermute x9, starting transfers between devices, shards(): across = [lax.ppermute(block, 'gy', p) for p in exchanges(columns)]  10.2 us
    ppermute x6, starting transfers between devices, totals_of(): lax.ppermute(sums, 'gy', pairs)  6.98 us
    ppermute x3, waiting for transfers between devices, shards(): block = lax.ppermute(mine, 'ma', pairs)  5.95 us
    ppermute x6, waiting for transfers between devices, totals_of(): lax.ppermute(sums, 'gy', pairs)  5.41 us
    ppermute x9, waiting for transfers between devices, shards(): across = [lax.ppermute(block, 'gy', p) for p in exchanges(columns)]  4.66 us
  transfers between devices with their start and end apart: 34, of which 24 were waited for; matrix products, arithmetic and copies ran while one was open for 0% of the time, Pallas kernels for 4%

profile of v6, /device:TPU:0, one launch (start us, length us, event | category | flops | bytes accessed | tf_op | source)
XLA Modules:
  0.0 136.7 jit_solution(16558998094635908185)
XLA Ops:
  0.9 1.7 %shard_map.73 = (f32[2,2,32,256]{3,2,1,0:T(8,128)S(1)}, f32[2,128,256]{2,1,0:T(8,128)S(1)}, f32[2,128,128]{2,1,0:T(8,128)S(1)}, f32[2,128,128]{2,1,0:T(8,128)S(1)}) custom-call(s32[5]{0:T(128)S(1)} %stack.52.refs_0_, f32[2,2,256,256]{3,2,1,0:T(8,128)} %refs_8_.1, f32[2,128,256]{2,1,0:T(8,128)} %refs_2_.1), custom_call_target="tpu_custom_call" | custom-call | tf_op jit(solution)/shard_map/pallas_call | solution.py:89
  2.6 3.0 %collective-permute-start = (f32[2,128,128]{2,1,0:T(8,128)S(1)}, f32[2,128,128]{2,1,0:T(8,128)S(1)}, u32[]{:S(2)}, u32[]{:S(2)}) collective-permute-start(f32[2,128,128]{2,1,0:T(8,128)S(1)} %get-tuple-element.45), channel_id=1, source_target_pairs={{0,4},{4,0},{8,12},{12,8},{1,5},{5,1},{9,13},{13,9},{2,6},{6,2},{1... | collective-permute-start | bytes 393224 | tf_op jit(solution)/shard_map/ppermute | solution.py:59
  5.7 1.5 %collective-permute-start.1 = (f32[2,128,128]{2,1,0:T(8,128)S(1)}, f32[2,128,128]{2,1,0:T(8,128)S(1)}, u32[]{:S(2)}, u32[]{:S(2)}) collective-permute-start(f32[2,128,128]{2,1,0:T(8,128)S(1)} %get-tuple-element.46), channel_id=1, source_target_pairs={{4,8},{12,0},{8,4},{0,12},{5,9},{13,1},{9,5},{1,13},{6,10},{14,2},... | collective-permute-start | bytes 393224 | tf_op jit(solution)/shard_map/ppermute | solution.py:59
  7.2 2.4 %collective-permute-done.refs_2_ = f32[2,128,128]{2,1,0:T(8,128)S(1)} collective-permute-done((f32[2,128,128]{2,1,0:T(8,128)S(1)}, f32[2,128,128]{2,1,0:T(8,128)S(1)}, u32[]{:S(2)}, u32[]{:S(2)}) %collective-permute-start) | collective-permute-done | bytes 131104 | tf_op jit(solution)/shard_map/ppermute | solution.py:59
  9.6 3.6 %collective-permute-done.1.refs_3_ = f32[2,128,128]{2,1,0:T(8,128)S(1)} collective-permute-done((f32[2,128,128]{2,1,0:T(8,128)S(1)}, f32[2,128,128]{2,1,0:T(8,128)S(1)}, u32[]{:S(2)}, u32[]{:S(2)}) %collective-permute-start.1) | collective-permute-done | bytes 131104 | tf_op jit(solution)/shard_map/ppermute | solution.py:59
  13.8 2.7 %collective-permute-start.7 = (f32[2,2,32,256]{3,2,1,0:T(8,128)S(1)}, f32[2,2,32,256]{3,2,1,0:T(8,128)S(1)}, u32[]{:S(2)}, u32[]{:S(2)}) collective-permute-start(f32[2,2,32,256]{3,2,1,0:T(8,128)S(1)} %get-tuple-element.50.refs_4_), channel_id=1, source_target_pairs={{0,2},{1,3},{2,0},{3,1},{4,6},{5,7},{6,4},{7,5},{8,10},{9,11},{10,... | collective-permute-start | bytes 393224 | tf_op jit(solution)/shard_map/ppermute | solution.py:585
  16.5 1.6 %collective-permute-start.3 = (f32[2,2,32,256]{3,2,1,0:T(8,128)S(1)}, f32[2,2,32,256]{3,2,1,0:T(8,128)S(1)}, u32[]{:S(2)}, u32[]{:S(2)}) collective-permute-start(f32[2,2,32,256]{3,2,1,0:T(8,128)S(1)} %get-tuple-element.50.refs_4_), channel_id=1, source_target_pairs={{0,1},{1,0},{2,3},{3,2},{4,5},{5,4},{6,7},{7,6},{8,9},{9,8},{10,11... | collective-permute-start | bytes 393224 | tf_op jit(solution)/shard_map/ppermute | solution.py:585
  18.3 5.7 %collective-permute-done.7.refs_0_ = f32[2,2,32,256]{3,2,1,0:T(8,128)S(1)} collective-permute-done((f32[2,2,32,256]{3,2,1,0:T(8,128)S(1)}, f32[2,2,32,256]{3,2,1,0:T(8,128)S(1)}, u32[]{:S(2)}, u32[]{:S(2)}) %collective-permute-start.7) | collective-permute-done | bytes 131104 | tf_op jit(solution)/shard_map/ppermute | solution.py:585
  24.0 1.4 %collective-permute-start.10 = (f32[2,2,32,256]{3,2,1,0:T(8,128)S(1)}, f32[2,2,32,256]{3,2,1,0:T(8,128)S(1)}, u32[]{:S(2)}, u32[]{:S(2)}) collective-permute-start(f32[2,2,32,256]{3,2,1,0:T(8,128)S(1)} %collective-permute-done.7.refs_0_), channel_id=1, source_target_pairs={{0,12},{4,8},{8,4},{12,0},{1,13},{5,9},{9,5},{13,1},{2,14},{6,10},... | collective-permute-start | bytes 393224 | tf_op jit(solution)/shard_map/ppermute | solution.py:586
  25.4 1.5 %collective-permute-start.6 = (f32[2,2,32,256]{3,2,1,0:T(8,128)S(1)}, f32[2,2,32,256]{3,2,1,0:T(8,128)S(1)}, u32[]{:S(2)}, u32[]{:S(2)}) collective-permute-start(f32[2,2,32,256]{3,2,1,0:T(8,128)S(1)} %collective-permute-done.3.refs_0_), channel_id=1, source_target_pairs={{0,12},{4,8},{8,4},{12,0},{1,13},{5,9},{9,5},{13,1},{2,14},{6,10},... | collective-permute-start | bytes 393224 | tf_op jit(solution)/shard_map/ppermute | solution.py:586
  27.4 1.5 %collective-permute-start.4 = (f32[2,2,32,256]{3,2,1,0:T(8,128)S(1)}, f32[2,2,32,256]{3,2,1,0:T(8,128)S(1)}, u32[]{:S(2)}, u32[]{:S(2)}) collective-permute-start(f32[2,2,32,256]{3,2,1,0:T(8,128)S(1)} %collective-permute-done.3.refs_0_), channel_id=1, source_target_pairs={{0,4},{4,0},{8,12},{12,8},{1,5},{5,1},{9,13},{13,9},{2,6},{6,2},{1... | collective-permute-start | bytes 393224 | tf_op jit(solution)/shard_map/ppermute | solution.py:586
  28.9 2.4 %collective-permute-done.10.refs_3_ = f32[2,2,32,256]{3,2,1,0:T(8,128)S(1)} collective-permute-done((f32[2,2,32,256]{3,2,1,0:T(8,128)S(1)}, f32[2,2,32,256]{3,2,1,0:T(8,128)S(1)}, u32[]{:S(2)}, u32[]{:S(2)}) %collective-permute-start.10) | collective-permute-done | bytes 131104 | tf_op jit(solution)/shard_map/ppermute | solution.py:586
  31.3 2.3 %collective-permute-done.6.refs_3_ = f32[2,2,32,256]{3,2,1,0:T(8,128)S(1)} collective-permute-done((f32[2,2,32,256]{3,2,1,0:T(8,128)S(1)}, f32[2,2,32,256]{3,2,1,0:T(8,128)S(1)}, u32[]{:S(2)}, u32[]{:S(2)}) %collective-permute-start.6) | collective-permute-done | bytes 131104 | tf_op jit(solution)/shard_map/ppermute | solution.py:586
  33.6 2.0 %collective-permute-start.8 = (f32[2,2,32,256]{3,2,1,0:T(8,128)S(1)}, f32[2,2,32,256]{3,2,1,0:T(8,128)S(1)}, u32[]{:S(2)}, u32[]{:S(2)}) collective-permute-start(f32[2,2,32,256]{3,2,1,0:T(8,128)S(1)} %collective-permute-done.7.refs_0_), channel_id=1, source_target_pairs={{0,4},{4,0},{8,12},{12,8},{1,5},{5,1},{9,13},{13,9},{2,6},{6,2},{1... | collective-permute-start | bytes 393224 | tf_op jit(solution)/shard_map/ppermute | solution.py:586
  35.6 0.8 collective-permute-start.14
  36.5 1.6 %collective-permute-start.13 = (f32[2,2,32,256]{3,2,1,0:T(8,128)S(1)}, f32[2,2,32,256]{3,2,1,0:T(8,128)S(1)}, u32[]{:S(2)}, u32[]{:S(2)}) collective-permute-start(f32[2,2,32,256]{3,2,1,0:T(8,128)S(1)} %collective-permute-done.11.refs_0_), channel_id=1, source_target_pairs={{0,8},{4,12},{8,0},{12,4},{1,9},{5,13},{9,1},{13,5},{2,10},{6,14},... | collective-permute-start | bytes 393224 | tf_op jit(solution)/shard_map/ppermute | solution.py:586
  38.1 1.0 collective-permute-start.12
  39.8 4.9 %shard_map.75 = (f32[8,2,256,256]{3,2,1,0:T(8,128)S(1)}, f32[16,256,512]{2,1,0:T(8,128)S(1)}, f32[2,2,256,256]{3,2,1,0:T(8,128)S(1)}, f32[2,256,256]{2,1,0:T(8,1...) custom-call(s32[5]{0:T(128)S(1)} %stack.52.refs_0_, s32[2,2]{1,0:T(2,128)S(1)} %bitcast.16, ...), custom_call_target="tpu_custom_call" | custom-call | tf_op jit(solution)/shard_map/pallas_call | solution.py:89
  45.6 1.1 collective-permute-done.15.refs_8_
  46.8 0.7 collective-permute-done.16.refs_9_
  48.3 10.5 %shard_map.79 = (f32[8,2,256,256]{3,2,1,0:T(8,128)S(1)}, f32[16,256,512]{2,1,0:T(8,128)S(1)}, f32[2,256,256]{2,1,0:T(8,128)S(1)}, f32[2,128,512]{2,1,0:T(8,128)S(1)}, f32[2,128,512]{2,1,0:T(8,128)S(1)}) custom-call(s32[5]{0:T(128)S(1)} %stack.52.refs_0_, s32[2,2]{1,0:T(2,128)S(1)} %bitcast.17, ...), custom_call_target="tpu_custom_call", output_to_operand_aliasing={{0}: (2, {}), {1}: (3, {})} | custom-call | tf_op jit(solution)/shard_map/pallas_call | solution.py:89
  59.0 1.8 %collective-permute-done.18.refs_3_ = f32[2,128,512]{2,1,0:T(8,128)S(1)} collective-permute-done((f32[2,128,512]{2,1,0:T(8,128)S(1)}, f32[2,128,512]{2,1,0:T(8,128)S(1)}, u32[]{:S(2)}, u32[]{:S(2)}) %collective-permute-start.18) | collective-permute-done | bytes 524320 | tf_op jit(solution)/shard_map/ppermute | solution.py:59
  60.7 0.8 shard_map.80
  61.5 1.0 collective-permute-start.19
  63.2 7.5 %collective-permute-done.19.refs_3_ = f32[2,128,256]{2,1,0:T(8,128)S(1)} collective-permute-done((f32[2,128,256]{2,1,0:T(8,128)S(1)}, f32[2,128,256]{2,1,0:T(8,128)S(1)}, u32[]{:S(2)}, u32[]{:S(2)}) %collective-permute-start.19) | collective-permute-done | bytes 262176 | tf_op jit(solution)/shard_map/ppermute | solution.py:59
  70.7 4.4 %collective-permute-done.20.refs_4_ = f32[2,128,256]{2,1,0:T(8,128)S(1)} collective-permute-done((f32[2,128,256]{2,1,0:T(8,128)S(1)}, f32[2,128,256]{2,1,0:T(8,128)S(1)}, u32[]{:S(2)}, u32[]{:S(2)}) %collective-permute-start.20) | collective-permute-done | bytes 262176 | tf_op jit(solution)/shard_map/ppermute | solution.py:59
  76.0 1.9 %collective-permute-done.21.refs_4_ = f32[2,128,512]{2,1,0:T(8,128)S(1)} collective-permute-done((f32[2,128,512]{2,1,0:T(8,128)S(1)}, f32[2,128,512]{2,1,0:T(8,128)S(1)}, u32[]{:S(2)}, u32[]{:S(2)}) %collective-permute-start.21) | collective-permute-done | bytes 524320 | tf_op jit(solution)/shard_map/ppermute | solution.py:59
  77.9 7.5 %shard_map.82 = (f32[2]{0:T(128)S(1)}, f32[16,256,512]{2,1,0:T(8,128)S(1)}, f32[2,256,256]{2,1,0:T(8,128)S(1)}, f32[2,256,256]{2,1,0:T(8,128)S(1)}) custom-call(s32[5]{0:T(128)S(1)} %stack.52.refs_0_, s32[2,2]{1,0:T(2,128)S(1)} %bitcast.18, f32[2]{0:T(128)S(1)} %get-tuple-element.41.refs_2_.refs_1_, f32[2,128,512]{2,1,0:T(8,128)S(1)} %shard_map.81.refs_3_.refs_6_, ...), custom_call_target="tpu_custom_call" | custom-call | tf_op jit(solution)/shard_map/pallas_call | solution.py:89
  85.6 1.0 collective-permute-done.22
  86.6 2.3 %collective-permute-start.25 = (f32[2]{0:T(128)S(1)}, f32[2]{0:T(128)S(1)}, u32[]{:S(2)}, u32[]{:S(2)}) collective-permute-start(f32[2]{0:T(128)S(1)} %add.26.refs_2_), channel_id=1, source_target_pairs={{0,12},{4,8},{8,4},{12,0},{1,13},{5,9},{9,5},{13,1},{2,14},{6,10},... | collective-permute-start | bytes 32 | tf_op jit(solution)/shard_map/ppermute | solution.py:523
  89.3 0.8 collective-permute-start.23
  90.1 1.0 collective-permute-done.25.refs_5_
  91.0 1.4 %collective-permute-done.24.refs_4_ = f32[2]{0:T(128)S(1)} collective-permute-done((f32[2]{0:T(128)S(1)}, f32[2]{0:T(128)S(1)}, u32[]{:S(2)}, u32[]{:S(2)}) %collective-permute-start.24) | collective-permute-done | bytes 40 | tf_op jit(solution)/shard_map/ppermute | solution.py:523
  92.9 7.0 %shard_map.83 = (f32[16,256,512]{2,1,0:T(8,128)S(1)}, f32[1]{0:T(128)}, f32[2,128,512]{2,1,0:T(8,128)S(1)}, f32[2,128,512]{2,1,0:T(8,128)S(1)}) custom-call(s32[5]{0:T(128)S(1)} %stack.52.refs_0_, s32[2,2]{1,0:T(2,128)S(1)} %bitcast.19, f32[2]{0:T(128)S(1)} %add.26.refs_2_, f32[2]{0:T(128)S(1)} %collective-permute-done.23.refs_3_, ...), custom_call_target="tpu_custom_call" | custom-call | tf_op jit(solution)/shard_map/pallas_call | solution.py:89
  100.0 1.9 %collective-permute-done.26.refs_3_ = f32[2,128,512]{2,1,0:T(8,128)S(1)} collective-permute-done((f32[2,128,512]{2,1,0:T(8,128)S(1)}, f32[2,128,512]{2,1,0:T(8,128)S(1)}, u32[]{:S(2)}, u32[]{:S(2)}) %collective-permute-start.26) | collective-permute-done | bytes 524320 | tf_op jit(solution)/shard_map/ppermute | solution.py:59
  101.9 0.8 shard_map.84
  102.7 0.8 collective-permute-start.27
  103.5 2.3 %collective-permute-start.28 = (f32[2,128,256]{2,1,0:T(8,128)S(1)}, f32[2,128,256]{2,1,0:T(8,128)S(1)}, u32[]{:S(2)}, u32[]{:S(2)}) collective-permute-start(f32[2,128,256]{2,1,0:T(8,128)S(1)} %get-tuple-element.70), channel_id=1, source_target_pairs={{4,8},{12,0},{8,4},{0,12},{5,9},{13,1},{9,5},{1,13},{6,10},{14,2},... | collective-permute-start | bytes 786440 | tf_op jit(solution)/shard_map/ppermute | solution.py:59
  105.8 6.1 %collective-permute-done.27.refs_3_ = f32[2,128,256]{2,1,0:T(8,128)S(1)} collective-permute-done((f32[2,128,256]{2,1,0:T(8,128)S(1)}, f32[2,128,256]{2,1,0:T(8,128)S(1)}, u32[]{:S(2)}, u32[]{:S(2)}) %collective-permute-start.27) | collective-permute-done | bytes 262176 | tf_op jit(solution)/shard_map/ppermute | solution.py:59
  111.9 5.8 %collective-permute-done.28.refs_4_ = f32[2,128,256]{2,1,0:T(8,128)S(1)} collective-permute-done((f32[2,128,256]{2,1,0:T(8,128)S(1)}, f32[2,128,256]{2,1,0:T(8,128)S(1)}, u32[]{:S(2)}, u32[]{:S(2)}) %collective-permute-start.28) | collective-permute-done | bytes 262176 | tf_op jit(solution)/shard_map/ppermute | solution.py:59
  118.5 1.9 %collective-permute-done.29.refs_4_ = f32[2,128,512]{2,1,0:T(8,128)S(1)} collective-permute-done((f32[2,128,512]{2,1,0:T(8,128)S(1)}, f32[2,128,512]{2,1,0:T(8,128)S(1)}, u32[]{:S(2)}, u32[]{:S(2)}) %collective-permute-start.29) | collective-permute-done | bytes 524320 | tf_op jit(solution)/shard_map/ppermute | solution.py:59
  120.4 7.0 %shard_map.86 = f32[2]{0:T(128)S(1)} custom-call(s32[5]{0:T(128)S(1)} %stack.52.refs_0_, s32[2,2]{1,0:T(2,128)S(1)} %bitcast.20, f32[2]{0:T(128)S(1)} %get-tuple-element.41.refs_2_.refs_1_, f32[2,128,512]{2,1,0:T(8,128)S(1)} %shard_map.85.refs_3_.refs_7_, f32[2,128,512]{2,1,0:T(8,128)S(1)} %collective-permute-done.29.refs_4_, ...), custom_call_target="tpu_custom_call" | custom-call | tf_op jit(solution)/shard_map/pallas_call | solution.py:89
  127.7 1.0 collective-permute-done.30
  129.4 1.8 %collective-permute-start.32 = (f32[2]{0:T(128)S(1)}, f32[2]{0:T(128)S(1)}, u32[]{:S(2)}, u32[]{:S(2)}) collective-permute-start(f32[2]{0:T(128)S(1)} %add.27.refs_0_), channel_id=1, source_target_pairs={{0,8},{4,12},{8,0},{12,4},{1,9},{5,13},{9,1},{13,5},{2,10},{6,14},... | collective-permute-start | bytes 32 | tf_op jit(solution)/shard_map/ppermute | solution.py:523
  131.2 1.0 collective-permute-start.31
  132.2 1.0 collective-permute-done.33.refs_3_
  133.2 1.6 %collective-permute-done.31.refs_1_ = f32[2]{0:T(128)S(1)} collective-permute-done((f32[2]{0:T(128)S(1)}, f32[2]{0:T(128)S(1)}, u32[]{:S(2)}, u32[]{:S(2)}) %collective-permute-start.31) | collective-permute-done | bytes 40 | tf_op jit(solution)/shard_map/ppermute | solution.py:523
  134.8 1.9 %shard_map.87 = f32[2,128,256]{2,1,0:T(8,128)} custom-call(f32[2]{0:T(128)S(1)} %add.27.refs_0_, f32[2]{0:T(128)S(1)} %collective-permute-done.31.refs_1_, f32[2]{0:T(128)S(1)} %collective-permute-done.32.refs_2_, f32[2]{0:T(128)S(1)} %collective-permute-done.33.refs_3_, f32[1]{0:T(128)} %get-tuple-element.72.refs_4_, ...), custom_call_target="tpu_custom_call" | custom-call | tf_op jit(solution)/shard_map/pallas_call | solution.py:89
  (42 shorter events, 8.5 us)
Async XLA Ops:
  2.6 6.9 %collective-permute-start = (f32[2,128,128]{2,1,0:T(8,128)S(1)}, f32[2,128,128]{2,1,0:T(8,128)S(1)}, u32[]{:S(2)}, u32[]{:S(2)}) collective-permute-start(f32[2,128,128]{2,1,0:T(8,128)S(1)} %get-tuple-element.45), channel_id=1, source_target_pairs={{0,4},{4,0},{8,12},{12,8},{1,5},{5,1},{9,13},{13,9},{2,6},{6,2},{1... | collective-permute-start | bytes 393224 | tf_op jit(solution)/shard_map/ppermute | solution.py:59
  5.7 7.5 %collective-permute-start.1 = (f32[2,128,128]{2,1,0:T(8,128)S(1)}, f32[2,128,128]{2,1,0:T(8,128)S(1)}, u32[]{:S(2)}, u32[]{:S(2)}) collective-permute-start(f32[2,128,128]{2,1,0:T(8,128)S(1)} %get-tuple-element.46), channel_id=1, source_target_pairs={{4,8},{12,0},{8,4},{0,12},{5,9},{13,1},{9,5},{1,13},{6,10},{14,2},... | collective-permute-start | bytes 393224 | tf_op jit(solution)/shard_map/ppermute | solution.py:59
  13.8 24.3 %collective-permute-start.2 = (f32[2,128,512]{2,1,0:T(8,128)S(1)}, f32[2,128,512]{2,1,0:T(8,128)S(1)}, u32[]{:S(2)}, u32[]{:S(2)}) collective-permute-start(f32[2,128,512]{2,1,0:T(8,128)S(1)} %shard_map.74.refs_3_), channel_id=1, source_target_pairs={{0,16},{16,0},{1,17},{17,1},{2,18},{18,2},{3,19},{19,3},{4,20},{20... | collective-permute-start | bytes 1572872 | tf_op jit(solution)/shard_map/ppermute | solution.py:59
  13.8 10.2 %collective-permute-start.7 = (f32[2,2,32,256]{3,2,1,0:T(8,128)S(1)}, f32[2,2,32,256]{3,2,1,0:T(8,128)S(1)}, u32[]{:S(2)}, u32[]{:S(2)}) collective-permute-start(f32[2,2,32,256]{3,2,1,0:T(8,128)S(1)} %get-tuple-element.50.refs_4_), channel_id=1, source_target_pairs={{0,2},{1,3},{2,0},{3,1},{4,6},{5,7},{6,4},{7,5},{8,10},{9,11},{10,... | collective-permute-start | bytes 393224 | tf_op jit(solution)/shard_map/ppermute | solution.py:585
  16.5 8.9 %collective-permute-start.3 = (f32[2,2,32,256]{3,2,1,0:T(8,128)S(1)}, f32[2,2,32,256]{3,2,1,0:T(8,128)S(1)}, u32[]{:S(2)}, u32[]{:S(2)}) collective-permute-start(f32[2,2,32,256]{3,2,1,0:T(8,128)S(1)} %get-tuple-element.50.refs_4_), channel_id=1, source_target_pairs={{0,1},{1,0},{2,3},{3,2},{4,5},{5,4},{6,7},{7,6},{8,9},{9,8},{10,11... | collective-permute-start | bytes 393224 | tf_op jit(solution)/shard_map/ppermute | solution.py:585
  18.1 9.3 %collective-permute-start.11 = (f32[2,2,32,256]{3,2,1,0:T(8,128)S(1)}, f32[2,2,32,256]{3,2,1,0:T(8,128)S(1)}, u32[]{:S(2)}, u32[]{:S(2)}) collective-permute-start(f32[2,2,32,256]{3,2,1,0:T(8,128)S(1)} %get-tuple-element.50.refs_4_), channel_id=1, source_target_pairs={{0,3},{1,2},{2,1},{3,0},{4,7},{5,6},{6,5},{7,4},{8,11},{9,10},{10,... | collective-permute-start | bytes 393224 | tf_op jit(solution)/shard_map/ppermute | solution.py:585
  24.0 7.3 %collective-permute-start.10 = (f32[2,2,32,256]{3,2,1,0:T(8,128)S(1)}, f32[2,2,32,256]{3,2,1,0:T(8,128)S(1)}, u32[]{:S(2)}, u32[]{:S(2)}) collective-permute-start(f32[2,2,32,256]{3,2,1,0:T(8,128)S(1)} %collective-permute-done.7.refs_0_), channel_id=1, source_target_pairs={{0,12},{4,8},{8,4},{12,0},{1,13},{5,9},{9,5},{13,1},{2,14},{6,10},... | collective-permute-start | bytes 393224 | tf_op jit(solution)/shard_map/ppermute | solution.py:586
  25.4 8.1 %collective-permute-start.6 = (f32[2,2,32,256]{3,2,1,0:T(8,128)S(1)}, f32[2,2,32,256]{3,2,1,0:T(8,128)S(1)}, u32[]{:S(2)}, u32[]{:S(2)}) collective-permute-start(f32[2,2,32,256]{3,2,1,0:T(8,128)S(1)} %collective-permute-done.3.refs_0_), channel_id=1, source_target_pairs={{0,12},{4,8},{8,4},{12,0},{1,13},{5,9},{9,5},{13,1},{2,14},{6,10},... | collective-permute-start | bytes 393224 | tf_op jit(solution)/shard_map/ppermute | solution.py:586
  26.9 8.7 %collective-permute-start.5 = (f32[2,2,32,256]{3,2,1,0:T(8,128)S(1)}, f32[2,2,32,256]{3,2,1,0:T(8,128)S(1)}, u32[]{:S(2)}, u32[]{:S(2)}) collective-permute-start(f32[2,2,32,256]{3,2,1,0:T(8,128)S(1)} %collective-permute-done.3.refs_0_), channel_id=1, source_target_pairs={{0,8},{4,12},{8,0},{12,4},{1,9},{5,13},{9,1},{13,5},{2,10},{6,14},... | collective-permute-start | bytes 393224 | tf_op jit(solution)/shard_map/ppermute | solution.py:586
  27.4 9.1 %collective-permute-start.4 = (f32[2,2,32,256]{3,2,1,0:T(8,128)S(1)}, f32[2,2,32,256]{3,2,1,0:T(8,128)S(1)}, u32[]{:S(2)}, u32[]{:S(2)}) collective-permute-start(f32[2,2,32,256]{3,2,1,0:T(8,128)S(1)} %collective-permute-done.3.refs_0_), channel_id=1, source_target_pairs={{0,4},{4,0},{8,12},{12,8},{1,5},{5,1},{9,13},{13,9},{2,6},{6,2},{1... | collective-permute-start | bytes 393224 | tf_op jit(solution)/shard_map/ppermute | solution.py:586
  31.3 13.5 %collective-permute-start.9 = (f32[2,2,32,256]{3,2,1,0:T(8,128)S(1)}, f32[2,2,32,256]{3,2,1,0:T(8,128)S(1)}, u32[]{:S(2)}, u32[]{:S(2)}) collective-permute-start(f32[2,2,32,256]{3,2,1,0:T(8,128)S(1)} %collective-permute-done.7.refs_0_), channel_id=1, source_target_pairs={{0,8},{4,12},{8,0},{12,4},{1,9},{5,13},{9,1},{13,5},{2,10},{6,14},... | collective-permute-start | bytes 393224 | tf_op jit(solution)/shard_map/ppermute | solution.py:586
  33.6 11.3 %collective-permute-start.8 = (f32[2,2,32,256]{3,2,1,0:T(8,128)S(1)}, f32[2,2,32,256]{3,2,1,0:T(8,128)S(1)}, u32[]{:S(2)}, u32[]{:S(2)}) collective-permute-start(f32[2,2,32,256]{3,2,1,0:T(8,128)S(1)} %collective-permute-done.7.refs_0_), channel_id=1, source_target_pairs={{0,4},{4,0},{8,12},{12,8},{1,5},{5,1},{9,13},{13,9},{2,6},{6,2},{1... | collective-permute-start | bytes 393224 | tf_op jit(solution)/shard_map/ppermute | solution.py:586
  35.6 9.8 %collective-permute-start.14 = (f32[2,2,32,256]{3,2,1,0:T(8,128)S(1)}, f32[2,2,32,256]{3,2,1,0:T(8,128)S(1)}, u32[]{:S(2)}, u32[]{:S(2)}) collective-permute-start(f32[2,2,32,256]{3,2,1,0:T(8,128)S(1)} %collective-permute-done.11.refs_0_), channel_id=1, source_target_pairs={{0,12},{4,8},{8,4},{12,0},{1,13},{5,9},{9,5},{13,1},{2,14},{6,10},... | collective-permute-start | bytes 393224 | tf_op jit(solution)/shard_map/ppermute | solution.py:586
  36.5 9.0 %collective-permute-start.13 = (f32[2,2,32,256]{3,2,1,0:T(8,128)S(1)}, f32[2,2,32,256]{3,2,1,0:T(8,128)S(1)}, u32[]{:S(2)}, u32[]{:S(2)}) collective-permute-start(f32[2,2,32,256]{3,2,1,0:T(8,128)S(1)} %collective-permute-done.11.refs_0_), channel_id=1, source_target_pairs={{0,8},{4,12},{8,0},{12,4},{1,9},{5,13},{9,1},{13,5},{2,10},{6,14},... | collective-permute-start | bytes 393224 | tf_op jit(solution)/shard_map/ppermute | solution.py:586
  38.1 7.4 %collective-permute-start.12 = (f32[2,2,32,256]{3,2,1,0:T(8,128)S(1)}, f32[2,2,32,256]{3,2,1,0:T(8,128)S(1)}, u32[]{:S(2)}, u32[]{:S(2)}) collective-permute-start(f32[2,2,32,256]{3,2,1,0:T(8,128)S(1)} %collective-permute-done.11.refs_0_), channel_id=1, source_target_pairs={{0,4},{4,0},{8,12},{12,8},{1,5},{5,1},{9,13},{13,9},{2,6},{6,2},{1... | collective-permute-start | bytes 393224 | tf_op jit(solution)/shard_map/ppermute | solution.py:586
  39.2 0.7 copy-start
  44.8 2.0 %collective-permute-start.15 = (f32[4,2,2,32,256]{4,3,2,1,0:T(8,128)S(1)}, f32[4,2,2,32,256]{4,3,2,1,0:T(8,128)S(1)}, u32[]{:S(2)}, u32[]{:S(2)}) collective-permute-start(f32[4,2,2,32,256]{4,3,2,1,0:T(8,128)S(1)} %shard_map.76.refs_5_), channel_id=1, source_target_pairs={{0,16},{16,0},{1,17},{17,1},{2,18},{18,2},{3,19},{19,3},{4,20},{20... | collective-permute-start | bytes 1572872 | tf_op jit(solution)/shard_map/ppermute | solution.py:59
  44.9 2.6 %collective-permute-start.16 = (f32[4,2,2,32,256]{4,3,2,1,0:T(8,128)S(1)}, f32[4,2,2,32,256]{4,3,2,1,0:T(8,128)S(1)}, u32[]{:S(2)}, u32[]{:S(2)}) collective-permute-start(f32[4,2,2,32,256]{4,3,2,1,0:T(8,128)S(1)} %shard_map.77.refs_6_), channel_id=1, source_target_pairs={{0,16},{16,0},{1,17},{17,1},{2,18},{18,2},{3,19},{19,3},{4,20},{20... | collective-permute-start | bytes 1572872 | tf_op jit(solution)/shard_map/ppermute | solution.py:59
  45.5 2.7 %collective-permute-start.17 = (f32[4,2,2,32,256]{4,3,2,1,0:T(8,128)S(1)}, f32[4,2,2,32,256]{4,3,2,1,0:T(8,128)S(1)}, u32[]{:S(2)}, u32[]{:S(2)}) collective-permute-start(f32[4,2,2,32,256]{4,3,2,1,0:T(8,128)S(1)} %shard_map.78.refs_7_), channel_id=1, source_target_pairs={{0,16},{16,0},{1,17},{17,1},{2,18},{18,2},{3,19},{19,3},{4,20},{20... | collective-permute-start | bytes 1572872 | tf_op jit(solution)/shard_map/ppermute | solution.py:59
  58.7 2.0 %collective-permute-start.18 = (f32[2,128,512]{2,1,0:T(8,128)S(1)}, f32[2,128,512]{2,1,0:T(8,128)S(1)}, u32[]{:S(2)}, u32[]{:S(2)}) collective-permute-start(f32[2,128,512]{2,1,0:T(8,128)S(1)} %get-tuple-element.55), channel_id=1, source_target_pairs={{0,16},{16,0},{1,17},{17,1},{2,18},{18,2},{3,19},{19,3},{4,20},{20... | collective-permute-start | bytes 1572872 | tf_op jit(solution)/shard_map/ppermute | solution.py:59
  61.5 9.2 %collective-permute-start.19 = (f32[2,128,256]{2,1,0:T(8,128)S(1)}, f32[2,128,256]{2,1,0:T(8,128)S(1)}, u32[]{:S(2)}, u32[]{:S(2)}) collective-permute-start(f32[2,128,256]{2,1,0:T(8,128)S(1)} %get-tuple-element.57), channel_id=1, source_target_pairs={{0,4},{4,0},{8,12},{12,8},{1,5},{5,1},{9,13},{13,9},{2,6},{6,2},{1... | collective-permute-start | bytes 786440 | tf_op jit(solution)/shard_map/ppermute | solution.py:59
  62.5 12.6 %collective-permute-start.20 = (f32[2,128,256]{2,1,0:T(8,128)S(1)}, f32[2,128,256]{2,1,0:T(8,128)S(1)}, u32[]{:S(2)}, u32[]{:S(2)}) collective-permute-start(f32[2,128,256]{2,1,0:T(8,128)S(1)} %get-tuple-element.58), channel_id=1, source_target_pairs={{4,8},{12,0},{8,4},{0,12},{5,9},{13,1},{9,5},{1,13},{6,10},{14,2},... | collective-permute-start | bytes 786440 | tf_op jit(solution)/shard_map/ppermute | solution.py:59
  75.9 2.0 %collective-permute-start.21 = (f32[2,128,512]{2,1,0:T(8,128)S(1)}, f32[2,128,512]{2,1,0:T(8,128)S(1)}, u32[]{:S(2)}, u32[]{:S(2)}) collective-permute-start(f32[2,128,512]{2,1,0:T(8,128)S(1)} %shard_map.81.refs_3_.refs_6_), channel_id=1, source_target_pairs={{0,16},{16,0},{1,17},{17,1},{2,18},{18,2},{3,19},{19,3},{4,20},{20... | collective-permute-start | bytes 1572872 | tf_op jit(solution)/shard_map/ppermute | solution.py:59
  85.3 1.2 collective-permute-start.22
  86.6 4.5 %collective-permute-start.25 = (f32[2]{0:T(128)S(1)}, f32[2]{0:T(128)S(1)}, u32[]{:S(2)}, u32[]{:S(2)}) collective-permute-start(f32[2]{0:T(128)S(1)} %add.26.refs_2_), channel_id=1, source_target_pairs={{0,12},{4,8},{8,4},{12,0},{1,13},{5,9},{9,5},{13,1},{2,14},{6,10},... | collective-permute-start | bytes 32 | tf_op jit(solution)/shard_map/ppermute | solution.py:523
  88.9 3.6 %collective-permute-start.24 = (f32[2]{0:T(128)S(1)}, f32[2]{0:T(128)S(1)}, u32[]{:S(2)}, u32[]{:S(2)}) collective-permute-start(f32[2]{0:T(128)S(1)} %add.26.refs_2_), channel_id=1, source_target_pairs={{0,8},{4,12},{8,0},{12,4},{1,9},{5,13},{9,1},{13,5},{2,10},{6,14},... | collective-permute-start | bytes 32 | tf_op jit(solution)/shard_map/ppermute | solution.py:523
  89.3 3.6 %collective-permute-start.23 = (f32[2]{0:T(128)S(1)}, f32[2]{0:T(128)S(1)}, u32[]{:S(2)}, u32[]{:S(2)}) collective-permute-start(f32[2]{0:T(128)S(1)} %add.26.refs_2_), channel_id=1, source_target_pairs={{0,4},{4,0},{8,12},{12,8},{1,5},{5,1},{9,13},{13,9},{2,6},{6,2},{1... | collective-permute-start | bytes 32 | tf_op jit(solution)/shard_map/ppermute | solution.py:523
  99.9 2.0 %collective-permute-start.26 = (f32[2,128,512]{2,1,0:T(8,128)S(1)}, f32[2,128,512]{2,1,0:T(8,128)S(1)}, u32[]{:S(2)}, u32[]{:S(2)}) collective-permute-start(f32[2,128,512]{2,1,0:T(8,128)S(1)} %get-tuple-element.67), channel_id=1, source_target_pairs={{0,16},{16,0},{1,17},{17,1},{2,18},{18,2},{3,19},{19,3},{4,20},{20... | collective-permute-start | bytes 1572872 | tf_op jit(solution)/shard_map/ppermute | solution.py:59
  102.7 9.2 %collective-permute-start.27 = (f32[2,128,256]{2,1,0:T(8,128)S(1)}, f32[2,128,256]{2,1,0:T(8,128)S(1)}, u32[]{:S(2)}, u32[]{:S(2)}) collective-permute-start(f32[2,128,256]{2,1,0:T(8,128)S(1)} %get-tuple-element.69), channel_id=1, source_target_pairs={{0,4},{4,0},{8,12},{12,8},{1,5},{5,1},{9,13},{13,9},{2,6},{6,2},{1... | collective-permute-start | bytes 786440 | tf_op jit(solution)/shard_map/ppermute | solution.py:59
  103.5 14.2 %collective-permute-start.28 = (f32[2,128,256]{2,1,0:T(8,128)S(1)}, f32[2,128,256]{2,1,0:T(8,128)S(1)}, u32[]{:S(2)}, u32[]{:S(2)}) collective-permute-start(f32[2,128,256]{2,1,0:T(8,128)S(1)} %get-tuple-element.70), channel_id=1, source_target_pairs={{4,8},{12,0},{8,4},{0,12},{5,9},{13,1},{9,5},{1,13},{6,10},{14,2},... | collective-permute-start | bytes 786440 | tf_op jit(solution)/shard_map/ppermute | solution.py:59
  118.5 2.0 %collective-permute-start.29 = (f32[2,128,512]{2,1,0:T(8,128)S(1)}, f32[2,128,512]{2,1,0:T(8,128)S(1)}, u32[]{:S(2)}, u32[]{:S(2)}) collective-permute-start(f32[2,128,512]{2,1,0:T(8,128)S(1)} %shard_map.85.refs_3_.refs_7_), channel_id=1, source_target_pairs={{0,16},{16,0},{1,17},{17,1},{2,18},{18,2},{3,19},{19,3},{4,20},{20... | collective-permute-start | bytes 1572872 | tf_op jit(solution)/shard_map/ppermute | solution.py:59
  127.5 1.2 collective-permute-start.30
  128.7 4.5 %collective-permute-start.33 = (f32[2]{0:T(128)S(1)}, f32[2]{0:T(128)S(1)}, u32[]{:S(2)}, u32[]{:S(2)}) collective-permute-start(f32[2]{0:T(128)S(1)} %add.27.refs_0_), channel_id=1, source_target_pairs={{0,12},{4,8},{8,4},{12,0},{1,13},{5,9},{9,5},{13,1},{2,14},{6,10},... | collective-permute-start | bytes 32 | tf_op jit(solution)/shard_map/ppermute | solution.py:523
  129.4 3.8 %collective-permute-start.32 = (f32[2]{0:T(128)S(1)}, f32[2]{0:T(128)S(1)}, u32[]{:S(2)}, u32[]{:S(2)}) collective-permute-start(f32[2]{0:T(128)S(1)} %add.27.refs_0_), channel_id=1, source_target_pairs={{0,8},{4,12},{8,0},{12,4},{1,9},{5,13},{9,1},{13,5},{2,10},{6,14},... | collective-permute-start | bytes 32 | tf_op jit(solution)/shard_map/ppermute | solution.py:523
  131.2 3.6 %collective-permute-start.31 = (f32[2]{0:T(128)S(1)}, f32[2]{0:T(128)S(1)}, u32[]{:S(2)}, u32[]{:S(2)}) collective-permute-start(f32[2]{0:T(128)S(1)} %add.27.refs_0_), channel_id=1, source_target_pairs={{0,4},{4,0},{8,12},{12,8},{1,5},{5,1},{9,13},{13,9},{2,6},{6,2},{1... | collective-permute-start | bytes 32 | tf_op jit(solution)/shard_map/ppermute | solution.py:523
